TPU v7x, 512 devices: a whole 4x8x8 slice. The times are simulated.
512 devices in a mesh: lat: 32 (over y, z_hi, core), lev: 16 (over x, z_lo).
Axes of the slice: x: 4, y: 8, z: 8 (z_hi: 2, z_lo: 4; z = z_hi * 4 + z_lo), core: 2. Of those that a mesh axis runs over, the one named last changes fastest.
Arguments:
- tracer: float32 [32, 640, 1280], P('lev', 'lat'), may hold values from -6 to 6
- offsets: int32 [2, 640, 1280], P(None, 'lat'), may hold values from -3 to 3
- stencil: float32 [7, 7], replicated, may hold values from -0.6 to 0.6
- assign: int32 [640], replicated, may hold values from 0 to 639, as said below
- legendre: bfloat16 [640, 2, 320, 320], P('lat', None, 'lev'), may hold values from -0.3125 to 0.3125
- damping: float32 [32], replicated, may hold values from 0.5 to 8
- vert_vecs: float32 [32, 32], replicated, may hold values from -1 to 1
- vert_inv: float32 [32, 32], replicated, may hold values from -1 to 1
Outputs:
- tracer_new: float32 [32, 640, 1280], P('lev', 'lat')
- spectral_new: float32 [640, 2, 320, 64], P('lat', None, 'lev')
Inputs may be any that keep to these rules, and one draw needn't show every extreme that they name: `assign`: a permutation of 0 to 639 in which slots 2 u and 2 u + 1 hold the wavenumbers m and 639 - m.
All inputs are finite; a program needn't handle non-finite values.
Results may differ from a plain program's by a relative error of at most 0.0036.
Values may be sent and summed in bfloat16 or wider, within the bound.
No kernel may reach another device: no remote copies, remote signals or barrier semaphores. Data moves between devices by JAX's collectives and lax.ppermute only.
A program may use at most 128 MiB of HBM per device.

v0:
```python
import math

import jax
import jax.numpy as jnp
from jax import lax
from jax.sharding import Mesh
from jax.sharding import PartitionSpec as P

M = 640
LEV = ("lev_0", "lev_1")


EXACT = lax.Precision.HIGHEST


def padded_2(cells, sides, width):
    for axis, dim in sides:
        count = lax.axis_size(axis)
        ends = count - 1
        head = lax.slice_in_dim(cells, 0, width, axis=dim)
        tail = lax.slice_in_dim(cells, cells.shape[dim] - width, cells.shape[dim], axis=dim)
        cells = jnp.concatenate(
            [
                lax.ppermute(tail, axis, [(i, (i + 1) % count) for i in range(ends)]),
                cells,
                lax.ppermute(head, axis, [((i + 1) % count, i) for i in range(ends)]),
            ],
            axis=dim,
        )
    return cells


def whole_of(value, axes, dim):
    if not axes:
        return value
    nearer = lax.all_gather(value, axes[-1], axis=dim, tiled=True)
    return whole_of(nearer, axes[:-1], dim)


def transport(padded, offsets, stencil):
    row_count = offsets.shape[1]
    summed = jnp.zeros((padded.shape[0], row_count, padded.shape[2]), jnp.float32)
    for row_step in range(-3, 4):
        band_rows = padded[:, 3 + row_step : 3 + row_step + row_count, :]
        for col_step in range(-3, 4):
            shifted = jnp.roll(band_rows, -col_step, axis=2)
            picked = jnp.logical_and(offsets[0] == row_step, offsets[1] == col_step).astype(
                jnp.float32
            )
            summed = summed + (stencil[row_step + 3, col_step + 3] + picked)[None, :, :] * shifted
    return summed


def wave_angles(assign, lon_cells):
    longitudes = jnp.arange(lon_cells, dtype=jnp.int32)
    phase_index = longitudes[:, None] * assign[None, :] % lon_cells
    angles = phase_index.astype(jnp.float32) * (2.0 * math.pi / lon_cells)
    return (angles, 1.0 / math.sqrt(lon_cells))


def forward_table(assign, lon_cells):
    angles, norm_scale = wave_angles(assign, lon_cells)
    return jnp.stack([jnp.cos(angles) * norm_scale, -jnp.sin(angles) * norm_scale], axis=2)


def inverse_table(assign, lon_cells):
    angles, norm_scale = wave_angles(assign, lon_cells)
    weights = jnp.where(assign == 0, 1.0, 2.0).astype(jnp.float32) * norm_scale
    cosines = jnp.cos(angles).T * weights[:, None]
    sines = -jnp.sin(angles).T * weights[:, None]
    return jnp.stack([cosines, sines], axis=1)


def split_hemispheres(fourier):
    half_lat = fourier.shape[-1] // 2
    north_half = fourier[..., :half_lat]
    south_half = fourier[..., ::-1][..., :half_lat]
    return jnp.stack([north_half + south_half, north_half - south_half], axis=1).astype(
        jnp.bfloat16
    )


def vertical(spectra, my_waves, first_degree, damping, vert_vecs, vert_inv):
    degree_span = spectra.shape[2]
    degrees = first_degree + jnp.arange(degree_span, dtype=jnp.int32)
    parity = jnp.arange(2, dtype=jnp.int32)
    degree_n = my_waves[:, None, None] + 2 * degrees[None, None, :] + parity[None, :, None]
    inside = (degree_n <= M - 1).astype(jnp.float32)
    forcing = spectra * inside[:, :, :, None, None]
    modal = jnp.einsum("kq,rpicq->rpick", vert_inv, forcing, precision=EXACT)
    scaled_n = degree_n.astype(jnp.float32)
    growth = scaled_n * (scaled_n + 1.0) / float(M * M)
    denominator = 1.0 + growth[:, :, :, None, None] * damping[None, None, None, None, :]
    modal = modal / denominator
    return jnp.einsum("kq,rpicq->rpick", vert_vecs, modal, precision=EXACT)


def on_device(tracer, offsets, stencil, assign, legendre, damping, vert_vecs, vert_inv):
    lon_cells = tracer.shape[2]
    padded = padded_2(tracer, (("lat", 1),), 3)
    advected = transport(padded, offsets, stencil)
    fourier = jnp.einsum(
        "lij,jrc->rcli", advected, forward_table(assign, lon_cells), precision=EXACT
    )
    by_wave = lax.all_to_all(fourier, "lat", split_axis=0, concat_axis=3, tiled=True)
    hemispheres = split_hemispheres(by_wave)
    slot_count = legendre.shape[0]
    my_waves = lax.dynamic_slice_in_dim(assign, lax.axis_index("lat") * slot_count, slot_count)
    first_degree = lax.axis_index(LEV) * legendre.shape[2]
    full_table = whole_of(legendre, LEV, 2)
    spectra_all = jnp.einsum(
        "rpij,rpclj->rpicl", full_table, hemispheres, preferred_element_type=jnp.float32
    )
    spectra = lax.all_to_all(spectra_all, LEV, split_axis=2, concat_axis=4, tiled=True)
    solved = vertical(spectra, my_waves, first_degree, damping, vert_vecs, vert_inv)
    packed = solved.astype(jnp.bfloat16)
    spread = lax.all_to_all(packed, LEV, split_axis=4, concat_axis=2, tiled=True)
    back_terms = jnp.einsum(
        "rpij,rpicl->lrpcj", full_table, spread, preferred_element_type=jnp.float32
    )
    north_half = back_terms[:, :, 0] + back_terms[:, :, 1]
    south_half = back_terms[:, :, 0] - back_terms[:, :, 1]
    zonal = jnp.concatenate([north_half, south_half[..., ::-1]], axis=-1)
    lat_rows = lax.all_to_all(zonal, "lat", split_axis=3, concat_axis=1, tiled=True)
    tracer_new = jnp.einsum(
        "lrci,rcj->lij", lat_rows, inverse_table(assign, lon_cells), precision=EXACT
    )
    spectral_new = solved.reshape(solved.shape[0], 2, solved.shape[2], 2 * solved.shape[4])
    return (tracer_new, spectral_new)


def solution(mesh):
    split = Mesh(mesh.devices.reshape(mesh.shape["lat"], 4, 4), ("lat", "lev_0", "lev_1"))
    placed = (
        P(LEV, "lat", None),
        P(None, "lat", None),
        P(),
        P(),
        P("lat", None, LEV, None),
        P(),
        P(),
        P(),
    )
    return jax.shard_map(
        on_device,
        mesh=split,
        in_specs=placed,
        out_specs=(P(LEV, "lat", None), P("lat", None, LEV, None)),
        check_vma=False,
    )
```

profile of v0, /device:TPU:1, one launch (start us, length us, event | category | flops | bytes accessed | tf_op | source)
XLA Modules:
  0.0 290.4 jit_solution(7828020050133421824)
XLA Ops:
  7.2 2.3 copy.69
  9.6 1.4 fusion.106
  11.0 12.0 %collective-permute-start = (f32[2,3,1280]{2,0,1:T(2,128)}, f32[2,3,1280]{2,0,1:T(2,128)}, u32[]{:S(2)}, u32[]{:S(2)}) collective-permute-start(f32[2,3,1280]{2,0,1:T(2,128)} %get-tuple-element.115), channel_id=1, source_target_pairs={{0,16},{16,32},{32,48},{48,64},{64,80},{80,96},{96,112},{112,128},... | collective-permute-start | bytes 92168 | tf_op jit(solution)/shard_map/ppermute | solution.py:24
  23.0 1.9 collective-permute-start.1
  25.0 1.8 fusion.115
  26.7 2.1 fusion.114
  28.8 2.1 fusion.113
  30.9 1.4 fusion.107
  32.3 1.4 fusion.109
  33.7 1.2 fusion.105
  35.6 8.0 %add_bitcast_fusion.41 = (f32[20,1280]{1,0:T(8,128)S(1)}, pred[1,20,1280]{2,1,0:T(8,128)(4,1)S(1)}, f32[20,1280]{1,0:T(8,128)S(1)}, pred[1,20,1280]{2,1,0:T(8,12...) fusion(pred[1,20,1280]{2,1,0:T(8,128)(4,1)S(1)} %get-tuple-elem, ...), kind=kLoop, calls=%fused_computation.202 | loop fusion | flops 1228800 | bytes 1792048 | tf_op jit(solution)/shard_map/mul | solution.py:50
  43.6 1.2 add_bitcast_fusion.21
  44.8 29.5 %all-gather.3.cloned.1.call-done = bf16[20,2,80,320]{3,1,0,2:T(2,128)(2,1)} async-done(((bf16[20,2,20,320]{3,1,0,2:T(2,128)(2,1)}), bf16[20,2,80,320]{3,1,0,2:T(2,128)(2,1)}) %all-gather.3.cloned.1.call-update) | async-done | bytes 2048016 | tf_op jit(solution)/shard_map/all_gather | solution.py:36
  74.4 3.4 %copy.70 = bf16[20,2,80,320]{3,2,1,0:T(8,128)(2,1)} copy(bf16[20,2,80,320]{3,1,0,2:T(2,128)(2,1)} %all-gather.3.cloned.1.call-done) | data formatting | bytes 4096000 | tf_op jit(solution)/shard_map/all_gather | solution.py:36
  79.4 7.9 %add_bitcast_fusion.26 = (f32[20,1280]{1,0:T(8,128)}, f32[20,1280]{1,0:T(8,128)}, f32[20,1280]{1,0:T(8,128)}, f32[20,1280]{1,0:T(8,128)}, f32[20,1280]{1,0:T(8,1...) fusion(pred[1,20,1280]{2,1,0:T(8,128)(4,1)S(1)} %get-tuple-elem, ...), kind=kLoop, calls=%fused_computation.187 | loop fusion | flops 844800 | bytes 1331244 | tf_op jit(solution)/shard_map/mul | solution.py:50
  87.2 8.8 %add_bitcast_fusion.40 = (f32[20,1280]{1,0:T(8,128)}, f32[20,1280]{1,0:T(8,128)}, f32[20,1280]{1,0:T(8,128)}, f32[20,1280]{1,0:T(8,128)}, f32[20,1280]{1,0:T(8,1...) fusion(pred[1,20,1280]{2,1,0:T(8,128)(4,1)S(1)} %get-tuple-elem, ...), kind=kLoop, calls=%fused_computation.201 | loop fusion | flops 921600 | bytes 1408048 | tf_op jit(solution)/shard_map/mul | solution.py:50
  96.0 8.9 %add_bitcast_fusion.38 = (f32[20,1280]{1,0:T(8,128)}, f32[20,1280]{1,0:T(8,128)}, f32[20,1280]{1,0:T(8,128)}, f32[20,1280]{1,0:T(8,128)}, f32[20,1280]{1,0:T(8,1...) fusion(pred[1,20,1280]{2,1,0:T(8,128)(4,1)S(1)} %get-tuple-elem, ...), kind=kLoop, calls=%fused_computation.199 | loop fusion | flops 921600 | bytes 1408048 | tf_op jit(solution)/shard_map/mul | solution.py:50
  104.9 14.8 %cosine_multiply_fusion.1 = (f32[1280,640,1]{1,0,2:T(8,128)}, f32[1280,640,1]{1,0,2:T(8,128)}) fusion(s32[640]{0:T(1024)S(1)} %copy-done.41), kind=kLoop, calls=%fused_computation.24 | loop fusion | flops 9830400 | bytes 6556160 | tf_op jit(solution)/shard_map/mul | solution.py:63
  127.6 13.0 %fusion.35 = f32[2,20,1280]{2,0,1:T(2,128)S(1)} fusion(f32[2,23,1280]{2,0,1:T(2,128)S(1)} %constant_dynamic-update-slice_fusion.2, f32[2,20,1278]{2,0,1:T(2,128)S(1)} %get-tuple-element.95, f32[2,20,2]{2,0,1:T(2,128)S(1)} %get-tuple-element.89, f32[2,20,1279]{2,0,1:T(2,128)S(1)} %get-tuple-element.107, f32[2,20,1]{2,0,1:T(2,128)S(1)} %get-tuple-element.101, ...), kind=kLoop, calls=%fused_computation.46 | loop fusion | flops 7116800 | bytes 15257600 | tf_op jit(solution)/shard_map/add | solution.py:50
  140.7 4.2 %fusion.4 = f32[640,2,2,20]{0,3,2,1:T(8,128)S(1)} fusion(f32[1280,640,1]{1,0,2:T(8,128)S(1)} %copy-done.3, f32[1280,640,1]{1,0,2:T(8,128)S(1)} %copy-done.2, f32[2,20,1280]{2,0,1:T(2,128)S(1)} %fusion.35), kind=kOutput, calls=%fused_computation.5 | convolution fusion | flops 788070400 | bytes 6963200 | tf_op jit(solution)/shard_map/lij,jrc->rcli/dot_general | solution.py:102
  145.8 2.9 reshape.275
  148.7 11.9 %all-to-all-start = ((f32[32,1,1600]{2,1,0:T(1,128)}), f32[32,1,1600]{2,1,0:T(1,128)S(1)}, u32[]{:S(2)}, u32[]{:S(2)}) async-start(f32[32,1,1600]{2,1,0:T(1,128)} %reshape.275), calls=%async_computation | async-start | bytes 425984 | tf_op jit(solution)/shard_map/all_to_all | solution.py:105
  160.8 14.2 %all-to-all-done = f32[32,1,1600]{2,1,0:T(1,128)S(1)} async-done(((f32[32,1,1600]{2,1,0:T(1,128)}), f32[32,1,1600]{2,1,0:T(1,128)S(1)}, u32[]{:S(2)}, u32[]{:S(2)}) %all-to-all-start) | async-done | bytes 204832 | tf_op jit(solution)/shard_map/all_to_all | solution.py:105
  175.6 1.1 reduce
  176.7 2.1 reshape.276
  179.3 1.2 all_to_all.55
  181.5 6.8 %fusion.22 = f32[20,2,320,2,2]{2,4,3,1,0:T(2,128)S(1)} fusion(bf16[20,2,320,320]{3,2,1,0:T(8,128)(2,1)} %all-gather.5.cloned.1.call-done, bf16[20,1,2,2,320]{4,3,2,1,0:T(2,128)(2,1)S(1)} %fusion.85, bf16[20,1,2,2,320]{4,3,2,1,0:T(2,128)(2,1)S(1)} %get-tuple-element.10), kind=kOutput, calls=%fused_computation.35 | convolution fusion | flops 32972800 | bytes 8499200 | tf_op jit(solution)/shard_map/rpij,rpclj->rpicl/dot_general | solution.py:111
  189.1 2.9 reshape.277
  192.0 7.0 %all-to-all-start.1 = ((f32[16,1,3200]{2,1,0:T(1,128)}), f32[16,1,3200]{2,1,0:T(1,128)S(1)}, u32[]{:S(2)}, u32[]{:S(2)}) async-start(f32[16,1,3200]{2,1,0:T(1,128)} %reshape.277), calls=%async_computation.1 | async-start | bytes 409600 | tf_op jit(solution)/shard_map/all_to_all | solution.py:114
  199.1 1.0 multiply_add_fusion
  200.0 6.8 %all-to-all-done.1 = f32[16,1,3200]{2,1,0:T(1,128)S(1)} async-done(((f32[16,1,3200]{2,1,0:T(1,128)}), f32[16,1,3200]{2,1,0:T(1,128)S(1)}, u32[]{:S(2)}, u32[]{:S(2)}) %all-to-all-start.1) | async-done | bytes 204832 | tf_op jit(solution)/shard_map/all_to_all | solution.py:114
  206.9 1.1 reduce.1
  208.0 2.2 reshape.278
  210.1 2.4 copy.72
  212.6 3.3 %convolution_divide_fusion = f32[20,2,20,2,32]{4,2,3,1,0:T(8,128)S(1)} fusion(f32[20,2,20,2,32]{2,4,3,1,0:T(8,128)S(1)} %bitcast.257, f32[20,2,20]{2,1,0:T(2,128)S(1)} %compare_convert_fusion, f32[20,2,20,32]{3,2,1,0:T(8,128)} %multiply_add_fusion, f32[32,32]{1,0:T(8,128)S(1)} %copy-done.43), kind=kOutput, calls=%fused_computation.31 | convolution fusion | flops 19763200 | bytes 519296 | tf_op jit(solution)/shard_map/kq,rpicq->rpick/dot_general | solution.py:90
  217.6 1.4 reshape.279
  219.0 5.3 %all-to-all-start.2 = ((bf16[16,2,1600]{2,1,0:T(2,128)(2,1)}), bf16[16,2,1600]{2,1,0:T(2,128)(2,1)S(1)}, u32[]{:S(2)}, u32[]{:S(2)}) async-start(bf16[16,2,1600]{2,1,0:T(2,128)(2,1)} %reshape.279), calls=%async_computation.2 | async-start | bytes 212992 | tf_op jit(solution)/shard_map/all_to_all | solution.py:117
  224.4 7.2 %all-to-all-done.2 = bf16[16,2,1600]{2,1,0:T(2,128)(2,1)S(1)} async-done(((bf16[16,2,1600]{2,1,0:T(2,128)(2,1)}), bf16[16,2,1600]{2,1,0:T(2,128)(2,1)S(1)}, u32[]{:S(2)}, u32[]{:S(2)}) %all-to-all-start.2) | async-done | bytes 102432 | tf_op jit(solution)/shard_map/all_to_all | solution.py:117
  233.6 5.5 %fusion.25 = f32[2,20,2,2,320]{4,0,3,2,1:T(2,128)S(1)} fusion(bf16[20,2,320,2,2]{2,4,3,1,0:T(2,128)(2,1)S(1)} %all_to_all.63, bf16[20,2,320,320]{3,2,1,0:T(8,128)(2,1)} %all-gather.5.cloned.1.call-done), kind=kOutput, calls=%fused_computation.36 | convolution fusion | flops 32768000 | bytes 8499200 | tf_op jit(solution)/shard_map/rpij,rpicl->lrpcj/dot_general | solution.py:118
  240.2 1.4 copy.80
  241.6 2.9 reshape.281
  244.5 9.6 %all-to-all-start.3 = ((f32[32,1,1600]{2,1,0:T(1,128)}), f32[32,1,1600]{2,1,0:T(1,128)S(1)}, u32[]{:S(2)}, u32[]{:S(2)}) async-start(f32[32,1,1600]{2,1,0:T(1,128)} %reshape.281), calls=%async_computation.3 | async-start | bytes 425984 | tf_op jit(solution)/shard_map/all_to_all | solution.py:124
  254.1 16.0 %cosine_multiply_fusion = (f32[640,1,1280]{2,0,1:T(8,128)}, f32[640,1,1280]{2,0,1:T(8,128)}) fusion(f32[640]{0:T(1024)S(1)} %select_multiply_fusion, s32[640]{0:T(1024)S(1)} %copy-done.41), kind=kLoop, calls=%fused_computation.19 | loop fusion | flops 9830400 | bytes 6558720 | tf_op jit(solution)/shard_map/mul | solution.py:69
  270.5 1.5 reshape.267
  272.0 1.1 reduce.2
  273.1 2.1 reshape.282
  275.7 1.2 all_to_all.67
  276.8 5.7 %fusion.20 = f32[2,20,1280]{2,1,0:T(8,128)S(1)} fusion(f32[640,1,1280]{2,0,1:T(8,128)} %get-tuple-element.185, f32[640,1,1280]{2,0,1:T(8,128)} %get-tuple-element.184, f32[2,640,2,20]{1,2,3,0:T(2,128)S(1)} %all_to_all.67), kind=kOutput, calls=%fused_computation.30 | convolution fusion | flops 788070400 | bytes 6963200 | tf_op jit(solution)/shard_map/lrci,rcj->lij/dot_general | solution.py:125
  (144 shorter events, 19.9 us)
Async XLA Ops:
  7.2 208.7 %copy-start = (f32[32,32]{1,0:T(8,128)S(1)}, f32[32,32]{1,0:T(8,128)}, u32[]{:S(2)}) copy-start(f32[32,32]{1,0:T(8,128)} %param.14) | copy-start | bytes 12292
  7.2 67.2 %all-gather.3.cloned.1.call-start = ((), (), s32[]{:S(2)}) async-start(), calls=%async_computation.4 | async-start | bytes 3072000 | tf_op jit(solution)/shard_map/all_gather | solution.py:36
  9.6 171.9 %all-gather.5.cloned.1.call-start = ((), (), s32[]{:S(2)}) async-start(), calls=%async_computation.5 | async-start | bytes 12288000 | tf_op jit(solution)/shard_map/all_gather | solution.py:36
  11.0 108.7 %collective-permute-start = (f32[2,3,1280]{2,0,1:T(2,128)}, f32[2,3,1280]{2,0,1:T(2,128)}, u32[]{:S(2)}, u32[]{:S(2)}) collective-permute-start(f32[2,3,1280]{2,0,1:T(2,128)} %get-tuple-element.115), channel_id=1, source_target_pairs={{0,16},{16,32},{32,48},{48,64},{64,80},{80,96},{96,112},{112,128},... | collective-permute-start | bytes 92168 | tf_op jit(solution)/shard_map/ppermute | solution.py:24
  23.0 97.6 %collective-permute-start.1 = (f32[2,3,1280]{2,0,1:T(2,128)}, f32[2,3,1280]{2,0,1:T(2,128)}, u32[]{:S(2)}, u32[]{:S(2)}) collective-permute-start(f32[2,3,1280]{2,0,1:T(2,128)} %get-tuple-element.116), channel_id=1, source_target_pairs={{16,0},{32,16},{48,32},{64,48},{80,64},{96,80},{112,96},{128,112},... | collective-permute-start | bytes 92168 | tf_op jit(solution)/shard_map/ppermute | solution.py:26
  44.8 33.0 %copy-start.1 = (f32[2,20,1280]{2,0,1:T(2,128)S(1)}, f32[2,20,1280]{2,0,1:T(2,128)}, u32[]{:S(2)}) copy-start(f32[2,20,1280]{2,0,1:T(2,128)} %param.8) | copy-start | bytes 614404
  78.8 26.1 %copy-start.41 = (s32[640]{0:T(1024)S(1)}, s32[640]{0:T(1024)}, u32[]{:S(2)}) copy-start(s32[640]{0:T(1024)} %param.11) | copy-start | bytes 7684
  124.5 2.7 copy-start.4
  124.5 2.7 copy-start.5
  124.6 2.7 copy-start.6
  124.6 2.7 copy-start.7
  124.6 2.7 copy-start.8
  124.6 2.7 copy-start.9
  124.6 2.7 copy-start.10
  124.6 2.7 copy-start.11
  124.6 2.7 copy-start.12
  124.6 2.7 copy-start.13
  124.6 2.7 copy-start.14
  124.7 2.7 copy-start.15
  124.7 2.7 copy-start.16
  124.7 2.7 copy-start.17
  124.7 2.7 copy-start.18
  124.7 2.7 copy-start.19
  124.7 2.7 copy-start.20
  124.7 2.7 copy-start.21
  124.7 2.7 copy-start.22
  124.7 2.7 copy-start.23
  124.7 2.7 copy-start.24
  124.8 2.7 copy-start.25
  124.8 2.7 copy-start.26
  124.8 2.7 copy-start.27
  124.8 2.7 copy-start.28
  124.8 2.7 copy-start.29
  124.8 2.7 copy-start.30
  124.8 2.7 copy-start.31
  124.8 2.7 copy-start.32
  124.8 2.7 copy-start.33
  124.8 2.7 copy-start.34
  124.9 2.7 copy-start.35
  124.9 2.7 copy-start.36
  127.6 13.1 %copy-start.2 = (f32[1280,640,1]{1,0,2:T(8,128)S(1)}, f32[1280,640,1]{1,0,2:T(8,128)}, u32[]{:S(2)}) copy-start(f32[1280,640,1]{1,0,2:T(8,128)} %get-tuple-element.235) | copy-start | bytes 9830404
  127.6 13.1 %copy-start.3 = (f32[1280,640,1]{1,0,2:T(8,128)S(1)}, f32[1280,640,1]{1,0,2:T(8,128)}, u32[]{:S(2)}) copy-start(f32[1280,640,1]{1,0,2:T(8,128)} %get-tuple-element.236) | copy-start | bytes 9830404
  148.7 26.3 %all-to-all-start = ((f32[32,1,1600]{2,1,0:T(1,128)}), f32[32,1,1600]{2,1,0:T(1,128)S(1)}, u32[]{:S(2)}, u32[]{:S(2)}) async-start(f32[32,1,1600]{2,1,0:T(1,128)} %reshape.275), calls=%async_computation | async-start | bytes 425984 | tf_op jit(solution)/shard_map/all_to_all | solution.py:105
  188.2 10.8 %copy-start.42 = (f32[32]{0:T(128)S(1)}, f32[32]{0:T(128)}, u32[]{:S(2)}) copy-start(f32[32]{0:T(128)} %param.13) | copy-start | bytes 388
  189.1 23.4 %copy-start.43 = (f32[32,32]{1,0:T(8,128)S(1)}, f32[32,32]{1,0:T(8,128)}, u32[]{:S(2)}) copy-start(f32[32,32]{1,0:T(8,128)} %param.15) | copy-start | bytes 12292
  192.0 14.8 %all-to-all-start.1 = ((f32[16,1,3200]{2,1,0:T(1,128)}), f32[16,1,3200]{2,1,0:T(1,128)S(1)}, u32[]{:S(2)}, u32[]{:S(2)}) async-start(f32[16,1,3200]{2,1,0:T(1,128)} %reshape.277), calls=%async_computation.1 | async-start | bytes 409600 | tf_op jit(solution)/shard_map/all_to_all | solution.py:114
  219.0 12.5 %all-to-all-start.2 = ((bf16[16,2,1600]{2,1,0:T(2,128)(2,1)}), bf16[16,2,1600]{2,1,0:T(2,128)(2,1)S(1)}, u32[]{:S(2)}, u32[]{:S(2)}) async-start(bf16[16,2,1600]{2,1,0:T(2,128)(2,1)} %reshape.279), calls=%async_computation.2 | async-start | bytes 212992 | tf_op jit(solution)/shard_map/all_to_all | solution.py:117
  244.5 27.5 %all-to-all-start.3 = ((f32[32,1,1600]{2,1,0:T(1,128)}), f32[32,1,1600]{2,1,0:T(1,128)S(1)}, u32[]{:S(2)}, u32[]{:S(2)}) async-start(f32[32,1,1600]{2,1,0:T(1,128)} %reshape.281), calls=%async_computation.3 | async-start | bytes 425984 | tf_op jit(solution)/shard_map/all_to_all | solution.py:124
  (4 other events, 10.8 us)
Sparse Core Ops, SparseCore 0:
  10.1 64.2 all-gather.2
  77.9 100.2 all-gather.4
where the time goes:
time: 295 us; the launch traced here: 290 us
  other arithmetic  84.3 us (29%)
  local copies, waits for them, and re-layouts  58.7 us (20%)
  waiting for transfers between devices  57.8 us (20%)
  starting transfers between devices  47.9 us (16%)
  matrix products  26.4 us (9%)
  between operations  15.4 us (5%)
    mul x6, other arithmetic, transport(): (stencil[row_step + 3, col_step + 3] + picked)[None, :, :] * shifted  35.4 us
    all_gather x2, waiting for transfers between devices, whole_of(): nearer = lax.all_gather(value, axes[-1], axis=dim, tiled=True)  29.5 us
    unnamed x102, local copies, waits for them, and re-layouts  22.7 us
    mul x1, other arithmetic, inverse_table(): cosines = jnp.cos(angles).T * weights[:, None]  16 us
    mul x1, other arithmetic, forward_table(): jnp.cos(angles) * norm_scale  14.8 us
    all_to_all x1, waiting for transfers between devices, on_device(): lax.all_to_all(fourier, 'lat', split_axis=0, concat_axis=3, tiled=True)  14.2 us
    add x1, other arithmetic, transport(): summed + (stencil[row_step + 3, col_step + 3] + picked)[None, :, :] * shi...  13 us
    ppermute x1, starting transfers between devices, padded_2(): lax.ppermute(tail, axis, [(i, (i + 1) % count) for i in range(ends)])  12 us
  transfers between devices with their start and end apart: 8, of which 4 were waited for; matrix products, arithmetic and copies ran while one was open for 41% of the time, Pallas kernels for 0%

commit v1 on v0

v1 whole, which is shorter than its diff:
```python
import functools
import math

import jax
import jax.numpy as jnp
from jax import lax
from jax.experimental import pallas as pl
from jax.experimental.pallas import tpu as pltpu
from jax.sharding import PartitionSpec as P

INTERPRET = False
N_LAT, N_LEV = 32, 16
N_DEV = N_LAT * N_LEV
M = 640
NLON, HALF_LON = 1280, 640
ROWS = 20
LV = 2
NLEV = 32
QB = 40
QP = N_LEV * QB
HL = 320
SLOTS = 20
MSG = LV * ROWS
F32, BF16 = jnp.float32, jnp.bfloat16
NT = (((1,), (1,)), ((), ()))
NN = (((1,), (0,)), ((), ()))
HIGH = lax.Precision.HIGHEST


def first_rc(b):
    return (5 * b) >> 1


def call(kernel, out_shape, in_specs, scratch, name, flops=10**7):
    many = isinstance(out_shape, (tuple, list))
    vm = pl.BlockSpec(memory_space=pltpu.VMEM)
    return pl.pallas_call(
        kernel,
        out_shape=out_shape,
        in_specs=in_specs,
        out_specs=[vm] * len(out_shape) if many else vm,
        scratch_shapes=scratch,
        name=name,
        interpret=INTERPRET,
        cost_estimate=pl.CostEstimate(flops=flops, bytes_accessed=10**6, transcendentals=0),
    )


VM = pl.BlockSpec(memory_space=pltpu.VMEM)
ANY = pl.BlockSpec(memory_space=pl.ANY)
SM = pl.BlockSpec(memory_space=pltpu.SMEM)


def cos_sin(phase):
    quad = jnp.floor((phase + 160.5) * (1.0 / 320.0))
    x = (phase - 320.0 * quad) * (2.0 * math.pi / NLON)
    z = x * x
    s = x * (1.0 + z * (-1.6666654611e-1 + z * (8.3321608736e-3 - z * 1.9515295891e-4)))
    c = 1.0 - 0.5 * z + z * z * (
        4.166664568298827e-2 + z * (-1.388731625493765e-3 + z * 2.443315711809948e-5)
    )
    odd = jnp.logical_or(quad == 1.0, quad == 3.0)
    c, s = jnp.where(odd, s, c), jnp.where(odd, c, s)
    c = jnp.where(jnp.logical_or(quad == 1.0, quad == 2.0), -c, c)
    s = jnp.where(jnp.logical_or(quad == 2.0, quad == 3.0), -s, s)
    return c, s


def wrapped(count):
    return count - NLON * jnp.floor((count + 0.5) * (1.0 / NLON))


CHUNK = 64


def tables_kernel(assign_ref, t_ref, even_ref, weight_ref):
    slots = lax.broadcasted_iota(jnp.int32, (CHUNK, M), 1)
    lane = lax.broadcasted_iota(jnp.int32, (CHUNK, 128), 1)
    lane_f = lane.astype(F32)
    assign = assign_ref[...]

    def step(i, carry):
        r0 = pl.multiple_of(i * CHUNK, CHUNK)
        d = r0 + lax.broadcasted_iota(jnp.int32, (CHUNK, 1), 0)
        rc0 = ((d & 15) * 5) >> 1
        evens, weights, waves = [], [], []
        for j in range(3):
            slot = (d >> 4) * SLOTS + ((rc0 + j) >> 1)
            waves.append(jnp.sum(jnp.where(slots == slot, assign, 0.0), axis=1, keepdims=True))
            evens.append(jnp.where(waves[j] == 2.0 * jnp.floor(waves[j] * 0.5), 1.0, 0.0))
            weights.append(jnp.where(waves[j] == 0.0, 1.0, 2.0))
        packed = jnp.where(lane == 0, waves[0], jnp.where(lane == 1, waves[1], waves[2]))
        turn_c, turn_s = cos_sin(wrapped(packed * 128.0))
        for j in range(3):
            quarter = jnp.where(((rc0 + j) & 1) == 1, 320.0, 0.0)
            c, s = cos_sin(wrapped(waves[j] * lane_f + quarter))
            c = c * (1.0 / math.sqrt(NLON))
            s = s * (1.0 / math.sqrt(NLON))
            cd, sd = turn_c[:, j : j + 1], turn_s[:, j : j + 1]
            for block in range(5):
                high = c.astype(BF16)
                t_ref[j, pl.ds(r0, CHUNK), 128 * block : 128 * block + 128] = high
                t_ref[
                    j, pl.ds(r0, CHUNK), HALF_LON + 128 * block : HALF_LON + 128 * block + 128
                ] = (c - high.astype(F32)).astype(BF16)
                if block < 4:
                    c, s = c * cd - s * sd, s * cd + c * sd
        even_ref[pl.ds(r0, CHUNK), :] = jnp.where(
            lane < MSG, evens[0], jnp.where(lane < 2 * MSG, evens[1], evens[2])
        )
        weight_ref[pl.ds(r0, CHUNK), :] = jnp.where(
            lane < MSG, weights[0], jnp.where(lane < 2 * MSG, weights[1], weights[2])
        )
        return carry

    lax.fori_loop(0, N_DEV // CHUNK, step, 0)


def tables(assign):
    return call(
        tables_kernel,
        (
            jax.ShapeDtypeStruct((3, N_DEV, NLON), BF16),
            jax.ShapeDtypeStruct((N_DEV, 128), F32),
            jax.ShapeDtypeStruct((N_DEV, 128), F32),
        ),
        [VM],
        [],
        "tables",
    )(assign.astype(F32).reshape(1, M))


def forward_kernel(
    stencil_ref,
    tracer_ref,
    north_ref,
    south_ref,
    off_ref,
    t_any,
    even_ref,
    out_ref,
    pad,
    rolled,
    codes,
    adv,
    fe,
    fo,
    t_ref,
    t_sem,
):
    fetch = pltpu.make_async_copy(t_any, t_ref, t_sem)
    fetch.start()
    pad[...] = jnp.zeros((64, NLON), F32)
    for i in range(3):
        pad[2 + 2 * i : 4 + 2 * i, :] = north_ref[i]
        pad[48 + 2 * i : 50 + 2 * i, :] = south_ref[i]
    for i in range(ROWS):
        pad[8 + 2 * i : 10 + 2 * i, :] = tracer_ref[i]
        codes[2 * i : 2 * i + 2, :] = off_ref[i]
    for bi in range(7):
        shift = (3 - bi) % NLON
        rolled[bi] = pltpu.roll(pad[...], shift, 1) if shift else pad[...]

    first = (lax.broadcasted_iota(jnp.int32, (2 * ROWS, 128), 0) & 1) == 0

    def chunk(ci, carry):
        l0 = pl.multiple_of(ci * 128, 128)
        value = codes[:, pl.ds(l0, 128)]
        part = jnp.where(first, value * 7, value)
        code = part + jnp.where(first, jnp.roll(part, -1, 0), jnp.roll(part, 1, 0))
        acc = jnp.zeros((2 * ROWS, 128), F32)
        for ai in range(7):
            for bi in range(7):
                s = stencil_ref[ai, bi]
                w = jnp.where(code == (ai - 3) * 7 + (bi - 3), s + 1.0, s)
                acc = acc + w * rolled[bi, 2 + 2 * ai : 42 + 2 * ai, pl.ds(l0, 128)]
        adv[ci] = acc
        return carry

    lax.fori_loop(0, NLON // 128, chunk, 0)
    levels = [
        jnp.concatenate([every_other(adv, ci, k) for ci in range(NLON // 128)], axis=1) for k in range(LV)
    ]
    x = jnp.concatenate(
        [v[:, :HALF_LON] + v[:, HALF_LON:] for v in levels] + [v[:, :HALF_LON] - v[:, HALF_LON:] for v in levels], axis=0
    )
    high = x.astype(BF16)
    low = (x - high.astype(F32)).astype(BF16)
    right = jnp.concatenate(
        [
            jnp.concatenate([high, high], axis=1),
            jnp.concatenate([low, jnp.zeros_like(low)], axis=1),
        ],
        axis=0,
    )
    fe[...] = jnp.zeros((N_DEV, 128), F32)
    fo[...] = jnp.zeros((N_DEV, 128), F32)
    fetch.wait()
    for j in range(3):
        prod = lax.dot_general(t_ref[j], right, NT, preferred_element_type=F32)
        fe[:, MSG * j : MSG * (j + 1)] = prod[:, 0:MSG] + prod[:, 2 * MSG : 3 * MSG]
        fo[:, MSG * j : MSG * (j + 1)] = prod[:, MSG : 2 * MSG] + prod[:, 3 * MSG : 4 * MSG]
    out_ref[...] = jnp.where(even_ref[...] > 0.5, fe[...], fo[...])


def every_other(ref, ci, k):
    return ref[ci][k::2] if INTERPRET else ref[ci, pl.ds(k, ROWS, 2), :]


def forward(stencil, tracer, north, south, offsets, table, even):
    return call(
        forward_kernel,
        jax.ShapeDtypeStruct((N_DEV, 128), F32),
        [SM, VM, VM, VM, VM, ANY, VM],
        [
            pltpu.VMEM((64, NLON), F32),
            pltpu.VMEM((7, 64, NLON), F32),
            pltpu.VMEM((2 * ROWS, NLON), jnp.int32),
            pltpu.VMEM((NLON // 128, 2 * ROWS, 128), F32),
            pltpu.VMEM((N_DEV, 128), F32),
            pltpu.VMEM((N_DEV, 128), F32),
            pltpu.VMEM((3, N_DEV, NLON), BF16),
            pltpu.SemaphoreType.DMA,
        ],
        "forward",
        10**9,
    )(stencil, tracer, north, south, offsets, table, even)


def mirror_matrix():
    src = lax.broadcasted_iota(jnp.int32, (128, 128), 0)
    dst = lax.broadcasted_iota(jnp.int32, (128, 128), 1)
    hit = jnp.zeros((128, 128), jnp.bool_)
    for g in range(6):
        hit = jnp.logical_or(
            hit, jnp.logical_and(jnp.logical_and(dst >= 20 * g, dst < 20 * g + 20), src + dst == 40 * g + 19)
        )
    return hit.astype(F32)


def spectral_kernel(
    info_ref, msg_ref, table_ref, damping_ref, inv_ref, vec_ref, vecp_ref, out_ref, spec_ref, nbuf, sbuf, flip, zn, zs, sall
):
    mirror = mirror_matrix()
    half = N_DEV // 2
    flip[...] = lax.dot_general(msg_ref[half:, :], mirror, NN, precision=HIGH, preferred_element_type=F32)
    for a in range(N_LAT // 2):
        top = msg_ref[16 * a : 16 * a + 16, :]
        low = flip[16 * (15 - a) : 16 * (15 - a) + 16, :]
        for j in range(3):
            for k in range(LV):
                lane = MSG * j + ROWS * k
                nbuf[j, 16 * k : 16 * k + 16, ROWS * a : ROWS * a + ROWS] = top[:, lane : lane + ROWS]
                sbuf[j, 16 * k : 16 * k + 16, ROWS * a : ROWS * a + ROWS] = low[:, lane : lane + ROWS]
    parity = info_ref[2]
    lev_odd = info_ref[3]
    lane = lax.broadcasted_iota(jnp.int32, (32, QP), 1)
    odd = lane & 1
    damp = damping_ref[...]
    matrix = [table_ref[0], table_ref[parity], table_ref[1]]
    degree = [
        lane + (info_ref[0] if j == 0 else (info_ref[1] if j == 2 else jnp.where(parity == 1, info_ref[1], info_ref[0])))
        for j in range(3)
    ]
    for j in range(3):
        north, south = nbuf[j], sbuf[j]
        hemi = jnp.concatenate([north + south, north - south], axis=0).astype(BF16)
        prod = lax.dot_general(hemi, matrix[j], NT, preferred_element_type=F32)
        keep = degree[j] <= M - 1
        if j == 0:
            keep = jnp.logical_and(keep, odd >= lev_odd)
        if j == 2:
            keep = jnp.logical_and(keep, odd <= lev_odd)
        sall[32 * j : 32 * j + 32, :] = jnp.where(keep, jnp.where(odd == 1, prod[32:], prod[:32]), 0.0)
    modal = lax.dot_general(inv_ref[...], sall[...], NN, precision=HIGH, preferred_element_type=F32)
    for j in range(3):
        n = degree[j].astype(F32)
        growth = n * (n + 1.0) / float(M * M)
        sall[32 * j : 32 * j + 32, :] = modal[32 * j : 32 * j + 32, :] / (1.0 + growth * damp)
    modal = sall[...]
    solved = lax.dot_general(vec_ref[...], modal, NN, precision=HIGH, preferred_element_type=F32).T
    for b in range(N_LEV):
        spec_ref[b] = solved[QB * b : QB * b + QB].astype(BF16)
    sall[...] = lax.dot_general(vecp_ref[...], modal, NN, precision=HIGH, preferred_element_type=F32)
    for j in range(3):
        mine = sall[32 * j : 32 * j + 32, :]
        left = jnp.concatenate([mine, jnp.where(odd == 1, -mine, mine)], axis=0).astype(BF16)
        both = lax.dot_general(left, matrix[j], NN, preferred_element_type=F32)
        zn[j] = both[:32]
        zs[j] = both[32:]
    out_ref[...] = jnp.zeros((N_DEV, 128), F32)
    flip[...] = jnp.zeros((half, 128), F32)
    for a in range(N_LAT // 2):
        for j in range(3):
            for k in range(LV):
                lane = MSG * j + ROWS * k
                out_ref[16 * a : 16 * a + 16, lane : lane + ROWS] = zn[j, 16 * k : 16 * k + 16, ROWS * a : ROWS * a + ROWS]
                flip[16 * (15 - a) : 16 * (15 - a) + 16, lane : lane + ROWS] = zs[
                    j, 16 * k : 16 * k + 16, ROWS * a : ROWS * a + ROWS
                ]
    out_ref[half:, :] = lax.dot_general(flip[...], mirror, NN, precision=HIGH, preferred_element_type=F32)


def spectral(info, msgs, table, damping, inv, vec, vecp):
    return call(
        spectral_kernel,
        (jax.ShapeDtypeStruct((N_DEV, 128), F32), jax.ShapeDtypeStruct((N_LEV, QB, 96), BF16)),
        [SM, VM, VM, VM, VM, VM, VM],
        [
            pltpu.VMEM((3, 32, HL), F32),
            pltpu.VMEM((3, 32, HL), F32),
            pltpu.VMEM((N_DEV // 2, 128), F32),
            pltpu.VMEM((3, 32, HL), F32),
            pltpu.VMEM((3, 32, HL), F32),
            pltpu.VMEM((96, QP), F32),
        ],
        "spectral",
        10**9,
    )(info, msgs, table, damping, inv, vec, vecp)


def inverse_kernel(msg_ref, t_any, even_ref, weight_ref, out_ref, t_ref, t_sem):
    fetch = pltpu.make_async_copy(t_any.at[:, :, pl.ds(0, HALF_LON)], t_ref, t_sem)
    fetch.start()
    lane = lax.broadcasted_iota(jnp.int32, (N_DEV, 128), 1)
    scaled = jnp.where(lane < 3 * MSG, msg_ref[...] * weight_ref[...], 0.0)
    even = (scaled * even_ref[...]).T
    odd = (scaled * (1.0 - even_ref[...])).T
    total = jnp.zeros((2 * MSG, HALF_LON), F32)
    fetch.wait()
    for j in range(3):
        left = jnp.concatenate([even[MSG * j : MSG * (j + 1)], odd[MSG * j : MSG * (j + 1)]], axis=0).astype(BF16)
        total = total + lax.dot_general(left, t_ref[j], NN, preferred_element_type=F32)
    near = total[:MSG] + total[MSG:]
    far = total[:MSG] - total[MSG:]
    for k in range(LV):
        out_ref[:, k, :HALF_LON] = near[ROWS * k : ROWS * (k + 1)]
        out_ref[:, k, HALF_LON:] = far[ROWS * k : ROWS * (k + 1)]


def inverse(msgs, table, even, weight):
    return call(
        inverse_kernel,
        jax.ShapeDtypeStruct((ROWS, LV, NLON), F32),
        [VM, ANY, VM, VM],
        [pltpu.VMEM((3, N_DEV, HALF_LON), BF16), pltpu.SemaphoreType.DMA],
        "inverse",
        10**8,
    )(msgs, table, even, weight)


def place_kernel(spec_ref, out_ref):
    for slot in range(SLOTS):
        for c in range(2):
            w, o = divmod(2 * slot + c, 5)
            parts = []
            if o <= 2:
                parts.append((2 * w, o))
            if o >= 2:
                parts.append((2 * w + 1, o - 2))
            value = sum(spec_ref[b, :, 32 * j : 32 * j + 32].astype(F32) for b, j in parts)
            out_ref[slot, :, 32 * c : 32 * c + 32] = value


def place(spec):
    return call(place_kernel, jax.ShapeDtypeStruct((SLOTS, QB, 64), F32), [VM], [], "place", 10**6)(spec)


def by_block(matrix):
    return jnp.kron(jnp.eye(3, dtype=F32), matrix)


def level_order(value, axis):
    shape = value.shape
    split = shape[:axis] + (16, 2) + shape[axis + 1 :]
    return jnp.swapaxes(value.reshape(split), axis, axis + 1).reshape(shape)


def send_kernel(table_ref, out_ref, sems):
    copies = []
    for b in range(N_LEV):
        first = first_rc(b) >> 1
        copies.append(pltpu.make_async_copy(table_ref.at[pl.ds(first, 2)], out_ref.at[b], sems.at[b]))
    for copy in copies:
        copy.start()
    for copy in copies:
        copy.wait()


def send_tables(legendre):
    return pl.pallas_call(
        send_kernel,
        out_shape=jax.ShapeDtypeStruct((N_LEV, 2, 20, 2, HL), BF16),
        in_specs=[ANY],
        out_specs=ANY,
        scratch_shapes=[pltpu.SemaphoreType.DMA((N_LEV,))],
        name="send_tables",
        interpret=INTERPRET,
        cost_estimate=pl.CostEstimate(flops=10**6, bytes_accessed=2 * 10**6, transcendentals=0),
    )(jnp.swapaxes(legendre, 1, 2))


def received_tables(got):
    return jnp.swapaxes(got, 0, 1).reshape(2, QP, HL)


def exchange(value, axes):
    return lax.all_to_all(value, axes, split_axis=0, concat_axis=0, tiled=True)


def on_device(tracer, offsets, stencil, assign, legendre, damping, vert_vecs, vert_inv):
    up = [(i, i + 1) for i in range(N_LAT - 1)]
    down = [(i + 1, i) for i in range(N_LAT - 1)]
    rows = jnp.swapaxes(tracer, 0, 1)
    north = lax.ppermute(rows[ROWS - 3 :], "lat", up)
    south = lax.ppermute(rows[:3], "lat", down)
    table, even, weight = tables(assign)
    with jax.named_scope("tabx"):
        matrices = exchange(send_tables(legendre), "lev")
    matrices = received_tables(matrices)
    msgs = forward(stencil, rows, north, south, jnp.swapaxes(offsets, 0, 1), table, even)
    with jax.named_scope("fwdx"):
        got = exchange(msgs.reshape(N_DEV, 1, 128), ("lat", "lev")).reshape(N_DEV, 128)
    lev = lax.axis_index("lev")
    rc0 = (5 * lev) >> 1
    waves = lax.dynamic_slice_in_dim(assign, lax.axis_index("lat") * SLOTS + (rc0 >> 1), 2)
    info = jnp.concatenate([waves, jnp.stack([rc0 & 1, lev & 1])]).astype(jnp.int32)
    back, spec = spectral(
        info,
        got,
        matrices,
        damping.reshape(32, 1),
        by_block(level_order(vert_inv, 1)),
        by_block(vert_vecs),
        by_block(level_order(vert_vecs, 0)),
    )
    with jax.named_scope("bwdx"):
        home = exchange(back.reshape(N_DEV, 1, 128), ("lat", "lev")).reshape(N_DEV, 128)
    with jax.named_scope("specx"):
        spec = exchange(spec, "lev")
    tracer_new = inverse(home, table, even, weight)
    spectral_new = place(spec).reshape(SLOTS, 20, 2, 64)
    return jnp.swapaxes(tracer_new, 0, 1), jnp.swapaxes(spectral_new, 1, 2)


def solution(mesh):
    placed = (
        P("lev", "lat", None),
        P(None, "lat", None),
        P(),
        P(),
        P("lat", None, "lev", None),
        P(),
        P(),
        P(),
    )
    return jax.shard_map(
        on_device,
        mesh=mesh,
        in_specs=placed,
        out_specs=(P("lev", "lat", None), P("lat", None, "lev", None)),
        check_vma=False,
    )
```

time: 295 us -> 157 us (0.53); the launches traced: 290 us -> 156 us
  other arithmetic: 84.3 us -> 1.46 us
  Pallas kernels: 0 us -> 54.1 us
  local copies, waits for them, and re-layouts: 58.7 us -> 9.33 us
  waiting for transfers between devices: 57.8 us -> 30.9 us
  matrix products: 26.4 us -> 0 us
  between operations: 15.4 us -> 0.92 us
  blocking collectives: 0 us -> 11.5 us
    mul x10 -> x1, other arithmetic: 66.2 us -> 0.16 us  [by_block(): return jnp.kron(jnp.eye(3, dtype=F32), matrix)]
    pallas_call x0 -> x6, Pallas kernels: none -> 54.1 us  [the longest x1 31 us: send_tables(): pl.pallas_call(send_kernel, out_shape=jax.ShapeDtypeStruct((N_LEV, 2, 20,...]
    all_gather x2 -> x0, waiting for transfers between devices: 29.5 us -> none  [whole_of(): nearer = lax.all_gather(value, axes[-1], axis=dim, tiled=True)]
    dot_general x6 -> x0, matrix products: 26.4 us -> none  [the longest x1 6.75 us: on_device(): jnp.einsum('rpij,rpclj->rpicl', full_table, hemispheres, preferred_elemen...]
    unnamed x102 -> x15, local copies, waits for them, and re-layouts: 22.7 us -> 2.1 us
    slice x24 -> x1, local copies, waits for them, and re-layouts: 18.4 us -> 0.78 us  [on_device(): south = lax.ppermute(rows[:3], 'lat', down)]
    add x4 -> x0, other arithmetic: 14.2 us -> none  [the longest x1 13 us: transport(): summed + (stencil[row_step + 3, col_step + 3] + picked)[None, :, :] * shi...]
    all_to_all x0 -> x1, blocking collectives: none -> 11.5 us  [exchange(): return lax.all_to_all(value, axes, split_axis=0, concat_axis=0, tiled=True)]
  transfers between devices with their start and end apart: 8 -> 5, of which waited for: 4 -> 3; matrix products, arithmetic and copies ran while one was open for 41% -> 6% of each run, Pallas kernels for 0% -> 9%
where the time goes in v1:
time: 157 us; the launch traced here: 156 us
  Pallas kernels  54.1 us (34%)
  starting transfers between devices  47.6 us (30%)
  waiting for transfers between devices  30.9 us (20%)
  blocking collectives  11.5 us (7%)
  local copies, waits for them, and re-layouts  9.33 us (6%)
    all_to_all x3, starting transfers between devices, exchange(): return lax.all_to_all(value, axes, split_axis=0, concat_axis=0, tiled=True)  36.9 us
    pallas_call x1, Pallas kernels, send_tables(): pl.pallas_call(send_kernel, out_shape=jax.ShapeDtypeStruct((N_LEV, 2, 20,...  31 us
    all_to_all x3, waiting for transfers between devices, exchange(): return lax.all_to_all(value, axes, split_axis=0, concat_axis=0, tiled=True)  26 us
    all_to_all x1, blocking collectives, exchange(): return lax.all_to_all(value, axes, split_axis=0, concat_axis=0, tiled=True)  11.5 us
    ppermute x1, starting transfers between devices, on_device(): north = lax.ppermute(rows[ROWS - 3:], 'lat', up)  7.84 us
    pallas_call x1, Pallas kernels, forward(): call(forward_kernel, jax.ShapeDtypeStruct((N_DEV, 128), F32), [SM, VM, VM...  6.45 us
    pallas_call x1, Pallas kernels, tables(): call(tables_kernel, (jax.ShapeDtypeStruct((3, N_DEV, NLON), BF16), jax.Sh...  6.22 us
    ppermute x1, waiting for transfers between devices, on_device(): south = lax.ppermute(rows[:3], 'lat', down)  4.97 us
  transfers between devices with their start and end apart: 5, of which 3 were waited for; matrix products, arithmetic and copies ran while one was open for 6% of the time, Pallas kernels for 9%

profile of v1, /device:TPU:1, one launch (start us, length us, event | category | flops | bytes accessed | tf_op | source)
XLA Modules:
  0.0 155.9 jit_solution(2129898265789290663)
XLA Ops:
  0.6 31.0 %send_tables.1 = bf16[16,2,20,2,320]{4,3,2,1,0:T(2,128)(2,1)} custom-call(bf16[20,20,2,320]{3,2,1,0:T(2,128)(2,1)} %bitcast.32), custom_call_target="tpu_custom_call" | custom-call | flops 1000000 | bytes 2000000 | tf_op jit(solution)/shard_map/tabx/send_tables/pallas_call | solution.py:391
  31.7 0.0 copy-start.6
  31.7 0.0 copy-start.5
  31.7 0.0 copy-start.2
  31.7 10.5 %all-to-all-start.1 = ((bf16[16,2,20,2,320]{4,3,2,1,0:T(2,128)(2,1)}), bf16[16,2,20,2,320]{4,3,2,1,0:T(2,128)(2,1)S(1)}, u32[]{:S(2)}, u32[]{:S(2)}) async-start(bf16[16,2,20,2,320]{4,3,2,1,0:T(2,128)(2,1)} %send_tables.1), calls=%async_computation.1 | async-start | bytes 1966080 | tf_op jit(solution)/shard_map/tabx/all_to_all | solution.py:408
  42.2 0.8 fusion.1
  43.0 2.9 %collective-permute-start.1 = (f32[3,2,1280]{2,1,0:T(2,128)S(1)}, f32[3,2,1280]{2,1,0:T(2,128)S(1)}, u32[]{:S(2)}, u32[]{:S(2)}) collective-permute-start(f32[3,2,1280]{2,1,0:T(2,128)S(1)} %get-tuple-element.12), channel_id=1, source_target_pairs={{16,0},{32,16},{48,32},{64,48},{80,64},{96,80},{112,96},{128,112},... | collective-permute-start | bytes 92168 | tf_op jit(solution)/shard_map/ppermute | solution.py:416
  45.9 7.8 %collective-permute-start = (f32[3,2,1280]{2,1,0:T(2,128)S(1)}, f32[3,2,1280]{2,1,0:T(2,128)S(1)}, u32[]{:S(2)}, u32[]{:S(2)}) collective-permute-start(f32[3,2,1280]{2,1,0:T(2,128)S(1)} %get-tuple-element.13), channel_id=1, source_target_pairs={{0,16},{16,32},{32,48},{48,64},{64,80},{80,96},{96,112},{112,128},... | collective-permute-start | bytes 92168 | tf_op jit(solution)/shard_map/ppermute | solution.py:415
  53.7 0.7 convert_element_type.16
  54.4 0.6 reshape.62.assign_ref
  55.0 6.2 %tables.1 = (bf16[3,512,1280]{2,1,0:T(8,128)(2,1)}, f32[512,128]{1,0:T(8,128)}, f32[512,128]{1,0:T(8,128)}) custom-call(f32[1,640]{1,0:T(1,128)} %reshape.62.assign_ref), custom_call_target="tpu_custom_call" | custom-call | flops 10000000 | bytes 1000000 | tf_op jit(solution)/shard_map/tables/pallas_call | solution.py:120
  61.2 5.0 %collective-permute-done.1.south_ref = f32[3,2,1280]{2,1,0:T(2,128)S(1)} collective-permute-done((f32[3,2,1280]{2,1,0:T(2,128)S(1)}, f32[3,2,1280]{2,1,0:T(2,128)S(1)}, u32[]{:S(2)}, u32[]{:S(2)}) %collective-permute-start.1) | collective-permute-done | bytes 30752 | tf_op jit(solution)/shard_map/ppermute | solution.py:416
  66.2 0.0 copy-start.3
  66.2 0.0 collective-permute-done.north_ref
  66.2 0.0 copy-start.4
  66.2 0.6 copy-done.3
  66.8 0.0 copy-done.4
  66.8 6.4 %forward.1 = f32[512,128]{1,0:T(8,128)} custom-call(f32[7,7]{1,0:T(8,128)} %stencil_ref.1, f32[20,2,1280]{2,1,0:T(2,128)} %bitcast.35, f32[3,2,1280]{2,1,0:T(2,128)} %copy-done.4, f32[3,2,1280]{2,1,0:T(2,128)} %copy-done.3, s32[20,2,1280]{2,1,0:T(2,128)} %bitcast.38, bf16[3,512,1280]{2,1,0:T(8,128)(2,1)} %get-tuple-element.7.t_any, ...), custom_call_target="tpu_custom_call" | custom-call | flops 1000000000 | bytes 1000000 | tf_op jit(solution)/shard_map/forward/pallas_call | solution.py:211
  73.2 0.0 all-to-all-done.1
  73.3 15.8 %all-to-all-start = ((f32[512,1,128]{2,1,0:T(1,128)}), f32[512,1,128]{2,1,0:T(1,128)S(1)}, u32[]{:S(2)}, u32[]{:S(2)}) async-start(f32[512,1,128]{2,1,0:T(1,128)} %bitcast.30), calls=%async_computation | async-start | bytes 524288 | tf_op jit(solution)/shard_map/fwdx/all_to_all | solution.py:408
  89.0 0.8 dynamic_slice.3
  89.8 0.0 copy-done.6
  89.8 0.7 copy.32.damping_ref
  90.5 0.0 copy-done.5
  90.5 0.1 copy.27
  90.6 0.1 copy.29
  90.6 0.0 copy-done.2
  90.7 0.2 broadcast_multiply_fusion
  90.8 0.7 mul.77.vecp_ref
  91.6 0.8 mul.73.vec_ref
  92.3 0.7 mul.70.inv_ref
  93.1 0.6 pad_add_fusion.info_ref
  93.7 1.0 copy.26
  94.7 1.1 copy.31.table_ref
  95.8 10.5 %all-to-all-done = f32[512,1,128]{2,1,0:T(1,128)S(1)} async-done(((f32[512,1,128]{2,1,0:T(1,128)}), f32[512,1,128]{2,1,0:T(1,128)S(1)}, u32[]{:S(2)}, u32[]{:S(2)}) %all-to-all-start) | async-done | bytes 262176 | tf_op jit(solution)/shard_map/fwdx/all_to_all | solution.py:408
  106.2 0.0 copy-start.1
  106.2 0.7 copy-done.1
  106.9 4.6 %spectral.1 = (f32[512,128]{1,0:T(8,128)}, bf16[16,40,96]{2,1,0:T(8,128)(2,1)}) custom-call(s32[4]{0:T(128)} %pad_add_fusion.info_ref, f32[512,128]{1,0:T(8,128)} %bitcast.36, bf16[2,640,320]{2,1,0:T(8,128)(2,1)} %copy.31.table_ref, f32[32,1]{1,0:T(8,128)} %copy.32.damping_ref, f32[96,96]{1,0:T(8,128)} %mul.70.inv_ref, f32[96,96]{1,0:T(8,128)} %mul.73.vec_ref, ...), custom_call_target="tpu_custom_call" | custom-call | flops 1000000000 | bytes 1000000 | tf_op jit(solution)/shard_map/spectral/pallas_call | solution.py:305
  111.6 11.5 %all_to_all.20.spec_ref = bf16[16,40,96]{2,1,0:T(8,128)(2,1)} all-to-all(bf16[16,40,96]{2,1,0:T(8,128)(2,1)} %get-tuple-element.11), channel_id=1, replica_groups=mesh['lat'=32,'lev'=16] {'lev'}, dimensions={0} | all-to-all | bytes 245760 | tf_op jit(solution)/shard_map/specx/all_to_all | solution.py:408
  123.1 10.7 %all-to-all-start.2 = ((f32[512,1,128]{2,1,0:T(1,128)}), f32[512,1,128]{2,1,0:T(1,128)S(1)}, u32[]{:S(2)}, u32[]{:S(2)}) async-start(f32[512,1,128]{2,1,0:T(1,128)} %bitcast.37), calls=%async_computation.2 | async-start | bytes 524288 | tf_op jit(solution)/shard_map/bwdx/all_to_all | solution.py:408
  133.7 2.0 %place.1 = f32[20,40,64]{2,1,0:T(8,128)} custom-call(bf16[16,40,96]{2,1,0:T(8,128)(2,1)} %all_to_all.20.spec_ref), custom_call_target="tpu_custom_call" | custom-call | flops 1000000 | bytes 1000000 | tf_op jit(solution)/shard_map/place/pallas_call | solution.py:366
  135.7 15.5 %all-to-all-done.2 = f32[512,1,128]{2,1,0:T(1,128)S(1)} async-done(((f32[512,1,128]{2,1,0:T(1,128)}), f32[512,1,128]{2,1,0:T(1,128)S(1)}, u32[]{:S(2)}, u32[]{:S(2)}) %all-to-all-start.2) | async-done | bytes 262176 | tf_op jit(solution)/shard_map/bwdx/all_to_all | solution.py:408
  151.2 0.0 copy-start
  151.2 0.7 copy-done
  151.9 3.8 %inverse.1 = f32[20,2,1280]{2,1,0:T(2,128)} custom-call(f32[512,128]{1,0:T(8,128)} %bitcast.31, bf16[3,512,1280]{2,1,0:T(8,128)(2,1)} %get-tuple-element.7.t_any, f32[512,128]{1,0:T(8,128)} %get-tuple-element.8.even_ref, f32[512,128]{1,0:T(8,128)} %get-tuple-element.10.weight_ref), custom_call_target="tpu_custom_call" | custom-call | flops 100000000 | bytes 1000000 | tf_op jit(solution)/shard_map/inverse/pallas_call | solution.py:342
  (3 shorter events, 0.0 us)
Async XLA Ops:
  31.7 58.1 %copy-start.6 = (f32[32]{0:T(128)S(1)}, f32[32]{0:T(128)}, u32[]{:S(2)}) copy-start(f32[32]{0:T(128)} %param.13) | copy-start | bytes 388
  31.7 58.8 %copy-start.5 = (f32[32,32]{1,0:T(8,128)S(1)}, f32[32,32]{1,0:T(8,128)}, u32[]{:S(2)}) copy-start(f32[32,32]{1,0:T(8,128)} %param.15) | copy-start | bytes 12292
  31.7 58.9 %copy-start.2 = (f32[32,32]{1,0:T(8,128)S(1)}, f32[32,32]{1,0:T(8,128)}, u32[]{:S(2)}) copy-start(f32[32,32]{1,0:T(8,128)} %param.14) | copy-start | bytes 12292
  31.7 41.5 %all-to-all-start.1 = ((bf16[16,2,20,2,320]{4,3,2,1,0:T(2,128)(2,1)}), bf16[16,2,20,2,320]{4,3,2,1,0:T(2,128)(2,1)S(1)}, u32[]{:S(2)}, u32[]{:S(2)}) async-start(bf16[16,2,20,2,320]{4,3,2,1,0:T(2,128)(2,1)} %send_tables.1), calls=%async_computation.1 | async-start | bytes 1966080 | tf_op jit(solution)/shard_map/tabx/all_to_all | solution.py:408
  43.0 23.2 %collective-permute-start.1 = (f32[3,2,1280]{2,1,0:T(2,128)S(1)}, f32[3,2,1280]{2,1,0:T(2,128)S(1)}, u32[]{:S(2)}, u32[]{:S(2)}) collective-permute-start(f32[3,2,1280]{2,1,0:T(2,128)S(1)} %get-tuple-element.12), channel_id=1, source_target_pairs={{16,0},{32,16},{48,32},{64,48},{80,64},{96,80},{112,96},{128,112},... | collective-permute-start | bytes 92168 | tf_op jit(solution)/shard_map/ppermute | solution.py:416
  45.9 20.3 %collective-permute-start = (f32[3,2,1280]{2,1,0:T(2,128)S(1)}, f32[3,2,1280]{2,1,0:T(2,128)S(1)}, u32[]{:S(2)}, u32[]{:S(2)}) collective-permute-start(f32[3,2,1280]{2,1,0:T(2,128)S(1)} %get-tuple-element.13), channel_id=1, source_target_pairs={{0,16},{16,32},{32,48},{48,64},{64,80},{80,96},{96,112},{112,128},... | collective-permute-start | bytes 92168 | tf_op jit(solution)/shard_map/ppermute | solution.py:415
  66.2 0.6 copy-start.3
  66.2 0.6 copy-start.4
  73.3 33.0 %all-to-all-start = ((f32[512,1,128]{2,1,0:T(1,128)}), f32[512,1,128]{2,1,0:T(1,128)S(1)}, u32[]{:S(2)}, u32[]{:S(2)}) async-start(f32[512,1,128]{2,1,0:T(1,128)} %bitcast.30), calls=%async_computation | async-start | bytes 524288 | tf_op jit(solution)/shard_map/fwdx/all_to_all | solution.py:408
  106.2 0.7 copy-start.1
  123.1 28.1 %all-to-all-start.2 = ((f32[512,1,128]{2,1,0:T(1,128)}), f32[512,1,128]{2,1,0:T(1,128)S(1)}, u32[]{:S(2)}, u32[]{:S(2)}) async-start(f32[512,1,128]{2,1,0:T(1,128)} %bitcast.37), calls=%async_computation.2 | async-start | bytes 524288 | tf_op jit(solution)/shard_map/bwdx/all_to_all | solution.py:408
  151.2 0.7 copy-start

commit v2 on v1

--- a/solution.py
+++ b/solution.py
@@ -27,8 +27,12 @@
 HIGH = lax.Precision.HIGHEST
 
 
-def first_rc(b):
-    return (5 * b) >> 1
+def own_slot(b):
+    return 5 * (b >> 2) + (b & 3)
+
+
+def shared_slot(b):
+    return 5 * (b >> 2) + 4
 
 
 def call(kernel, out_shape, in_specs, scratch, name, flops=10**7):
@@ -82,34 +86,38 @@
     def step(i, carry):
         r0 = pl.multiple_of(i * CHUNK, CHUNK)
         d = r0 + lax.broadcasted_iota(jnp.int32, (CHUNK, 1), 0)
-        rc0 = ((d & 15) * 5) >> 1
-        evens, weights, waves = [], [], []
-        for j in range(3):
-            slot = (d >> 4) * SLOTS + ((rc0 + j) >> 1)
-            waves.append(jnp.sum(jnp.where(slots == slot, assign, 0.0), axis=1, keepdims=True))
-            evens.append(jnp.where(waves[j] == 2.0 * jnp.floor(waves[j] * 0.5), 1.0, 0.0))
-            weights.append(jnp.where(waves[j] == 0.0, 1.0, 2.0))
-        packed = jnp.where(lane == 0, waves[0], jnp.where(lane == 1, waves[1], waves[2]))
-        turn_c, turn_s = cos_sin(wrapped(packed * 128.0))
-        for j in range(3):
-            quarter = jnp.where(((rc0 + j) & 1) == 1, 320.0, 0.0)
-            c, s = cos_sin(wrapped(waves[j] * lane_f + quarter))
+        lev = d & 15
+        waves, evens, weights = [], [], []
+        for slot in (own_slot(lev), shared_slot(lev)):
+            wave = jnp.sum(jnp.where(slots == (d >> 4) * SLOTS + slot, assign, 0.0), axis=1, keepdims=True)
+            waves.append(wave)
+            evens.append(jnp.where(wave == 2.0 * jnp.floor(wave * 0.5), 1.0, 0.0))
+            weights.append(jnp.where(wave == 0.0, 1.0, 2.0))
+        turn_c, turn_s = cos_sin(wrapped(jnp.where(lane == 0, waves[0], waves[1]) * 128.0))
+
+        def put(j, block, value):
+            high = value.astype(BF16)
+            t_ref[j, pl.ds(r0, CHUNK), 128 * block : 128 * block + 128] = high
+            low = (value - high.astype(F32)).astype(BF16)
+            t_ref[j, pl.ds(r0, CHUNK), HALF_LON + 128 * block : HALF_LON + 128 * block + 128] = low
+
+        for u in range(2):
+            start = wrapped(waves[u] * lane_f + (jnp.where((lev & 2) == 2, 320.0, 0.0) if u else 0.0))
+            c, s = cos_sin(start)
             c = c * (1.0 / math.sqrt(NLON))
             s = s * (1.0 / math.sqrt(NLON))
-            cd, sd = turn_c[:, j : j + 1], turn_s[:, j : j + 1]
+            cd, sd = turn_c[:, u : u + 1], turn_s[:, u : u + 1]
             for block in range(5):
-                high = c.astype(BF16)
-                t_ref[j, pl.ds(r0, CHUNK), 128 * block : 128 * block + 128] = high
-                t_ref[
-                    j, pl.ds(r0, CHUNK), HALF_LON + 128 * block : HALF_LON + 128 * block + 128
-                ] = (c - high.astype(F32)).astype(BF16)
+                put(2 * u, block, c)
+                if u == 0:
+                    put(1, block, -s)
                 if block < 4:
                     c, s = c * cd - s * sd, s * cd + c * sd
         even_ref[pl.ds(r0, CHUNK), :] = jnp.where(
-            lane < MSG, evens[0], jnp.where(lane < 2 * MSG, evens[1], evens[2])
+            lane < 2 * MSG, evens[0], evens[1]
         )
         weight_ref[pl.ds(r0, CHUNK), :] = jnp.where(
-            lane < MSG, weights[0], jnp.where(lane < 2 * MSG, weights[1], weights[2])
+            lane < 2 * MSG, weights[0], weights[1]
         )
         return carry
 
@@ -239,7 +247,22 @@
 
 
 def spectral_kernel(
-    info_ref, msg_ref, table_ref, damping_ref, inv_ref, vec_ref, vecp_ref, out_ref, spec_ref, nbuf, sbuf, flip, zn, zs, sall
+    info_ref,
+    msg_ref,
+    own_ref,
+    shared_ref,
+    damping_ref,
+    inv_ref,
+    vec_ref,
+    vecp_ref,
+    out_ref,
+    spec_ref,
+    nbuf,
+    sbuf,
+    flip,
+    zn,
+    zs,
+    solved,
 ):
     mirror = mirror_matrix()
     half = N_DEV // 2
@@ -252,42 +275,58 @@
                 lane = MSG * j + ROWS * k
                 nbuf[j, 16 * k : 16 * k + 16, ROWS * a : ROWS * a + ROWS] = top[:, lane : lane + ROWS]
                 sbuf[j, 16 * k : 16 * k + 16, ROWS * a : ROWS * a + ROWS] = low[:, lane : lane + ROWS]
-    parity = info_ref[2]
-    lev_odd = info_ref[3]
+    damp = damping_ref[...]
+
+    def exact(left, right):
+        return lax.dot_general(left, right, NN, precision=HIGH, preferred_element_type=F32)
+
+    def solve(units, matrix, degree, odd):
+        count = len(units)
+        hemi = jnp.concatenate(
+            [part for j in units for part in (nbuf[j] + sbuf[j], nbuf[j] - sbuf[j])], axis=0
+        ).astype(BF16)
+        prod = lax.dot_general(hemi, matrix, NT, preferred_element_type=F32)
+        keep = degree <= M - 1
+        forcing = jnp.concatenate(
+            [
+                jnp.where(keep, jnp.where(odd, prod[64 * u + 32 : 64 * u + 64], prod[64 * u : 64 * u + 32]), 0.0)
+                for u in range(count)
+            ],
+            axis=0,
+        )
+        size = 32 * count
+        n = degree.astype(F32)
+        denominator = 1.0 + (n * (n + 1.0) / float(M * M)) * damp
+        modal = exact(inv_ref[:size, :size], forcing)
+        modal = jnp.concatenate([modal[32 * u : 32 * u + 32] / denominator for u in range(count)], axis=0)
+        packed = exact(vecp_ref[:size, :size], modal)
+        left = jnp.concatenate(
+            [
+                part
+                for u in range(count)
+                for part in (
+                    packed[32 * u : 32 * u + 32],
+                    jnp.where(odd, -packed[32 * u : 32 * u + 32], packed[32 * u : 32 * u + 32]),
+                )
+            ],
+            axis=0,
+        ).astype(BF16)
+        back = lax.dot_general(left, matrix, NN, preferred_element_type=F32)
+        for u, j in enumerate(units):
+            zn[j] = back[64 * u : 64 * u + 32]
+            zs[j] = back[64 * u + 32 : 64 * u + 64]
+        return exact(vec_ref[:size, :size], modal).T
+
     lane = lax.broadcasted_iota(jnp.int32, (32, QP), 1)
-    odd = lane & 1
-    damp = damping_ref[...]
-    matrix = [table_ref[0], table_ref[parity], table_ref[1]]
-    degree = [
-        lane + (info_ref[0] if j == 0 else (info_ref[1] if j == 2 else jnp.where(parity == 1, info_ref[1], info_ref[0])))
-        for j in range(3)
-    ]
-    for j in range(3):
-        north, south = nbuf[j], sbuf[j]
-        hemi = jnp.concatenate([north + south, north - south], axis=0).astype(BF16)
-        prod = lax.dot_general(hemi, matrix[j], NT, preferred_element_type=F32)
-        keep = degree[j] <= M - 1
-        if j == 0:
-            keep = jnp.logical_and(keep, odd >= lev_odd)
-        if j == 2:
-            keep = jnp.logical_and(keep, odd <= lev_odd)
-        sall[32 * j : 32 * j + 32, :] = jnp.where(keep, jnp.where(odd == 1, prod[32:], prod[:32]), 0.0)
-    modal = lax.dot_general(inv_ref[...], sall[...], NN, precision=HIGH, preferred_element_type=F32)
-    for j in range(3):
-        n = degree[j].astype(F32)
-        growth = n * (n + 1.0) / float(M * M)
-        sall[32 * j : 32 * j + 32, :] = modal[32 * j : 32 * j + 32, :] / (1.0 + growth * damp)
-    modal = sall[...]
-    solved = lax.dot_general(vec_ref[...], modal, NN, precision=HIGH, preferred_element_type=F32).T
+    whole = solve((0, 1), own_ref[...], lane + info_ref[0], (lane & 1) == 1)
+    lane = lax.broadcasted_iota(jnp.int32, (32, QP // 2), 1)
+    block = jnp.floor((lane.astype(F32) + 0.5) * (1.0 / 20.0)).astype(jnp.int32)
+    part = solve((2,), shared_ref[...], lane + 20 * block + 20 * info_ref[2] + info_ref[1], (lane & 1) == 1)
+    solved[...] = jnp.zeros((N_LEV, QB, 96), F32)
     for b in range(N_LEV):
-        spec_ref[b] = solved[QB * b : QB * b + QB].astype(BF16)
-    sall[...] = lax.dot_general(vecp_ref[...], modal, NN, precision=HIGH, preferred_element_type=F32)
-    for j in range(3):
-        mine = sall[32 * j : 32 * j + 32, :]
-        left = jnp.concatenate([mine, jnp.where(odd == 1, -mine, mine)], axis=0).astype(BF16)
-        both = lax.dot_general(left, matrix[j], NN, preferred_element_type=F32)
-        zn[j] = both[:32]
-        zs[j] = both[32:]
+        solved[b, :, 0:64] = whole[QB * b : QB * b + QB]
+        solved[b, 0:20, 64:96] = part[20 * b : 20 * b + 20]
+    spec_ref[...] = solved[...].astype(BF16)
     out_ref[...] = jnp.zeros((N_DEV, 128), F32)
     flip[...] = jnp.zeros((half, 128), F32)
     for a in range(N_LAT // 2):
@@ -301,22 +340,22 @@
     out_ref[half:, :] = lax.dot_general(flip[...], mirror, NN, precision=HIGH, preferred_element_type=F32)
 
 
-def spectral(info, msgs, table, damping, inv, vec, vecp):
+def spectral(info, msgs, own, shared, damping, inv, vec, vecp):
     return call(
         spectral_kernel,
         (jax.ShapeDtypeStruct((N_DEV, 128), F32), jax.ShapeDtypeStruct((N_LEV, QB, 96), BF16)),
-        [SM, VM, VM, VM, VM, VM, VM],
+        [SM, VM, VM, VM, VM, VM, VM, VM],
         [
             pltpu.VMEM((3, 32, HL), F32),
             pltpu.VMEM((3, 32, HL), F32),
             pltpu.VMEM((N_DEV // 2, 128), F32),
             pltpu.VMEM((3, 32, HL), F32),
             pltpu.VMEM((3, 32, HL), F32),
-            pltpu.VMEM((96, QP), F32),
+            pltpu.VMEM((N_LEV, QB, 96), F32),
         ],
         "spectral",
         10**9,
-    )(info, msgs, table, damping, inv, vec, vecp)
+    )(info, msgs, own, shared, damping, inv, vec, vecp)
 
 
 def inverse_kernel(msg_ref, t_any, even_ref, weight_ref, out_ref, t_ref, t_sem):
@@ -350,16 +389,10 @@
 
 
 def place_kernel(spec_ref, out_ref):
-    for slot in range(SLOTS):
-        for c in range(2):
-            w, o = divmod(2 * slot + c, 5)
-            parts = []
-            if o <= 2:
-                parts.append((2 * w, o))
-            if o >= 2:
-                parts.append((2 * w + 1, o - 2))
-            value = sum(spec_ref[b, :, 32 * j : 32 * j + 32].astype(F32) for b, j in parts)
-            out_ref[slot, :, 32 * c : 32 * c + 32] = value
+    for b in range(N_LEV):
+        c, half = (b & 3) >> 1, b & 1
+        out_ref[own_slot(b)] = spec_ref[b, :, 0:64].astype(F32)
+        out_ref[shared_slot(b), 20 * half : 20 * half + 20, 32 * c : 32 * c + 32] = spec_ref[b, 0:20, 64:96].astype(F32)
 
 
 def place(spec):
@@ -367,7 +400,7 @@
 
 
 def by_block(matrix):
-    return jnp.kron(jnp.eye(3, dtype=F32), matrix)
+    return jnp.kron(jnp.eye(2, dtype=F32), matrix)
 
 
 def level_order(value, axis):
@@ -379,8 +412,9 @@
 def send_kernel(table_ref, out_ref, sems):
     copies = []
     for b in range(N_LEV):
-        first = first_rc(b) >> 1
-        copies.append(pltpu.make_async_copy(table_ref.at[pl.ds(first, 2)], out_ref.at[b], sems.at[b]))
+        copies.append(pltpu.make_async_copy(table_ref.at[own_slot(b)], out_ref.at[b, pl.ds(0, 20)], sems.at[2 * b]))
+        half = table_ref.at[shared_slot(b), pl.ds(10 * (b & 1), 10)]
+        copies.append(pltpu.make_async_copy(half, out_ref.at[b, pl.ds(20, 10)], sems.at[2 * b + 1]))
     for copy in copies:
         copy.start()
     for copy in copies:
@@ -390,10 +424,10 @@
 def send_tables(legendre):
     return pl.pallas_call(
         send_kernel,
-        out_shape=jax.ShapeDtypeStruct((N_LEV, 2, 20, 2, HL), BF16),
-        in_specs=[ANY],
+        out_shape=jax.ShapeDtypeStruct((N_LEV, 30, 2, HL), BF16),
+        in_specs=[VM],
         out_specs=ANY,
-        scratch_shapes=[pltpu.SemaphoreType.DMA((N_LEV,))],
+        scratch_shapes=[pltpu.SemaphoreType.DMA((2 * N_LEV,))],
         name="send_tables",
         interpret=INTERPRET,
         cost_estimate=pl.CostEstimate(flops=10**6, bytes_accessed=2 * 10**6, transcendentals=0),
@@ -401,7 +435,7 @@
 
 
 def received_tables(got):
-    return jnp.swapaxes(got, 0, 1).reshape(2, QP, HL)
+    return got[:, :20].reshape(QP, HL), got[:, 20:].reshape(QP // 2, HL)
 
 
 def exchange(value, axes):
@@ -417,18 +451,18 @@
     table, even, weight = tables(assign)
     with jax.named_scope("tabx"):
         matrices = exchange(send_tables(legendre), "lev")
-    matrices = received_tables(matrices)
+    own, shared = received_tables(matrices)
     msgs = forward(stencil, rows, north, south, jnp.swapaxes(offsets, 0, 1), table, even)
     with jax.named_scope("fwdx"):
         got = exchange(msgs.reshape(N_DEV, 1, 128), ("lat", "lev")).reshape(N_DEV, 128)
     lev = lax.axis_index("lev")
-    rc0 = (5 * lev) >> 1
-    waves = lax.dynamic_slice_in_dim(assign, lax.axis_index("lat") * SLOTS + (rc0 >> 1), 2)
-    info = jnp.concatenate([waves, jnp.stack([rc0 & 1, lev & 1])]).astype(jnp.int32)
+    mine = lax.dynamic_slice_in_dim(assign, lax.axis_index("lat") * SLOTS, SLOTS)
+    info = jnp.stack([mine[own_slot(lev)], mine[shared_slot(lev)], lev & 1]).astype(jnp.int32)
     back, spec = spectral(
         info,
         got,
-        matrices,
+        own,
+        shared,
         damping.reshape(32, 1),
         by_block(level_order(vert_inv, 1)),
         by_block(vert_vecs),

time: 157 us -> 127 us (0.81)
  Pallas kernels: 54.1 us -> 24.9 us
  waiting for transfers between devices: 30.9 us -> 24.9 us
  starting transfers between devices: 47.6 us -> 50.6 us
    pallas_call x1, Pallas kernels: 31 us -> 2.24 us  [send_tables(): pl.pallas_call(send_kernel, out_shape=jax.ShapeDtypeStruct((N_LEV, 30, 2,...]
    ppermute x1, waiting for transfers between devices: 4.97 us -> 1.32 us  [on_device(): south = lax.ppermute(rows[:3], 'lat', down)]
    all_to_all x3, starting transfers between devices: 36.9 us -> 39.9 us  [exchange(): return lax.all_to_all(value, axes, split_axis=0, concat_axis=0, tiled=True)]
    all_to_all x3, waiting for transfers between devices: 26 us -> 23.6 us  [exchange(): return lax.all_to_all(value, axes, split_axis=0, concat_axis=0, tiled=True)]
    another operation x0 -> x1, other arithmetic: none -> 1.96 us  [on_device(): jnp.stack([mine[own_slot(lev)], mine[shared_slot(lev)], lev & 1])]
  transfers between devices with their start and end apart: 5 -> 5, of which waited for: 3 -> 3; matrix products, arithmetic and copies ran while one was open for 6% -> 9% of each run, Pallas kernels for 9% -> 11%
where the time goes in v2:
time: 127 us; the launch traced here: 126 us
  starting transfers between devices  50.6 us (40%)
  Pallas kernels  24.9 us (20%)
  waiting for transfers between devices  24.9 us (20%)
  blocking collectives  11.5 us (9%)
  local copies, waits for them, and re-layouts  10.4 us (8%)
  other arithmetic  2.78 us (2%)
    all_to_all x3, starting transfers between devices, exchange(): return lax.all_to_all(value, axes, split_axis=0, concat_axis=0, tiled=True)  39.9 us
    all_to_all x3, waiting for transfers between devices, exchange(): return lax.all_to_all(value, axes, split_axis=0, concat_axis=0, tiled=True)  23.6 us
    all_to_all x1, blocking collectives, exchange(): return lax.all_to_all(value, axes, split_axis=0, concat_axis=0, tiled=True)  11.5 us
    ppermute x1, starting transfers between devices, on_device(): north = lax.ppermute(rows[ROWS - 3:], 'lat', up)  7.84 us
    pallas_call x1, Pallas kernels, forward(): call(forward_kernel, jax.ShapeDtypeStruct((N_DEV, 128), F32), [SM, VM, VM...  6.44 us
    pallas_call x1, Pallas kernels, tables(): call(tables_kernel, (jax.ShapeDtypeStruct((3, N_DEV, NLON), BF16), jax.Sh...  5.87 us
    pallas_call x1, Pallas kernels, spectral(): call(spectral_kernel, (jax.ShapeDtypeStruct((N_DEV, 128), F32), jax.Shape...  4.74 us
    pallas_call x1, Pallas kernels, inverse(): call(inverse_kernel, jax.ShapeDtypeStruct((ROWS, LV, NLON), F32), [VM, AN...  3.85 us
  transfers between devices with their start and end apart: 5, of which 3 were waited for; matrix products, arithmetic and copies ran while one was open for 9% of the time, Pallas kernels for 11%

profile of v2, /device:TPU:1, one launch (start us, length us, event | category | flops | bytes accessed | tf_op | source)
XLA Modules:
  0.0 126.0 jit_solution(16976408106239763365)
XLA Ops:
  0.6 0.0 copy-start.6
  0.6 2.2 %send_tables.1 = bf16[16,30,2,320]{3,2,1,0:T(2,128)(2,1)} custom-call(bf16[20,20,2,320]{3,2,1,0:T(2,128)(2,1)} %bitcast.27), custom_call_target="tpu_custom_call" | custom-call | flops 1000000 | bytes 2000000 | tf_op jit(solution)/shard_map/tabx/send_tables/pallas_call | solution.py:425
  2.9 0.0 copy-start.5
  2.9 0.0 copy-start.2
  2.9 10.4 %all-to-all-start.1 = ((bf16[16,30,2,320]{3,2,1,0:T(2,128)(2,1)}), bf16[16,30,2,320]{3,2,1,0:T(2,128)(2,1)S(1)}, u32[]{:S(2)}, u32[]{:S(2)}) async-start(bf16[16,30,2,320]{3,2,1,0:T(2,128)(2,1)} %send_tables.1), calls=%async_computation.1 | async-start | bytes 1474560 | tf_op jit(solution)/shard_map/tabx/all_to_all | solution.py:442
  13.3 0.8 fusion
  14.1 2.9 %collective-permute-start.1 = (f32[3,2,1280]{2,1,0:T(2,128)S(1)}, f32[3,2,1280]{2,1,0:T(2,128)S(1)}, u32[]{:S(2)}, u32[]{:S(2)}) collective-permute-start(f32[3,2,1280]{2,1,0:T(2,128)S(1)} %get-tuple-element.12), channel_id=1, source_target_pairs={{16,0},{32,16},{48,32},{64,48},{80,64},{96,80},{112,96},{128,112},... | collective-permute-start | bytes 92168 | tf_op jit(solution)/shard_map/ppermute | solution.py:450
  16.9 7.8 %collective-permute-start = (f32[3,2,1280]{2,1,0:T(2,128)S(1)}, f32[3,2,1280]{2,1,0:T(2,128)S(1)}, u32[]{:S(2)}, u32[]{:S(2)}) collective-permute-start(f32[3,2,1280]{2,1,0:T(2,128)S(1)} %get-tuple-element.13), channel_id=1, source_target_pairs={{0,16},{16,32},{32,48},{48,64},{64,80},{80,96},{96,112},{112,128},... | collective-permute-start | bytes 92168 | tf_op jit(solution)/shard_map/ppermute | solution.py:449
  24.8 0.7 convert_element_type.16
  25.5 0.6 reshape.65.assign_ref
  26.1 5.9 %tables.1 = (bf16[3,512,1280]{2,1,0:T(8,128)(2,1)}, f32[512,128]{1,0:T(8,128)}, f32[512,128]{1,0:T(8,128)}) custom-call(f32[1,640]{1,0:T(1,128)} %reshape.65.assign_ref), custom_call_target="tpu_custom_call" | custom-call | flops 10000000 | bytes 1000000 | tf_op jit(solution)/shard_map/tables/pallas_call | solution.py:128
  31.9 1.3 %collective-permute-done.1.south_ref = f32[3,2,1280]{2,1,0:T(2,128)S(1)} collective-permute-done((f32[3,2,1280]{2,1,0:T(2,128)S(1)}, f32[3,2,1280]{2,1,0:T(2,128)S(1)}, u32[]{:S(2)}, u32[]{:S(2)}) %collective-permute-start.1) | collective-permute-done | bytes 30752 | tf_op jit(solution)/shard_map/ppermute | solution.py:450
  33.2 0.0 copy-start.3
  33.2 0.0 collective-permute-done.north_ref
  33.2 0.0 copy-start.4
  33.2 0.6 copy-done.3
  33.9 0.0 copy-done.4
  33.9 6.4 %forward.1 = f32[512,128]{1,0:T(8,128)} custom-call(f32[7,7]{1,0:T(8,128)} %stencil_ref.1, f32[20,2,1280]{2,1,0:T(2,128)} %bitcast.30, f32[3,2,1280]{2,1,0:T(2,128)} %copy-done.4, f32[3,2,1280]{2,1,0:T(2,128)} %copy-done.3, s32[20,2,1280]{2,1,0:T(2,128)} %bitcast.33, bf16[3,512,1280]{2,1,0:T(8,128)(2,1)} %get-tuple-element.7.t_any, ...), custom_call_target="tpu_custom_call" | custom-call | flops 1000000000 | bytes 1000000 | tf_op jit(solution)/shard_map/forward/pallas_call | solution.py:219
  40.3 0.0 all-to-all-done.1
  40.3 16.5 %all-to-all-start = ((f32[512,1,128]{2,1,0:T(1,128)}), f32[512,1,128]{2,1,0:T(1,128)S(1)}, u32[]{:S(2)}, u32[]{:S(2)}) async-start(f32[512,1,128]{2,1,0:T(1,128)} %bitcast.25), calls=%async_computation | async-start | bytes 524288 | tf_op jit(solution)/shard_map/fwdx/all_to_all | solution.py:442
  56.9 0.0 copy-done.6
  56.9 0.7 copy.25.damping_ref
  57.6 0.0 copy-done.5
  57.6 0.1 copy.21
  57.7 0.1 copy.23
  57.7 0.0 copy-done.2
  57.8 0.1 broadcast_multiply_fusion
  57.9 0.7 mul.82.vecp_ref
  58.6 0.7 mul.78.vec_ref
  59.3 0.7 mul.75.inv_ref
  60.0 1.4 %fusion.1 = (s32[1]{0:T(128)}, s32[1]{0:T(128)}) fusion(s32[640]{0:T(1024)} %param.11, s32[]{:T(128)S(6)} %dynamic_slice.11, s32[]{:T(128)S(6)} %dynamic_slice.13), kind=kLoop, calls=%fused_computation.6 | loop fusion | bytes 24 | tf_op jit(solution)/shard_map/dynamic_slice | solution.py:460
  61.4 2.0 %pad_add_fusion.info_ref = s32[3]{0:T(128)} fusion(s32[1]{0:T(128)} %bitcast, s32[1]{0:T(128)} %get-tuple-element.15, s32[1]{0:T(128)} %get-tuple-element.14), kind=kLoop, calls=%fused_computation.4 | loop fusion | flops 6 | bytes 24 | tf_op jit(solution)/shard_map/stack | solution.py:460
  63.4 0.3 slice.18
  63.7 1.2 reshape.68.own_ref
  64.9 0.2 slice.19
  65.1 0.9 reshape.69.shared_ref
  66.0 8.1 %all-to-all-done = f32[512,1,128]{2,1,0:T(1,128)S(1)} async-done(((f32[512,1,128]{2,1,0:T(1,128)}), f32[512,1,128]{2,1,0:T(1,128)S(1)}, u32[]{:S(2)}, u32[]{:S(2)}) %all-to-all-start) | async-done | bytes 262176 | tf_op jit(solution)/shard_map/fwdx/all_to_all | solution.py:442
  74.1 0.0 copy-start.1
  74.1 0.7 copy-done.1
  74.8 4.7 %spectral.1 = (f32[512,128]{1,0:T(8,128)}, bf16[16,40,96]{2,1,0:T(8,128)(2,1)}) custom-call(s32[3]{0:T(128)} %pad_add_fusion.info_ref, f32[512,128]{1,0:T(8,128)} %bitcast.31, bf16[640,320]{1,0:T(8,128)(2,1)} %reshape.68.own_ref, bf16[320,320]{1,0:T(8,128)(2,1)} %reshape.69.shared_ref, f32[32,1]{1,0:T(8,128)} %copy.25.damping_ref, f32[64,64]{1,0:T(8,128)} %mul.75.inv_ref, ...), custom_call_target="tpu_custom_call" | custom-call | flops 1000000000 | bytes 1000000 | tf_op jit(solution)/shard_map/spectral/pallas_call | solution.py:344
  79.5 11.5 %all_to_all.20.spec_ref = bf16[16,40,96]{2,1,0:T(8,128)(2,1)} all-to-all(bf16[16,40,96]{2,1,0:T(8,128)(2,1)} %get-tuple-element.11), channel_id=1, replica_groups=mesh['lat'=32,'lev'=16] {'lev'}, dimensions={0} | all-to-all | bytes 245760 | tf_op jit(solution)/shard_map/specx/all_to_all | solution.py:442
  91.0 13.0 %all-to-all-start.2 = ((f32[512,1,128]{2,1,0:T(1,128)}), f32[512,1,128]{2,1,0:T(1,128)S(1)}, u32[]{:S(2)}, u32[]{:S(2)}) async-start(f32[512,1,128]{2,1,0:T(1,128)} %bitcast.32), calls=%async_computation.2 | async-start | bytes 524288 | tf_op jit(solution)/shard_map/bwdx/all_to_all | solution.py:442
  104.0 1.8 %place.1 = f32[20,40,64]{2,1,0:T(8,128)} custom-call(bf16[16,40,96]{2,1,0:T(8,128)(2,1)} %all_to_all.20.spec_ref), custom_call_target="tpu_custom_call" | custom-call | flops 1000000 | bytes 1000000 | tf_op jit(solution)/shard_map/place/pallas_call | solution.py:399
  105.8 15.5 %all-to-all-done.2 = f32[512,1,128]{2,1,0:T(1,128)S(1)} async-done(((f32[512,1,128]{2,1,0:T(1,128)}), f32[512,1,128]{2,1,0:T(1,128)S(1)}, u32[]{:S(2)}, u32[]{:S(2)}) %all-to-all-start.2) | async-done | bytes 262176 | tf_op jit(solution)/shard_map/bwdx/all_to_all | solution.py:442
  121.3 0.0 copy-start
  121.3 0.7 copy-done
  122.0 3.8 %inverse.1 = f32[20,2,1280]{2,1,0:T(2,128)} custom-call(f32[512,128]{1,0:T(8,128)} %bitcast.26, bf16[3,512,1280]{2,1,0:T(8,128)(2,1)} %get-tuple-element.7.t_any, f32[512,128]{1,0:T(8,128)} %get-tuple-element.8.even_ref, f32[512,128]{1,0:T(8,128)} %get-tuple-element.10.weight_ref), custom_call_target="tpu_custom_call" | custom-call | flops 100000000 | bytes 1000000 | tf_op jit(solution)/shard_map/inverse/pallas_call | solution.py:381
  (3 shorter events, 0.0 us)
Async XLA Ops:
  0.6 56.3 %copy-start.6 = (f32[32]{0:T(128)S(1)}, f32[32]{0:T(128)}, u32[]{:S(2)}) copy-start(f32[32]{0:T(128)} %param.13) | copy-start | bytes 388
  2.9 54.7 %copy-start.5 = (f32[32,32]{1,0:T(8,128)S(1)}, f32[32,32]{1,0:T(8,128)}, u32[]{:S(2)}) copy-start(f32[32,32]{1,0:T(8,128)} %param.15) | copy-start | bytes 12292
  2.9 54.8 %copy-start.2 = (f32[32,32]{1,0:T(8,128)S(1)}, f32[32,32]{1,0:T(8,128)}, u32[]{:S(2)}) copy-start(f32[32,32]{1,0:T(8,128)} %param.14) | copy-start | bytes 12292
  2.9 37.4 %all-to-all-start.1 = ((bf16[16,30,2,320]{3,2,1,0:T(2,128)(2,1)}), bf16[16,30,2,320]{3,2,1,0:T(2,128)(2,1)S(1)}, u32[]{:S(2)}, u32[]{:S(2)}) async-start(bf16[16,30,2,320]{3,2,1,0:T(2,128)(2,1)} %send_tables.1), calls=%async_computation.1 | async-start | bytes 1474560 | tf_op jit(solution)/shard_map/tabx/all_to_all | solution.py:442
  14.1 19.2 %collective-permute-start.1 = (f32[3,2,1280]{2,1,0:T(2,128)S(1)}, f32[3,2,1280]{2,1,0:T(2,128)S(1)}, u32[]{:S(2)}, u32[]{:S(2)}) collective-permute-start(f32[3,2,1280]{2,1,0:T(2,128)S(1)} %get-tuple-element.12), channel_id=1, source_target_pairs={{16,0},{32,16},{48,32},{64,48},{80,64},{96,80},{112,96},{128,112},... | collective-permute-start | bytes 92168 | tf_op jit(solution)/shard_map/ppermute | solution.py:450
  16.9 16.3 %collective-permute-start = (f32[3,2,1280]{2,1,0:T(2,128)S(1)}, f32[3,2,1280]{2,1,0:T(2,128)S(1)}, u32[]{:S(2)}, u32[]{:S(2)}) collective-permute-start(f32[3,2,1280]{2,1,0:T(2,128)S(1)} %get-tuple-element.13), channel_id=1, source_target_pairs={{0,16},{16,32},{32,48},{48,64},{64,80},{80,96},{96,112},{112,128},... | collective-permute-start | bytes 92168 | tf_op jit(solution)/shard_map/ppermute | solution.py:449
  33.2 0.6 copy-start.3
  33.2 0.6 copy-start.4
  40.3 33.7 %all-to-all-start = ((f32[512,1,128]{2,1,0:T(1,128)}), f32[512,1,128]{2,1,0:T(1,128)S(1)}, u32[]{:S(2)}, u32[]{:S(2)}) async-start(f32[512,1,128]{2,1,0:T(1,128)} %bitcast.25), calls=%async_computation | async-start | bytes 524288 | tf_op jit(solution)/shard_map/fwdx/all_to_all | solution.py:442
  74.1 0.7 copy-start.1
  91.0 30.3 %all-to-all-start.2 = ((f32[512,1,128]{2,1,0:T(1,128)}), f32[512,1,128]{2,1,0:T(1,128)S(1)}, u32[]{:S(2)}, u32[]{:S(2)}) async-start(f32[512,1,128]{2,1,0:T(1,128)} %bitcast.32), calls=%async_computation.2 | async-start | bytes 524288 | tf_op jit(solution)/shard_map/bwdx/all_to_all | solution.py:442
  121.3 0.7 copy-start

commit v3 on v2

--- a/solution.py
+++ b/solution.py
@@ -1,4 +1,3 @@
-import functools
 import math
 
 import jax
@@ -7,6 +6,7 @@
 from jax.experimental import pallas as pl
 from jax.experimental.pallas import tpu as pltpu
 from jax.sharding import PartitionSpec as P
+
 
 INTERPRET = False
 N_LAT, N_LEV = 32, 16
@@ -15,7 +15,6 @@
 NLON, HALF_LON = 1280, 640
 ROWS = 20
 LV = 2
-NLEV = 32
 QB = 40
 QP = N_LEV * QB
 HL = 320
@@ -35,7 +34,7 @@
     return 5 * (b >> 2) + 4
 
 
-def call(kernel, out_shape, in_specs, scratch, name, flops=10**7):
+def call(kernel, out_shape, in_specs, scratch, flops=10**7):
     many = isinstance(out_shape, (tuple, list))
     vm = pl.BlockSpec(memory_space=pltpu.VMEM)
     return pl.pallas_call(
@@ -44,7 +43,6 @@
         in_specs=in_specs,
         out_specs=[vm] * len(out_shape) if many else vm,
         scratch_shapes=scratch,
-        name=name,
         interpret=INTERPRET,
         cost_estimate=pl.CostEstimate(flops=flops, bytes_accessed=10**6, transcendentals=0),
     )
@@ -81,7 +79,7 @@
     slots = lax.broadcasted_iota(jnp.int32, (CHUNK, M), 1)
     lane = lax.broadcasted_iota(jnp.int32, (CHUNK, 128), 1)
     lane_f = lane.astype(F32)
-    assign = assign_ref[...]
+    assign = assign_ref[...].reshape(1, M).astype(F32)
 
     def step(i, carry):
         r0 = pl.multiple_of(i * CHUNK, CHUNK)
@@ -134,8 +132,7 @@
         ),
         [VM],
         [],
-        "tables",
-    )(assign.astype(F32).reshape(1, M))
+    )(assign)
 
 
 def forward_kernel(
@@ -230,7 +227,6 @@
             pltpu.VMEM((3, N_DEV, NLON), BF16),
             pltpu.SemaphoreType.DMA,
         ],
-        "forward",
         10**9,
     )(stencil, tracer, north, south, offsets, table, even)
 
@@ -353,7 +349,6 @@
             pltpu.VMEM((3, 32, HL), F32),
             pltpu.VMEM((N_LEV, QB, 96), F32),
         ],
-        "spectral",
         10**9,
     )(info, msgs, own, shared, damping, inv, vec, vecp)
 
@@ -383,7 +378,6 @@
         jax.ShapeDtypeStruct((ROWS, LV, NLON), F32),
         [VM, ANY, VM, VM],
         [pltpu.VMEM((3, N_DEV, HALF_LON), BF16), pltpu.SemaphoreType.DMA],
-        "inverse",
         10**8,
     )(msgs, table, even, weight)
 
@@ -396,7 +390,7 @@
 
 
 def place(spec):
-    return call(place_kernel, jax.ShapeDtypeStruct((SLOTS, QB, 64), F32), [VM], [], "place", 10**6)(spec)
+    return call(place_kernel, jax.ShapeDtypeStruct((SLOTS, QB, 64), F32), [VM], [], 10**6)(spec)
 
 
 def by_block(matrix):
@@ -442,19 +436,18 @@
     return lax.all_to_all(value, axes, split_axis=0, concat_axis=0, tiled=True)
 
 
-def on_device(tracer, offsets, stencil, assign, legendre, damping, vert_vecs, vert_inv):
+def step_of(tracer, offsets, stencil, assign, legendre, damping, vert_vecs, vert_inv):
     up = [(i, i + 1) for i in range(N_LAT - 1)]
     down = [(i + 1, i) for i in range(N_LAT - 1)]
     rows = jnp.swapaxes(tracer, 0, 1)
     north = lax.ppermute(rows[ROWS - 3 :], "lat", up)
     south = lax.ppermute(rows[:3], "lat", down)
     table, even, weight = tables(assign)
-    with jax.named_scope("tabx"):
-        matrices = exchange(send_tables(legendre), "lev")
+    packed = send_tables(legendre)
+    matrices = exchange(packed, "lev")
     own, shared = received_tables(matrices)
     msgs = forward(stencil, rows, north, south, jnp.swapaxes(offsets, 0, 1), table, even)
-    with jax.named_scope("fwdx"):
-        got = exchange(msgs.reshape(N_DEV, 1, 128), ("lat", "lev")).reshape(N_DEV, 128)
+    got = exchange(msgs.reshape(N_DEV, 1, 128), ("lat", "lev")).reshape(N_DEV, 128)
     lev = lax.axis_index("lev")
     mine = lax.dynamic_slice_in_dim(assign, lax.axis_index("lat") * SLOTS, SLOTS)
     info = jnp.stack([mine[own_slot(lev)], mine[shared_slot(lev)], lev & 1]).astype(jnp.int32)
@@ -468,10 +461,8 @@
         by_block(vert_vecs),
         by_block(level_order(vert_vecs, 0)),
     )
-    with jax.named_scope("bwdx"):
-        home = exchange(back.reshape(N_DEV, 1, 128), ("lat", "lev")).reshape(N_DEV, 128)
-    with jax.named_scope("specx"):
-        spec = exchange(spec, "lev")
+    home = exchange(back.reshape(N_DEV, 1, 128), ("lat", "lev")).reshape(N_DEV, 128)
+    spec = exchange(spec, "lev")
     tracer_new = inverse(home, table, even, weight)
     spectral_new = place(spec).reshape(SLOTS, 20, 2, 64)
     return jnp.swapaxes(tracer_new, 0, 1), jnp.swapaxes(spectral_new, 1, 2)
@@ -489,7 +480,7 @@
         P(),
     )
     return jax.shard_map(
-        on_device,
+        step_of,
         mesh=mesh,
         in_specs=placed,
         out_specs=(P("lev", "lat", None), P("lat", None, "lev", None)),

time: 127 us -> 126 us (level)
  waiting for transfers between devices: 24.9 us -> 26.2 us
  transfers between devices with their start and end apart: 5 -> 5, of which waited for: 3 -> 3; matrix products, arithmetic and copies ran while one was open for 9% -> 8% of each run, Pallas kernels for 11% -> 11%
where the time goes in v3:
time: 126 us; the launch traced here: 125 us
  starting transfers between devices  49.7 us (39%)
  waiting for transfers between devices  26.2 us (21%)
  Pallas kernels  24.9 us (20%)
  blocking collectives  11.5 us (9%)
  local copies, waits for them, and re-layouts  9.8 us (8%)
  other arithmetic  2.09 us (2%)
    all_to_all x3, starting transfers between devices, exchange(): return lax.all_to_all(value, axes, split_axis=0, concat_axis=0, tiled=True)  39 us
    all_to_all x3, waiting for transfers between devices, exchange(): return lax.all_to_all(value, axes, split_axis=0, concat_axis=0, tiled=True)  23.6 us
    all_to_all x1, blocking collectives, exchange(): return lax.all_to_all(value, axes, split_axis=0, concat_axis=0, tiled=True)  11.5 us
    ppermute x1, starting transfers between devices, step_of(): north = lax.ppermute(rows[ROWS - 3:], 'lat', up)  7.84 us
    pallas_call x1, Pallas kernels, forward(): call(forward_kernel, jax.ShapeDtypeStruct((N_DEV, 128), F32), [SM, VM, VM...  6.45 us
    pallas_call x1, Pallas kernels, tables(): call(tables_kernel, (jax.ShapeDtypeStruct((3, N_DEV, NLON), BF16), jax.Sh...  5.88 us
    pallas_call x1, Pallas kernels, spectral(): call(spectral_kernel, (jax.ShapeDtypeStruct((N_DEV, 128), F32), jax.Shape...  4.75 us
    pallas_call x1, Pallas kernels, inverse(): call(inverse_kernel, jax.ShapeDtypeStruct((ROWS, LV, NLON), F32), [VM, AN...  3.85 us
  transfers between devices with their start and end apart: 5, of which 3 were waited for; matrix products, arithmetic and copies ran while one was open for 8% of the time, Pallas kernels for 11%

profile of v3, /device:TPU:1, one launch (start us, length us, event | category | flops | bytes accessed | tf_op | source)
XLA Modules:
  0.0 125.2 jit_solution(6561094507672388280)
XLA Ops:
  0.6 0.0 copy-start.6
  0.6 0.0 copy-start.5
  0.7 2.2 %send_tables.1 = bf16[16,30,2,320]{3,2,1,0:T(2,128)(2,1)} custom-call(bf16[20,20,2,320]{3,2,1,0:T(2,128)(2,1)} %bitcast.27), custom_call_target="tpu_custom_call" | custom-call | flops 1000000 | bytes 2000000 | tf_op jit(solution)/shard_map/send_tables/pallas_call | solution.py:419
  2.9 0.0 copy-start.2
  2.9 10.4 %all-to-all-start.1 = ((bf16[16,30,2,320]{3,2,1,0:T(2,128)(2,1)}), bf16[16,30,2,320]{3,2,1,0:T(2,128)(2,1)S(1)}, u32[]{:S(2)}, u32[]{:S(2)}) async-start(bf16[16,30,2,320]{3,2,1,0:T(2,128)(2,1)} %send_tables.1), calls=%async_computation.1 | async-start | bytes 1474560 | tf_op jit(solution)/shard_map/all_to_all | solution.py:436
  13.3 0.8 fusion
  14.1 2.9 %collective-permute-start.1 = (f32[3,2,1280]{2,1,0:T(2,128)S(1)}, f32[3,2,1280]{2,1,0:T(2,128)S(1)}, u32[]{:S(2)}, u32[]{:S(2)}) collective-permute-start(f32[3,2,1280]{2,1,0:T(2,128)S(1)} %get-tuple-element.12), channel_id=1, source_target_pairs={{16,0},{32,16},{48,32},{64,48},{80,64},{96,80},{112,96},{128,112},... | collective-permute-start | bytes 92168 | tf_op jit(solution)/shard_map/ppermute | solution.py:444
  16.9 7.8 %collective-permute-start = (f32[3,2,1280]{2,1,0:T(2,128)S(1)}, f32[3,2,1280]{2,1,0:T(2,128)S(1)}, u32[]{:S(2)}, u32[]{:S(2)}) collective-permute-start(f32[3,2,1280]{2,1,0:T(2,128)S(1)} %get-tuple-element.13), channel_id=1, source_target_pairs={{0,16},{16,32},{32,48},{48,64},{64,80},{80,96},{96,112},{112,128},... | collective-permute-start | bytes 92168 | tf_op jit(solution)/shard_map/ppermute | solution.py:443
  24.8 5.9 %shard_map.95 = (bf16[3,512,1280]{2,1,0:T(8,128)(2,1)}, f32[512,128]{1,0:T(8,128)}, f32[512,128]{1,0:T(8,128)}) custom-call(s32[640]{0:T(1024)} %assign_ref.1), custom_call_target="tpu_custom_call" | custom-call | flops 10000000 | bytes 1000000 | tf_op jit(solution)/shard_map/pallas_call | solution.py:126
  30.7 2.6 %collective-permute-done.1.south_ref = f32[3,2,1280]{2,1,0:T(2,128)S(1)} collective-permute-done((f32[3,2,1280]{2,1,0:T(2,128)S(1)}, f32[3,2,1280]{2,1,0:T(2,128)S(1)}, u32[]{:S(2)}, u32[]{:S(2)}) %collective-permute-start.1) | collective-permute-done | bytes 30752 | tf_op jit(solution)/shard_map/ppermute | solution.py:444
  33.2 0.0 copy-start.3
  33.2 0.0 collective-permute-done.north_ref
  33.3 0.0 copy-start.4
  33.3 0.6 copy-done.3
  33.9 0.0 copy-done.4
  33.9 6.4 %shard_map.96 = f32[512,128]{1,0:T(8,128)} custom-call(f32[7,7]{1,0:T(8,128)} %stencil_ref.1, f32[20,2,1280]{2,1,0:T(2,128)} %bitcast.30, f32[3,2,1280]{2,1,0:T(2,128)} %copy-done.4, f32[3,2,1280]{2,1,0:T(2,128)} %copy-done.3, s32[20,2,1280]{2,1,0:T(2,128)} %bitcast.33, bf16[3,512,1280]{2,1,0:T(8,128)(2,1)} %get-tuple-element.7.t_any, ...), custom_call_target="tpu_custom_call" | custom-call | flops 1000000000 | bytes 1000000 | tf_op jit(solution)/shard_map/pallas_call | solution.py:216
  40.3 0.0 all-to-all-done.1
  40.3 15.6 %all-to-all-start = ((f32[512,1,128]{2,1,0:T(1,128)}), f32[512,1,128]{2,1,0:T(1,128)S(1)}, u32[]{:S(2)}, u32[]{:S(2)}) async-start(f32[512,1,128]{2,1,0:T(1,128)} %bitcast.25), calls=%async_computation | async-start | bytes 524288 | tf_op jit(solution)/shard_map/all_to_all | solution.py:436
  56.0 0.0 copy-done.6
  56.0 0.7 copy.25.damping_ref
  56.7 0.0 copy-done.5
  56.7 0.1 copy.21
  56.8 0.1 copy.23
  56.9 0.0 copy-done.2
  56.9 0.1 broadcast_multiply_fusion
  57.0 0.7 mul.82.vecp_ref
  57.7 0.7 mul.78.vec_ref
  58.4 0.7 mul.75.inv_ref
  59.1 1.4 %fusion.1 = (s32[1]{0:T(128)}, s32[1]{0:T(128)}) fusion(s32[640]{0:T(1024)} %assign_ref.1, s32[]{:T(128)S(6)} %dynamic_slice.11, s32[]{:T(128)S(6)} %dynamic_slice.13), kind=kLoop, calls=%fused_computation.6 | loop fusion | bytes 24 | tf_op jit(solution)/shard_map/dynamic_slice | solution.py:453
  60.6 2.0 %pad_add_fusion.info_ref = s32[3]{0:T(128)} fusion(s32[1]{0:T(128)} %bitcast, s32[1]{0:T(128)} %get-tuple-element.15, s32[1]{0:T(128)} %get-tuple-element.14), kind=kLoop, calls=%fused_computation.4 | loop fusion | flops 6 | bytes 24 | tf_op jit(solution)/shard_map/stack | solution.py:453
  62.5 0.3 slice.18
  62.9 1.2 reshape.64.own_ref
  64.0 0.2 slice.19
  64.2 0.9 reshape.65.shared_ref
  65.1 8.1 %all-to-all-done = f32[512,1,128]{2,1,0:T(1,128)S(1)} async-done(((f32[512,1,128]{2,1,0:T(1,128)}), f32[512,1,128]{2,1,0:T(1,128)S(1)}, u32[]{:S(2)}, u32[]{:S(2)}) %all-to-all-start) | async-done | bytes 262176 | tf_op jit(solution)/shard_map/all_to_all | solution.py:436
  73.2 0.0 copy-start.1
  73.2 0.7 copy-done.1
  73.9 4.8 %shard_map.97 = (f32[512,128]{1,0:T(8,128)}, bf16[16,40,96]{2,1,0:T(8,128)(2,1)}) custom-call(s32[3]{0:T(128)} %pad_add_fusion.info_ref, f32[512,128]{1,0:T(8,128)} %bitcast.31, bf16[640,320]{1,0:T(8,128)(2,1)} %reshape.64.own_ref, bf16[320,320]{1,0:T(8,128)(2,1)} %reshape.65.shared_ref, f32[32,1]{1,0:T(8,128)} %copy.25.damping_ref, f32[64,64]{1,0:T(8,128)} %mul.75.inv_ref, ...), custom_call_target="tpu_custom_call" | custom-call | flops 1000000000 | bytes 1000000 | tf_op jit(solution)/shard_map/pallas_call | solution.py:340
  78.6 11.5 %all_to_all.20.spec_ref = bf16[16,40,96]{2,1,0:T(8,128)(2,1)} all-to-all(bf16[16,40,96]{2,1,0:T(8,128)(2,1)} %get-tuple-element.11), channel_id=1, replica_groups=mesh['lat'=32,'lev'=16] {'lev'}, dimensions={0} | all-to-all | bytes 245760 | tf_op jit(solution)/shard_map/all_to_all | solution.py:436
  90.2 13.0 %all-to-all-start.2 = ((f32[512,1,128]{2,1,0:T(1,128)}), f32[512,1,128]{2,1,0:T(1,128)S(1)}, u32[]{:S(2)}, u32[]{:S(2)}) async-start(f32[512,1,128]{2,1,0:T(1,128)} %bitcast.32), calls=%async_computation.2 | async-start | bytes 524288 | tf_op jit(solution)/shard_map/all_to_all | solution.py:436
  103.2 1.8 %shard_map.99 = f32[20,40,64]{2,1,0:T(8,128)} custom-call(bf16[16,40,96]{2,1,0:T(8,128)(2,1)} %all_to_all.20.spec_ref), custom_call_target="tpu_custom_call" | custom-call | flops 1000000 | bytes 1000000 | tf_op jit(solution)/shard_map/pallas_call | solution.py:393
  104.9 15.5 %all-to-all-done.2 = f32[512,1,128]{2,1,0:T(1,128)S(1)} async-done(((f32[512,1,128]{2,1,0:T(1,128)}), f32[512,1,128]{2,1,0:T(1,128)S(1)}, u32[]{:S(2)}, u32[]{:S(2)}) %all-to-all-start.2) | async-done | bytes 262176 | tf_op jit(solution)/shard_map/all_to_all | solution.py:436
  120.5 0.0 copy-start
  120.5 0.7 copy-done
  121.2 3.8 %shard_map.98 = f32[20,2,1280]{2,1,0:T(2,128)} custom-call(f32[512,128]{1,0:T(8,128)} %bitcast.26, bf16[3,512,1280]{2,1,0:T(8,128)(2,1)} %get-tuple-element.7.t_any, f32[512,128]{1,0:T(8,128)} %get-tuple-element.8.even_ref, f32[512,128]{1,0:T(8,128)} %get-tuple-element.10.weight_ref), custom_call_target="tpu_custom_call" | custom-call | flops 100000000 | bytes 1000000 | tf_op jit(solution)/shard_map/pallas_call | solution.py:376
  (3 shorter events, 0.0 us)
Async XLA Ops:
  0.6 55.4 %copy-start.6 = (f32[32]{0:T(128)S(1)}, f32[32]{0:T(128)}, u32[]{:S(2)}) copy-start(f32[32]{0:T(128)} %param.13) | copy-start | bytes 388
  0.6 56.1 %copy-start.5 = (f32[32,32]{1,0:T(8,128)S(1)}, f32[32,32]{1,0:T(8,128)}, u32[]{:S(2)}) copy-start(f32[32,32]{1,0:T(8,128)} %param.15) | copy-start | bytes 12292
  2.9 53.9 %copy-start.2 = (f32[32,32]{1,0:T(8,128)S(1)}, f32[32,32]{1,0:T(8,128)}, u32[]{:S(2)}) copy-start(f32[32,32]{1,0:T(8,128)} %param.14) | copy-start | bytes 12292
  2.9 37.4 %all-to-all-start.1 = ((bf16[16,30,2,320]{3,2,1,0:T(2,128)(2,1)}), bf16[16,30,2,320]{3,2,1,0:T(2,128)(2,1)S(1)}, u32[]{:S(2)}, u32[]{:S(2)}) async-start(bf16[16,30,2,320]{3,2,1,0:T(2,128)(2,1)} %send_tables.1), calls=%async_computation.1 | async-start | bytes 1474560 | tf_op jit(solution)/shard_map/all_to_all | solution.py:436
  14.1 19.2 %collective-permute-start.1 = (f32[3,2,1280]{2,1,0:T(2,128)S(1)}, f32[3,2,1280]{2,1,0:T(2,128)S(1)}, u32[]{:S(2)}, u32[]{:S(2)}) collective-permute-start(f32[3,2,1280]{2,1,0:T(2,128)S(1)} %get-tuple-element.12), channel_id=1, source_target_pairs={{16,0},{32,16},{48,32},{64,48},{80,64},{96,80},{112,96},{128,112},... | collective-permute-start | bytes 92168 | tf_op jit(solution)/shard_map/ppermute | solution.py:444
  16.9 16.3 %collective-permute-start = (f32[3,2,1280]{2,1,0:T(2,128)S(1)}, f32[3,2,1280]{2,1,0:T(2,128)S(1)}, u32[]{:S(2)}, u32[]{:S(2)}) collective-permute-start(f32[3,2,1280]{2,1,0:T(2,128)S(1)} %get-tuple-element.13), channel_id=1, source_target_pairs={{0,16},{16,32},{32,48},{48,64},{64,80},{80,96},{96,112},{112,128},... | collective-permute-start | bytes 92168 | tf_op jit(solution)/shard_map/ppermute | solution.py:443
  33.2 0.6 copy-start.3
  33.3 0.6 copy-start.4
  40.3 32.9 %all-to-all-start = ((f32[512,1,128]{2,1,0:T(1,128)}), f32[512,1,128]{2,1,0:T(1,128)S(1)}, u32[]{:S(2)}, u32[]{:S(2)}) async-start(f32[512,1,128]{2,1,0:T(1,128)} %bitcast.25), calls=%async_computation | async-start | bytes 524288 | tf_op jit(solution)/shard_map/all_to_all | solution.py:436
  73.2 0.7 copy-start.1
  90.2 30.3 %all-to-all-start.2 = ((f32[512,1,128]{2,1,0:T(1,128)}), f32[512,1,128]{2,1,0:T(1,128)S(1)}, u32[]{:S(2)}, u32[]{:S(2)}) async-start(f32[512,1,128]{2,1,0:T(1,128)} %bitcast.32), calls=%async_computation.2 | async-start | bytes 524288 | tf_op jit(solution)/shard_map/all_to_all | solution.py:436
  120.5 0.7 copy-start

commit v4 on v3

--- a/solution.py
+++ b/solution.py
@@ -75,7 +75,11 @@
 CHUNK = 64
 
 
-def tables_kernel(assign_ref, t_ref, even_ref, weight_ref):
+def tables_kernel(assign_ref, t_out, even_ref, weight_ref, t_ref, sems):
+    def write(i):
+        rows = pl.ds(pl.multiple_of(i * CHUNK, CHUNK), CHUNK)
+        return pltpu.make_async_copy(t_ref.at[:, rows], t_out.at[:, rows], sems.at[i])
+
     slots = lax.broadcasted_iota(jnp.int32, (CHUNK, M), 1)
     lane = lax.broadcasted_iota(jnp.int32, (CHUNK, 128), 1)
     lane_f = lane.astype(F32)
@@ -117,29 +121,37 @@
         weight_ref[pl.ds(r0, CHUNK), :] = jnp.where(
             lane < 2 * MSG, weights[0], weights[1]
         )
+        write(i).start()
         return carry
 
     lax.fori_loop(0, N_DEV // CHUNK, step, 0)
+    for i in range(N_DEV // CHUNK):
+        write(i).wait()
 
 
 def tables(assign):
-    return call(
+    return pl.pallas_call(
         tables_kernel,
-        (
+        out_shape=(
             jax.ShapeDtypeStruct((3, N_DEV, NLON), BF16),
             jax.ShapeDtypeStruct((N_DEV, 128), F32),
             jax.ShapeDtypeStruct((N_DEV, 128), F32),
         ),
-        [VM],
-        [],
+        in_specs=[VM],
+        out_specs=(ANY, VM, VM),
+        scratch_shapes=[pltpu.VMEM((3, N_DEV, NLON), BF16), pltpu.SemaphoreType.DMA((N_DEV // CHUNK,))],
+        name="tables",
+        interpret=INTERPRET,
+        cost_estimate=pl.CostEstimate(flops=10**7, bytes_accessed=10**6, transcendentals=0),
     )(assign)
 
 
 def forward_kernel(
+    side_ref,
     stencil_ref,
     tracer_ref,
-    north_ref,
-    south_ref,
+    near_ref,
+    far_ref,
     off_ref,
     t_any,
     even_ref,
@@ -155,10 +167,11 @@
 ):
     fetch = pltpu.make_async_copy(t_any, t_ref, t_sem)
     fetch.start()
+    odd_band = side_ref[0] == 1
     pad[...] = jnp.zeros((64, NLON), F32)
     for i in range(3):
-        pad[2 + 2 * i : 4 + 2 * i, :] = north_ref[i]
-        pad[48 + 2 * i : 50 + 2 * i, :] = south_ref[i]
+        pad[2 + 2 * i : 4 + 2 * i, :] = jnp.where(odd_band, near_ref[i], far_ref[i])
+        pad[48 + 2 * i : 50 + 2 * i, :] = jnp.where(odd_band, far_ref[i], near_ref[i])
     for i in range(ROWS):
         pad[8 + 2 * i : 10 + 2 * i, :] = tracer_ref[i]
         codes[2 * i : 2 * i + 2, :] = off_ref[i]
@@ -212,11 +225,11 @@
     return ref[ci][k::2] if INTERPRET else ref[ci, pl.ds(k, ROWS, 2), :]
 
 
-def forward(stencil, tracer, north, south, offsets, table, even):
+def forward(side, stencil, tracer, near, far, offsets, table, even):
     return call(
         forward_kernel,
         jax.ShapeDtypeStruct((N_DEV, 128), F32),
-        [SM, VM, VM, VM, VM, ANY, VM],
+        [SM, SM, VM, VM, VM, VM, ANY, VM],
         [
             pltpu.VMEM((64, NLON), F32),
             pltpu.VMEM((7, 64, NLON), F32),
@@ -228,7 +241,7 @@
             pltpu.SemaphoreType.DMA,
         ],
         10**9,
-    )(stencil, tracer, north, south, offsets, table, even)
+    )(side, stencil, tracer, near, far, offsets, table, even)
 
 
 def mirror_matrix():
@@ -437,19 +450,21 @@
 
 
 def step_of(tracer, offsets, stencil, assign, legendre, damping, vert_vecs, vert_inv):
-    up = [(i, i + 1) for i in range(N_LAT - 1)]
-    down = [(i + 1, i) for i in range(N_LAT - 1)]
+    lat = lax.axis_index("lat")
+    side = lat & 1
     rows = jnp.swapaxes(tracer, 0, 1)
-    north = lax.ppermute(rows[ROWS - 3 :], "lat", up)
-    south = lax.ppermute(rows[:3], "lat", down)
+    near = lax.dynamic_slice_in_dim(rows, jnp.where(side == 1, 0, ROWS - 3), 3)
+    near = lax.ppermute(near, "lat", [(i, i ^ 1) for i in range(N_LAT)])
+    far = lax.dynamic_slice_in_dim(rows, jnp.where(side == 1, ROWS - 3, 0), 3)
+    far = lax.ppermute(far, "lat", [(i, i + 2 * (i & 1) - 1) for i in range(1, N_LAT - 1)])
     table, even, weight = tables(assign)
     packed = send_tables(legendre)
     matrices = exchange(packed, "lev")
     own, shared = received_tables(matrices)
-    msgs = forward(stencil, rows, north, south, jnp.swapaxes(offsets, 0, 1), table, even)
+    msgs = forward(side.reshape(1), stencil, rows, near, far, jnp.swapaxes(offsets, 0, 1), table, even)
     got = exchange(msgs.reshape(N_DEV, 1, 128), ("lat", "lev")).reshape(N_DEV, 128)
     lev = lax.axis_index("lev")
-    mine = lax.dynamic_slice_in_dim(assign, lax.axis_index("lat") * SLOTS, SLOTS)
+    mine = lax.dynamic_slice_in_dim(assign, lat * SLOTS, SLOTS)
     info = jnp.stack([mine[own_slot(lev)], mine[shared_slot(lev)], lev & 1]).astype(jnp.int32)
     back, spec = spectral(
         info,

time: 126 us -> 126 us (level)
  no operation moved by 1% of the time
where the time goes in v4:
time: 126 us; the launch traced here: 125 us
  starting transfers between devices  49.7 us (39%)
  waiting for transfers between devices  26.4 us (21%)
  Pallas kernels  24.7 us (20%)
  blocking collectives  11.5 us (9%)
  local copies, waits for them, and re-layouts  9.8 us (8%)
  other arithmetic  2.09 us (2%)
    all_to_all x3, starting transfers between devices, exchange(): return lax.all_to_all(value, axes, split_axis=0, concat_axis=0, tiled=True)  39 us
    all_to_all x3, waiting for transfers between devices, exchange(): return lax.all_to_all(value, axes, split_axis=0, concat_axis=0, tiled=True)  23.6 us
    all_to_all x1, blocking collectives, exchange(): return lax.all_to_all(value, axes, split_axis=0, concat_axis=0, tiled=True)  11.5 us
    ppermute x1, starting transfers between devices, step_of(): lax.ppermute(far, 'lat', [(i, i + 2 * (i & 1) - 1) for i in range(1, N_LA...  8.77 us
    pallas_call x1, Pallas kernels, forward(): call(forward_kernel, jax.ShapeDtypeStruct((N_DEV, 128), F32), [SM, SM, VM...  6.43 us
    pallas_call x1, Pallas kernels, tables(): pl.pallas_call(tables_kernel, out_shape=(jax.ShapeDtypeStruct((3, N_DEV,...  5.66 us
    pallas_call x1, Pallas kernels, spectral(): call(spectral_kernel, (jax.ShapeDtypeStruct((N_DEV, 128), F32), jax.Shape...  4.74 us
    pallas_call x1, Pallas kernels, inverse(): call(inverse_kernel, jax.ShapeDtypeStruct((ROWS, LV, NLON), F32), [VM, AN...  3.85 us
  transfers between devices with their start and end apart: 5, of which 3 were waited for; matrix products, arithmetic and copies ran while one was open for 8% of the time, Pallas kernels for 11%

profile of v4, /device:TPU:1, one launch (start us, length us, event | category | flops | bytes accessed | tf_op | source)
XLA Modules:
  0.0 125.2 jit_solution(4129883498236128201)
XLA Ops:
  0.6 0.0 copy-start.6
  0.6 0.0 copy-start.5
  0.7 2.2 %send_tables.1 = bf16[16,30,2,320]{3,2,1,0:T(2,128)(2,1)} custom-call(bf16[20,20,2,320]{3,2,1,0:T(2,128)(2,1)} %bitcast.32), custom_call_target="tpu_custom_call" | custom-call | flops 1000000 | bytes 2000000 | tf_op jit(solution)/shard_map/send_tables/pallas_call | solution.py:432
  2.9 0.0 copy-start.2
  2.9 10.4 %all-to-all-start.1 = ((bf16[16,30,2,320]{3,2,1,0:T(2,128)(2,1)}), bf16[16,30,2,320]{3,2,1,0:T(2,128)(2,1)S(1)}, u32[]{:S(2)}, u32[]{:S(2)}) async-start(bf16[16,30,2,320]{3,2,1,0:T(2,128)(2,1)} %send_tables.1), calls=%async_computation.1 | async-start | bytes 1474560 | tf_op jit(solution)/shard_map/all_to_all | solution.py:449
  13.3 0.8 dynamic-slice_bitcast_fusion
  14.1 8.8 %collective-permute-start.1 = (f32[3,2,1280]{2,1,0:T(2,128)S(1)}, f32[3,2,1280]{2,1,0:T(2,128)S(1)}, u32[]{:S(2)}, u32[]{:S(2)}) collective-permute-start(f32[3,2,1280]{2,1,0:T(2,128)S(1)} %get-tuple-element.12), channel_id=1, source_target_pairs={{16,32},{32,16},{48,64},{64,48},{80,96},{96,80},{112,128},{128,112... | collective-permute-start | bytes 92168 | tf_op jit(solution)/shard_map/ppermute | solution.py:459
  22.9 1.9 %collective-permute-start = (f32[3,2,1280]{2,1,0:T(2,128)S(1)}, f32[3,2,1280]{2,1,0:T(2,128)S(1)}, u32[]{:S(2)}, u32[]{:S(2)}) collective-permute-start(f32[3,2,1280]{2,1,0:T(2,128)S(1)} %get-tuple-element.13), channel_id=1, source_target_pairs={{0,16},{16,0},{32,48},{48,32},{64,80},{80,64},{96,112},{112,96},{1... | collective-permute-start | bytes 92168 | tf_op jit(solution)/shard_map/ppermute | solution.py:457
  24.8 5.7 %tables.1 = (bf16[3,512,1280]{2,1,0:T(8,128)(2,1)}, f32[512,128]{1,0:T(8,128)}, f32[512,128]{1,0:T(8,128)}) custom-call(s32[640]{0:T(1024)} %assign_ref.1), custom_call_target="tpu_custom_call" | custom-call | flops 10000000 | bytes 1000000 | tf_op jit(solution)/shard_map/tables/pallas_call | solution.py:133
  30.5 2.8 %collective-permute-done.1.far_ref = f32[3,2,1280]{2,1,0:T(2,128)S(1)} collective-permute-done((f32[3,2,1280]{2,1,0:T(2,128)S(1)}, f32[3,2,1280]{2,1,0:T(2,128)S(1)}, u32[]{:S(2)}, u32[]{:S(2)}) %collective-permute-start.1) | collective-permute-done | bytes 30752 | tf_op jit(solution)/shard_map/ppermute | solution.py:459
  33.2 0.0 copy-start.3
  33.2 0.0 collective-permute-done.near_ref
  33.3 0.0 copy-start.4
  33.3 0.6 copy-done.3
  33.9 0.0 copy-done.4
  33.9 6.4 %shard_map.95 = f32[512,128]{1,0:T(8,128)} custom-call(s32[1]{0:T(128)} %bitcast.1.side_ref, f32[7,7]{1,0:T(8,128)} %stencil_ref.1, f32[20,2,1280]{2,1,0:T(2,128)} %bitcast.34, f32[3,2,1280]{2,1,0:T(2,128)} %copy-done.4, f32[3,2,1280]{2,1,0:T(2,128)} %copy-done.3, s32[20,2,1280]{2,1,0:T(2,128)} %bitcast.37, bf16[3,512,1280]{2,1,0:T(8,128)(2,1)} %get-tuple-element.7.t_any, ...), custom_call_target="tpu_custom_call" | custom-call | flops 1000000000 | bytes 1000000 | tf_op jit(solution)/shard_map/pallas_call | solution.py:229
  40.3 0.0 all-to-all-done.1
  40.3 15.7 %all-to-all-start = ((f32[512,1,128]{2,1,0:T(1,128)}), f32[512,1,128]{2,1,0:T(1,128)S(1)}, u32[]{:S(2)}, u32[]{:S(2)}) async-start(f32[512,1,128]{2,1,0:T(1,128)} %bitcast.30), calls=%async_computation | async-start | bytes 524288 | tf_op jit(solution)/shard_map/all_to_all | solution.py:449
  56.0 0.0 copy-done.6
  56.0 0.7 copy.25.damping_ref
  56.7 0.0 copy-done.5
  56.7 0.1 copy.21
  56.8 0.1 copy.23
  56.9 0.0 copy-done.2
  56.9 0.1 broadcast_multiply_fusion
  57.0 0.7 mul.82.vecp_ref
  57.7 0.7 mul.78.vec_ref
  58.4 0.7 mul.75.inv_ref
  59.2 1.4 %fusion = (s32[1]{0:T(128)}, s32[1]{0:T(128)}) fusion(s32[640]{0:T(1024)} %assign_ref.1, s32[]{:T(128)S(6)} %dynamic_slice.17, s32[]{:T(128)S(6)} %dynamic_slice.19), kind=kLoop, calls=%fused_computation.7 | loop fusion | bytes 24 | tf_op jit(solution)/shard_map/dynamic_slice | solution.py:468
  60.6 2.0 %pad_add_fusion.info_ref = s32[3]{0:T(128)} fusion(s32[1]{0:T(128)} %bitcast, s32[1]{0:T(128)} %get-tuple-element.15, s32[1]{0:T(128)} %get-tuple-element.14), kind=kLoop, calls=%fused_computation.6 | loop fusion | flops 6 | bytes 24 | tf_op jit(solution)/shard_map/stack | solution.py:468
  62.5 0.3 slice.8
  62.9 1.2 reshape.68.own_ref
  64.1 0.2 slice.9
  64.2 0.9 reshape.69.shared_ref
  65.1 8.1 %all-to-all-done = f32[512,1,128]{2,1,0:T(1,128)S(1)} async-done(((f32[512,1,128]{2,1,0:T(1,128)}), f32[512,1,128]{2,1,0:T(1,128)S(1)}, u32[]{:S(2)}, u32[]{:S(2)}) %all-to-all-start) | async-done | bytes 262176 | tf_op jit(solution)/shard_map/all_to_all | solution.py:449
  73.2 0.0 copy-start.1
  73.2 0.7 copy-done.1
  73.9 4.7 %shard_map.96 = (f32[512,128]{1,0:T(8,128)}, bf16[16,40,96]{2,1,0:T(8,128)(2,1)}) custom-call(s32[3]{0:T(128)} %pad_add_fusion.info_ref, f32[512,128]{1,0:T(8,128)} %bitcast.35, bf16[640,320]{1,0:T(8,128)(2,1)} %reshape.68.own_ref, bf16[320,320]{1,0:T(8,128)(2,1)} %reshape.69.shared_ref, f32[32,1]{1,0:T(8,128)} %copy.25.damping_ref, f32[64,64]{1,0:T(8,128)} %mul.75.inv_ref, ...), custom_call_target="tpu_custom_call" | custom-call | flops 1000000000 | bytes 1000000 | tf_op jit(solution)/shard_map/pallas_call | solution.py:353
  78.7 11.5 %all_to_all.20.spec_ref = bf16[16,40,96]{2,1,0:T(8,128)(2,1)} all-to-all(bf16[16,40,96]{2,1,0:T(8,128)(2,1)} %get-tuple-element.11), channel_id=1, replica_groups=mesh['lat'=32,'lev'=16] {'lev'}, dimensions={0} | all-to-all | bytes 245760 | tf_op jit(solution)/shard_map/all_to_all | solution.py:449
  90.2 13.0 %all-to-all-start.2 = ((f32[512,1,128]{2,1,0:T(1,128)}), f32[512,1,128]{2,1,0:T(1,128)S(1)}, u32[]{:S(2)}, u32[]{:S(2)}) async-start(f32[512,1,128]{2,1,0:T(1,128)} %bitcast.36), calls=%async_computation.2 | async-start | bytes 524288 | tf_op jit(solution)/shard_map/all_to_all | solution.py:449
  103.2 1.8 %shard_map.98 = f32[20,40,64]{2,1,0:T(8,128)} custom-call(bf16[16,40,96]{2,1,0:T(8,128)(2,1)} %all_to_all.20.spec_ref), custom_call_target="tpu_custom_call" | custom-call | flops 1000000 | bytes 1000000 | tf_op jit(solution)/shard_map/pallas_call | solution.py:406
  104.9 15.5 %all-to-all-done.2 = f32[512,1,128]{2,1,0:T(1,128)S(1)} async-done(((f32[512,1,128]{2,1,0:T(1,128)}), f32[512,1,128]{2,1,0:T(1,128)S(1)}, u32[]{:S(2)}, u32[]{:S(2)}) %all-to-all-start.2) | async-done | bytes 262176 | tf_op jit(solution)/shard_map/all_to_all | solution.py:449
  120.5 0.0 copy-start
  120.5 0.7 copy-done
  121.2 3.8 %shard_map.97 = f32[20,2,1280]{2,1,0:T(2,128)} custom-call(f32[512,128]{1,0:T(8,128)} %bitcast.31, bf16[3,512,1280]{2,1,0:T(8,128)(2,1)} %get-tuple-element.7.t_any, f32[512,128]{1,0:T(8,128)} %get-tuple-element.8.even_ref, f32[512,128]{1,0:T(8,128)} %get-tuple-element.10.weight_ref), custom_call_target="tpu_custom_call" | custom-call | flops 100000000 | bytes 1000000 | tf_op jit(solution)/shard_map/pallas_call | solution.py:389
  (3 shorter events, 0.0 us)
Async XLA Ops:
  0.6 55.4 %copy-start.6 = (f32[32]{0:T(128)S(1)}, f32[32]{0:T(128)}, u32[]{:S(2)}) copy-start(f32[32]{0:T(128)} %param.13) | copy-start | bytes 388
  0.6 56.1 %copy-start.5 = (f32[32,32]{1,0:T(8,128)S(1)}, f32[32,32]{1,0:T(8,128)}, u32[]{:S(2)}) copy-start(f32[32,32]{1,0:T(8,128)} %param.15) | copy-start | bytes 12292
  2.9 54.0 %copy-start.2 = (f32[32,32]{1,0:T(8,128)S(1)}, f32[32,32]{1,0:T(8,128)}, u32[]{:S(2)}) copy-start(f32[32,32]{1,0:T(8,128)} %param.14) | copy-start | bytes 12292
  2.9 37.4 %all-to-all-start.1 = ((bf16[16,30,2,320]{3,2,1,0:T(2,128)(2,1)}), bf16[16,30,2,320]{3,2,1,0:T(2,128)(2,1)S(1)}, u32[]{:S(2)}, u32[]{:S(2)}) async-start(bf16[16,30,2,320]{3,2,1,0:T(2,128)(2,1)} %send_tables.1), calls=%async_computation.1 | async-start | bytes 1474560 | tf_op jit(solution)/shard_map/all_to_all | solution.py:449
  14.1 19.1 %collective-permute-start.1 = (f32[3,2,1280]{2,1,0:T(2,128)S(1)}, f32[3,2,1280]{2,1,0:T(2,128)S(1)}, u32[]{:S(2)}, u32[]{:S(2)}) collective-permute-start(f32[3,2,1280]{2,1,0:T(2,128)S(1)} %get-tuple-element.12), channel_id=1, source_target_pairs={{16,32},{32,16},{48,64},{64,48},{80,96},{96,80},{112,128},{128,112... | collective-permute-start | bytes 92168 | tf_op jit(solution)/shard_map/ppermute | solution.py:459
  22.9 10.4 %collective-permute-start = (f32[3,2,1280]{2,1,0:T(2,128)S(1)}, f32[3,2,1280]{2,1,0:T(2,128)S(1)}, u32[]{:S(2)}, u32[]{:S(2)}) collective-permute-start(f32[3,2,1280]{2,1,0:T(2,128)S(1)} %get-tuple-element.13), channel_id=1, source_target_pairs={{0,16},{16,0},{32,48},{48,32},{64,80},{80,64},{96,112},{112,96},{1... | collective-permute-start | bytes 92168 | tf_op jit(solution)/shard_map/ppermute | solution.py:457
  33.2 0.6 copy-start.3
  33.3 0.6 copy-start.4
  40.3 32.9 %all-to-all-start = ((f32[512,1,128]{2,1,0:T(1,128)}), f32[512,1,128]{2,1,0:T(1,128)S(1)}, u32[]{:S(2)}, u32[]{:S(2)}) async-start(f32[512,1,128]{2,1,0:T(1,128)} %bitcast.30), calls=%async_computation | async-start | bytes 524288 | tf_op jit(solution)/shard_map/all_to_all | solution.py:449
  73.2 0.7 copy-start.1
  90.2 30.3 %all-to-all-start.2 = ((f32[512,1,128]{2,1,0:T(1,128)}), f32[512,1,128]{2,1,0:T(1,128)S(1)}, u32[]{:S(2)}, u32[]{:S(2)}) async-start(f32[512,1,128]{2,1,0:T(1,128)} %bitcast.36), calls=%async_computation.2 | async-start | bytes 524288 | tf_op jit(solution)/shard_map/all_to_all | solution.py:449
  120.5 0.7 copy-start

commit v5 on v4

--- a/solution.py
+++ b/solution.py
@@ -20,6 +20,8 @@
 HL = 320
 SLOTS = 20
 MSG = LV * ROWS
+WIDE = 56
+ZROW = 25
 F32, BF16 = jnp.float32, jnp.bfloat16
 NT = (((1,), (1,)), ((), ()))
 NN = (((1,), (0,)), ((), ()))
@@ -265,13 +267,11 @@
     vec_ref,
     vecp_ref,
     out_ref,
-    spec_ref,
     nbuf,
     sbuf,
     flip,
-    zn,
-    zs,
-    solved,
+    zonal,
+    wide,
 ):
     mirror = mirror_matrix()
     half = N_DEV // 2
@@ -322,8 +322,9 @@
         ).astype(BF16)
         back = lax.dot_general(left, matrix, NN, preferred_element_type=F32)
         for u, j in enumerate(units):
-            zn[j] = back[64 * u : 64 * u + 32]
-            zs[j] = back[64 * u + 32 : 64 * u + 64]
+            lats = jnp.concatenate([back[64 * u : 64 * u + 32], back[64 * u + 32 : 64 * u + 64]], axis=1)
+            for tile in range(5):
+                zonal[tile, 32 * j : 32 * j + 32, :] = lats[:, 128 * tile : 128 * tile + 128]
         return exact(vec_ref[:size, :size], modal).T
 
     lane = lax.broadcasted_iota(jnp.int32, (32, QP), 1)
@@ -331,46 +332,79 @@
     lane = lax.broadcasted_iota(jnp.int32, (32, QP // 2), 1)
     block = jnp.floor((lane.astype(F32) + 0.5) * (1.0 / 20.0)).astype(jnp.int32)
     part = solve((2,), shared_ref[...], lane + 20 * block + 20 * info_ref[2] + info_ref[1], (lane & 1) == 1)
-    solved[...] = jnp.zeros((N_LEV, QB, 96), F32)
     for b in range(N_LEV):
-        solved[b, :, 0:64] = whole[QB * b : QB * b + QB]
-        solved[b, 0:20, 64:96] = part[20 * b : 20 * b + 20]
-    spec_ref[...] = solved[...].astype(BF16)
-    out_ref[...] = jnp.zeros((N_DEV, 128), F32)
-    flip[...] = jnp.zeros((half, 128), F32)
-    for a in range(N_LAT // 2):
-        for j in range(3):
-            for k in range(LV):
-                lane = MSG * j + ROWS * k
-                out_ref[16 * a : 16 * a + 16, lane : lane + ROWS] = zn[j, 16 * k : 16 * k + 16, ROWS * a : ROWS * a + ROWS]
-                flip[16 * (15 - a) : 16 * (15 - a) + 16, lane : lane + ROWS] = zs[
-                    j, 16 * k : 16 * k + 16, ROWS * a : ROWS * a + ROWS
-                ]
-    out_ref[half:, :] = lax.dot_general(flip[...], mirror, NN, precision=HIGH, preferred_element_type=F32)
+        wide[b, 0:20, 0:64] = whole[QB * b : QB * b + 20]
+        wide[b, 0:20, 64:128] = whole[QB * b + 20 : QB * b + 40]
+        for g in range(4):
+            wide[b, 20:25, 32 * g : 32 * g + 32] = part[20 * b + 5 * g : 20 * b + 5 * g + 5]
+        for tile in range(5):
+            wide[b, ZROW + 6 * tile : ZROW + 6 * tile + 6, :] = strided(zonal, tile, b, 6, 16)
+        wide[b, ZROW + 30 : WIDE, :] = jnp.zeros((WIDE - ZROW - 30, 128), F32)
+    out_ref[...] = wide[...].astype(BF16)
+
+
+def strided(ref, tile, start, count, stride):
+    if INTERPRET:
+        return ref[tile][start :: stride][:count]
+    return ref[tile, pl.ds(start, count, stride), :]
 
 
 def spectral(info, msgs, own, shared, damping, inv, vec, vecp):
     return call(
         spectral_kernel,
-        (jax.ShapeDtypeStruct((N_DEV, 128), F32), jax.ShapeDtypeStruct((N_LEV, QB, 96), BF16)),
+        jax.ShapeDtypeStruct((N_LEV, WIDE, 128), BF16),
         [SM, VM, VM, VM, VM, VM, VM, VM],
         [
             pltpu.VMEM((3, 32, HL), F32),
             pltpu.VMEM((3, 32, HL), F32),
             pltpu.VMEM((N_DEV // 2, 128), F32),
-            pltpu.VMEM((3, 32, HL), F32),
-            pltpu.VMEM((3, 32, HL), F32),
-            pltpu.VMEM((N_LEV, QB, 96), F32),
+            pltpu.VMEM((5, 96, 128), F32),
+            pltpu.VMEM((N_LEV, WIDE, 128), F32),
         ],
         10**9,
     )(info, msgs, own, shared, damping, inv, vec, vecp)
+
+
+def bands_kernel(wide_ref, out_ref, rows, out, flip):
+    half = N_DEV // 2
+    for b in range(N_LEV):
+        value = wide_ref[b].astype(F32)
+        for tile in range(5):
+            rows[tile, 8 * b : 8 * b + 6, :] = value[ZROW + 6 * tile : ZROW + 6 * tile + 6]
+    out[...] = jnp.zeros((half, 128), F32)
+    flip[...] = jnp.zeros((half, 128), F32)
+    for j in range(3):
+        for k in range(LV):
+            lane = MSG * j + ROWS * k
+            lats = jnp.concatenate([strided(rows, tile, LV * j + k, N_LEV, 8) for tile in range(5)], axis=1)
+            for a in range(N_LAT // 2):
+                out[16 * a : 16 * a + 16, lane : lane + ROWS] = lats[:, ROWS * a : ROWS * a + ROWS]
+                flip[16 * (15 - a) : 16 * (15 - a) + 16, lane : lane + ROWS] = lats[:, HL + ROWS * a : HL + ROWS * a + ROWS]
+    mirror = mirror_matrix().astype(BF16)
+    low = lax.dot_general(flip[...].astype(BF16), mirror, NN, preferred_element_type=F32)
+    out_ref[:half, :] = out[...].astype(BF16)
+    out_ref[half:, :] = low.astype(BF16)
+
+
+def bands(wide):
+    return call(
+        bands_kernel,
+        jax.ShapeDtypeStruct((N_DEV, 128), BF16),
+        [VM],
+        [
+            pltpu.VMEM((5, 8 * N_LEV, 128), F32),
+            pltpu.VMEM((N_DEV // 2, 128), F32),
+            pltpu.VMEM((N_DEV // 2, 128), F32),
+        ],
+        10**7,
+    )(wide)
 
 
 def inverse_kernel(msg_ref, t_any, even_ref, weight_ref, out_ref, t_ref, t_sem):
     fetch = pltpu.make_async_copy(t_any.at[:, :, pl.ds(0, HALF_LON)], t_ref, t_sem)
     fetch.start()
     lane = lax.broadcasted_iota(jnp.int32, (N_DEV, 128), 1)
-    scaled = jnp.where(lane < 3 * MSG, msg_ref[...] * weight_ref[...], 0.0)
+    scaled = jnp.where(lane < 3 * MSG, msg_ref[...].astype(F32) * weight_ref[...], 0.0)
     even = (scaled * even_ref[...]).T
     odd = (scaled * (1.0 - even_ref[...])).T
     total = jnp.zeros((2 * MSG, HALF_LON), F32)
@@ -398,8 +432,12 @@
 def place_kernel(spec_ref, out_ref):
     for b in range(N_LEV):
         c, half = (b & 3) >> 1, b & 1
-        out_ref[own_slot(b)] = spec_ref[b, :, 0:64].astype(F32)
-        out_ref[shared_slot(b), 20 * half : 20 * half + 20, 32 * c : 32 * c + 32] = spec_ref[b, 0:20, 64:96].astype(F32)
+        value = spec_ref[b].astype(F32)
+        out_ref[own_slot(b), 0:20, :] = value[0:20, 0:64]
+        out_ref[own_slot(b), 20:40, :] = value[0:20, 64:128]
+        for g in range(4):
+            first = 20 * half + 5 * g
+            out_ref[shared_slot(b), first : first + 5, 32 * c : 32 * c + 32] = value[20:25, 32 * g : 32 * g + 32]
 
 
 def place(spec):
@@ -466,7 +504,7 @@
     lev = lax.axis_index("lev")
     mine = lax.dynamic_slice_in_dim(assign, lat * SLOTS, SLOTS)
     info = jnp.stack([mine[own_slot(lev)], mine[shared_slot(lev)], lev & 1]).astype(jnp.int32)
-    back, spec = spectral(
+    solved = spectral(
         info,
         got,
         own,
@@ -476,10 +514,10 @@
         by_block(vert_vecs),
         by_block(level_order(vert_vecs, 0)),
     )
-    home = exchange(back.reshape(N_DEV, 1, 128), ("lat", "lev")).reshape(N_DEV, 128)
-    spec = exchange(spec, "lev")
+    solved = exchange(solved, "lev")
+    home = exchange(bands(solved).reshape(N_LAT, N_LEV, 128), "lat").reshape(N_DEV, 128)
     tracer_new = inverse(home, table, even, weight)
-    spectral_new = place(spec).reshape(SLOTS, 20, 2, 64)
+    spectral_new = place(solved).reshape(SLOTS, 20, 2, 64)
     return jnp.swapaxes(tracer_new, 0, 1), jnp.swapaxes(spectral_new, 1, 2)
 
 

time: 126 us -> 122 us (0.968)
  waiting for transfers between devices: 26.4 us -> 22.3 us
  starting transfers between devices: 49.7 us -> 46.3 us
  Pallas kernels: 24.7 us -> 26.6 us
  blocking collectives: 11.5 us -> 13.2 us
    all_to_all x3, waiting for transfers between devices: 23.6 us -> 19.5 us  [exchange(): return lax.all_to_all(value, axes, split_axis=0, concat_axis=0, tiled=True)]
    all_to_all x3, starting transfers between devices: 39 us -> 35.7 us  [exchange(): return lax.all_to_all(value, axes, split_axis=0, concat_axis=0, tiled=True)]
    pallas_call x1 -> x2, Pallas kernels: 4.74 us -> 6.63 us  [the longest x1 4.43 us: spectral(): call(spectral_kernel, jax.ShapeDtypeStruct((N_LEV, WIDE, 128), BF16), [SM...]
    all_to_all x1, blocking collectives: 11.5 us -> 13.2 us  [exchange(): return lax.all_to_all(value, axes, split_axis=0, concat_axis=0, tiled=True)]
  transfers between devices with their start and end apart: 5 -> 5, of which waited for: 3 -> 3; matrix products, arithmetic and copies ran while one was open for 8% -> 8% of each run, Pallas kernels for 11% -> 12%
where the time goes in v5:
time: 122 us; the launch traced here: 121 us
  starting transfers between devices  46.3 us (38%)
  Pallas kernels  26.6 us (22%)
  waiting for transfers between devices  22.3 us (18%)
  blocking collectives  13.2 us (11%)
  local copies, waits for them, and re-layouts  9.73 us (8%)
  other arithmetic  2 us (2%)
    all_to_all x3, starting transfers between devices, exchange(): return lax.all_to_all(value, axes, split_axis=0, concat_axis=0, tiled=True)  35.7 us
    all_to_all x3, waiting for transfers between devices, exchange(): return lax.all_to_all(value, axes, split_axis=0, concat_axis=0, tiled=True)  19.5 us
    all_to_all x1, blocking collectives, exchange(): return lax.all_to_all(value, axes, split_axis=0, concat_axis=0, tiled=True)  13.2 us
    ppermute x1, starting transfers between devices, step_of(): lax.ppermute(far, 'lat', [(i, i + 2 * (i & 1) - 1) for i in range(1, N_LA...  8.77 us
    pallas_call x1, Pallas kernels, forward(): call(forward_kernel, jax.ShapeDtypeStruct((N_DEV, 128), F32), [SM, SM, VM...  6.43 us
    pallas_call x1, Pallas kernels, tables(): pl.pallas_call(tables_kernel, out_shape=(jax.ShapeDtypeStruct((3, N_DEV,...  5.66 us
    pallas_call x1, Pallas kernels, spectral(): call(spectral_kernel, jax.ShapeDtypeStruct((N_LEV, WIDE, 128), BF16), [SM...  4.43 us
    pallas_call x1, Pallas kernels, inverse(): call(inverse_kernel, jax.ShapeDtypeStruct((ROWS, LV, NLON), F32), [VM, AN...  3.83 us
  transfers between devices with their start and end apart: 5, of which 3 were waited for; matrix products, arithmetic and copies ran while one was open for 8% of the time, Pallas kernels for 12%

profile of v5, /device:TPU:1, one launch (start us, length us, event | category | flops | bytes accessed | tf_op | source)
XLA Modules:
  0.0 121.0 jit_solution(10290795927499998033)
XLA Ops:
  0.6 0.0 copy-start.6
  0.6 0.0 copy-start.5
  0.7 2.2 %send_tables.1 = bf16[16,30,2,320]{3,2,1,0:T(2,128)(2,1)} custom-call(bf16[20,20,2,320]{3,2,1,0:T(2,128)(2,1)} %bitcast.29), custom_call_target="tpu_custom_call" | custom-call | flops 1000000 | bytes 2000000 | tf_op jit(solution)/shard_map/send_tables/pallas_call | solution.py:470
  2.9 0.0 copy-start.2
  2.9 10.4 %all-to-all-start.1 = ((bf16[16,30,2,320]{3,2,1,0:T(2,128)(2,1)}), bf16[16,30,2,320]{3,2,1,0:T(2,128)(2,1)S(1)}, u32[]{:S(2)}, u32[]{:S(2)}) async-start(bf16[16,30,2,320]{3,2,1,0:T(2,128)(2,1)} %send_tables.1), calls=%async_computation.1 | async-start | bytes 1474560 | tf_op jit(solution)/shard_map/all_to_all | solution.py:487
  13.3 0.8 dynamic-slice_bitcast_fusion
  14.1 8.8 %collective-permute-start.1 = (f32[3,2,1280]{2,1,0:T(2,128)S(1)}, f32[3,2,1280]{2,1,0:T(2,128)S(1)}, u32[]{:S(2)}, u32[]{:S(2)}) collective-permute-start(f32[3,2,1280]{2,1,0:T(2,128)S(1)} %get-tuple-element.8), channel_id=1, source_target_pairs={{16,32},{32,16},{48,64},{64,48},{80,96},{96,80},{112,128},{128,112... | collective-permute-start | bytes 92168 | tf_op jit(solution)/shard_map/ppermute | solution.py:497
  22.9 1.9 %collective-permute-start = (f32[3,2,1280]{2,1,0:T(2,128)S(1)}, f32[3,2,1280]{2,1,0:T(2,128)S(1)}, u32[]{:S(2)}, u32[]{:S(2)}) collective-permute-start(f32[3,2,1280]{2,1,0:T(2,128)S(1)} %get-tuple-element.9), channel_id=1, source_target_pairs={{0,16},{16,0},{32,48},{48,32},{64,80},{80,64},{96,112},{112,96},{1... | collective-permute-start | bytes 92168 | tf_op jit(solution)/shard_map/ppermute | solution.py:495
  24.8 5.7 %tables.1 = (bf16[3,512,1280]{2,1,0:T(8,128)(2,1)}, f32[512,128]{1,0:T(8,128)}, f32[512,128]{1,0:T(8,128)}) custom-call(s32[640]{0:T(1024)} %assign_ref.1), custom_call_target="tpu_custom_call" | custom-call | flops 10000000 | bytes 1000000 | tf_op jit(solution)/shard_map/tables/pallas_call | solution.py:135
  30.5 2.8 %collective-permute-done.1.far_ref = f32[3,2,1280]{2,1,0:T(2,128)S(1)} collective-permute-done((f32[3,2,1280]{2,1,0:T(2,128)S(1)}, f32[3,2,1280]{2,1,0:T(2,128)S(1)}, u32[]{:S(2)}, u32[]{:S(2)}) %collective-permute-start.1) | collective-permute-done | bytes 30752 | tf_op jit(solution)/shard_map/ppermute | solution.py:497
  33.2 0.0 copy-start.3
  33.2 0.0 collective-permute-done.near_ref
  33.2 0.0 copy-start.4
  33.2 0.6 copy-done.3
  33.8 0.0 copy-done.4
  33.9 6.4 %shard_map.95 = f32[512,128]{1,0:T(8,128)} custom-call(s32[1]{0:T(128)} %bitcast.1.side_ref, f32[7,7]{1,0:T(8,128)} %stencil_ref.1, f32[20,2,1280]{2,1,0:T(2,128)} %bitcast.33, f32[3,2,1280]{2,1,0:T(2,128)} %copy-done.4, f32[3,2,1280]{2,1,0:T(2,128)} %copy-done.3, s32[20,2,1280]{2,1,0:T(2,128)} %bitcast.35, bf16[3,512,1280]{2,1,0:T(8,128)(2,1)} %get-tuple-element.5.t_any, ...), custom_call_target="tpu_custom_call" | custom-call | flops 1000000000 | bytes 1000000 | tf_op jit(solution)/shard_map/pallas_call | solution.py:231
  40.3 0.0 all-to-all-done.1
  40.3 15.7 %all-to-all-start = ((f32[512,1,128]{2,1,0:T(1,128)}), f32[512,1,128]{2,1,0:T(1,128)S(1)}, u32[]{:S(2)}, u32[]{:S(2)}) async-start(f32[512,1,128]{2,1,0:T(1,128)} %bitcast.28), calls=%async_computation | async-start | bytes 524288 | tf_op jit(solution)/shard_map/all_to_all | solution.py:487
  56.0 0.0 copy-done.6
  56.0 0.7 copy.25.damping_ref
  56.7 0.0 copy-done.5
  56.7 0.1 copy.21
  56.8 0.1 copy.23
  56.9 0.0 copy-done.2
  56.9 0.1 broadcast_multiply_fusion
  57.0 0.7 mul.82.vecp_ref
  57.7 0.7 mul.78.vec_ref
  58.4 0.7 mul.75.inv_ref
  59.1 1.4 %fusion = (s32[1]{0:T(128)}, s32[1]{0:T(128)}) fusion(s32[640]{0:T(1024)} %assign_ref.1, s32[]{:T(128)S(6)} %dynamic_slice.17, s32[]{:T(128)S(6)} %dynamic_slice.19), kind=kLoop, calls=%fused_computation.7 | loop fusion | bytes 24 | tf_op jit(solution)/shard_map/dynamic_slice | solution.py:506
  60.5 1.9 %pad_add_fusion.info_ref = s32[3]{0:T(128)} fusion(s32[1]{0:T(128)} %bitcast, s32[1]{0:T(128)} %get-tuple-element.11, s32[1]{0:T(128)} %get-tuple-element.10), kind=kLoop, calls=%fused_computation.6 | loop fusion | flops 6 | bytes 24 | tf_op jit(solution)/shard_map/stack | solution.py:506
  62.4 0.3 slice.8
  62.8 1.2 reshape.68.own_ref
  63.9 0.2 slice.9
  64.1 0.9 reshape.69.shared_ref
  65.0 8.2 %all-to-all-done = f32[512,1,128]{2,1,0:T(1,128)S(1)} async-done(((f32[512,1,128]{2,1,0:T(1,128)}), f32[512,1,128]{2,1,0:T(1,128)S(1)}, u32[]{:S(2)}, u32[]{:S(2)}) %all-to-all-start) | async-done | bytes 262176 | tf_op jit(solution)/shard_map/all_to_all | solution.py:487
  73.2 0.0 copy-start.1
  73.2 0.7 copy-done.1
  73.9 4.4 %shard_map.96 = bf16[16,56,128]{2,1,0:T(8,128)(2,1)} custom-call(s32[3]{0:T(128)} %pad_add_fusion.info_ref, f32[512,128]{1,0:T(8,128)} %bitcast.34, bf16[640,320]{1,0:T(8,128)(2,1)} %reshape.68.own_ref, bf16[320,320]{1,0:T(8,128)(2,1)} %reshape.69.shared_ref, f32[32,1]{1,0:T(8,128)} %copy.25.damping_ref, f32[64,64]{1,0:T(8,128)} %mul.75.inv_ref, ...), custom_call_target="tpu_custom_call" | custom-call | flops 1000000000 | bytes 1000000 | tf_op jit(solution)/shard_map/pallas_call | solution.py:353
  78.3 13.2 %all_to_all.20.wide_ref.spec_ref = bf16[16,56,128]{2,1,0:T(8,128)(2,1)} all-to-all(bf16[16,56,128]{2,1,0:T(8,128)(2,1)} %shard_map.96), channel_id=1, replica_groups=mesh['lat'=32,'lev'=16] {'lev'}, dimensions={0} | all-to-all | bytes 458752 | tf_op jit(solution)/shard_map/all_to_all | solution.py:487
  91.6 2.2 %shard_map.97 = bf16[512,128]{1,0:T(8,128)(2,1)} custom-call(bf16[16,56,128]{2,1,0:T(8,128)(2,1)} %all_to_all.20.wide_ref.spec_ref), custom_call_target="tpu_custom_call" | custom-call | flops 10000000 | bytes 1000000 | tf_op jit(solution)/shard_map/pallas_call | solution.py:390
  93.8 9.6 %all-to-all-start.3 = ((bf16[32,16,128]{2,1,0:T(8,128)(2,1)}), bf16[32,16,128]{2,1,0:T(8,128)(2,1)S(1)}, u32[]{:S(2)}, u32[]{:S(2)}) async-start(bf16[32,16,128]{2,1,0:T(8,128)(2,1)} %bitcast.31), calls=%async_computation.3 | async-start | bytes 262144 | tf_op jit(solution)/shard_map/all_to_all | solution.py:487
  103.4 1.8 %shard_map.99 = f32[20,40,64]{2,1,0:T(8,128)} custom-call(bf16[16,56,128]{2,1,0:T(8,128)(2,1)} %all_to_all.20.wide_ref.spec_ref), custom_call_target="tpu_custom_call" | custom-call | flops 1000000 | bytes 1000000 | tf_op jit(solution)/shard_map/pallas_call | solution.py:444
  105.2 11.3 %all-to-all-done.3 = bf16[32,16,128]{2,1,0:T(8,128)(2,1)S(1)} async-done(((bf16[32,16,128]{2,1,0:T(8,128)(2,1)}), bf16[32,16,128]{2,1,0:T(8,128)(2,1)S(1)}, u32[]{:S(2)}, u32[]{:S(2)}) %all-to-all-start.3) | async-done | bytes 131104 | tf_op jit(solution)/shard_map/all_to_all | solution.py:487
  116.5 0.0 copy-start
  116.5 0.6 copy-done
  117.2 3.8 %shard_map.98 = f32[20,2,1280]{2,1,0:T(2,128)} custom-call(bf16[512,128]{1,0:T(8,128)(2,1)} %bitcast.30, bf16[3,512,1280]{2,1,0:T(8,128)(2,1)} %get-tuple-element.5.t_any, f32[512,128]{1,0:T(8,128)} %get-tuple-element.6.even_ref, f32[512,128]{1,0:T(8,128)} %get-tuple-element.7.weight_ref), custom_call_target="tpu_custom_call" | custom-call | flops 100000000 | bytes 1000000 | tf_op jit(solution)/shard_map/pallas_call | solution.py:423
  (3 shorter events, 0.0 us)
Async XLA Ops:
  0.6 55.4 %copy-start.6 = (f32[32]{0:T(128)S(1)}, f32[32]{0:T(128)}, u32[]{:S(2)}) copy-start(f32[32]{0:T(128)} %param.13) | copy-start | bytes 388
  0.6 56.1 %copy-start.5 = (f32[32,32]{1,0:T(8,128)S(1)}, f32[32,32]{1,0:T(8,128)}, u32[]{:S(2)}) copy-start(f32[32,32]{1,0:T(8,128)} %param.15) | copy-start | bytes 12292
  2.9 54.0 %copy-start.2 = (f32[32,32]{1,0:T(8,128)S(1)}, f32[32,32]{1,0:T(8,128)}, u32[]{:S(2)}) copy-start(f32[32,32]{1,0:T(8,128)} %param.14) | copy-start | bytes 12292
  2.9 37.4 %all-to-all-start.1 = ((bf16[16,30,2,320]{3,2,1,0:T(2,128)(2,1)}), bf16[16,30,2,320]{3,2,1,0:T(2,128)(2,1)S(1)}, u32[]{:S(2)}, u32[]{:S(2)}) async-start(bf16[16,30,2,320]{3,2,1,0:T(2,128)(2,1)} %send_tables.1), calls=%async_computation.1 | async-start | bytes 1474560 | tf_op jit(solution)/shard_map/all_to_all | solution.py:487
  14.1 19.1 %collective-permute-start.1 = (f32[3,2,1280]{2,1,0:T(2,128)S(1)}, f32[3,2,1280]{2,1,0:T(2,128)S(1)}, u32[]{:S(2)}, u32[]{:S(2)}) collective-permute-start(f32[3,2,1280]{2,1,0:T(2,128)S(1)} %get-tuple-element.8), channel_id=1, source_target_pairs={{16,32},{32,16},{48,64},{64,48},{80,96},{96,80},{112,128},{128,112... | collective-permute-start | bytes 92168 | tf_op jit(solution)/shard_map/ppermute | solution.py:497
  22.9 10.4 %collective-permute-start = (f32[3,2,1280]{2,1,0:T(2,128)S(1)}, f32[3,2,1280]{2,1,0:T(2,128)S(1)}, u32[]{:S(2)}, u32[]{:S(2)}) collective-permute-start(f32[3,2,1280]{2,1,0:T(2,128)S(1)} %get-tuple-element.9), channel_id=1, source_target_pairs={{0,16},{16,0},{32,48},{48,32},{64,80},{80,64},{96,112},{112,96},{1... | collective-permute-start | bytes 92168 | tf_op jit(solution)/shard_map/ppermute | solution.py:495
  33.2 0.6 copy-start.3
  33.2 0.6 copy-start.4
  40.3 32.9 %all-to-all-start = ((f32[512,1,128]{2,1,0:T(1,128)}), f32[512,1,128]{2,1,0:T(1,128)S(1)}, u32[]{:S(2)}, u32[]{:S(2)}) async-start(f32[512,1,128]{2,1,0:T(1,128)} %bitcast.28), calls=%async_computation | async-start | bytes 524288 | tf_op jit(solution)/shard_map/all_to_all | solution.py:487
  73.2 0.7 copy-start.1
  93.8 22.7 %all-to-all-start.3 = ((bf16[32,16,128]{2,1,0:T(8,128)(2,1)}), bf16[32,16,128]{2,1,0:T(8,128)(2,1)S(1)}, u32[]{:S(2)}, u32[]{:S(2)}) async-start(bf16[32,16,128]{2,1,0:T(8,128)(2,1)} %bitcast.31), calls=%async_computation.3 | async-start | bytes 262144 | tf_op jit(solution)/shard_map/all_to_all | solution.py:487
  116.5 0.6 copy-start

commit v6 on v5

--- a/solution.py
+++ b/solution.py
@@ -401,15 +401,18 @@
 
 
 def inverse_kernel(msg_ref, t_any, even_ref, weight_ref, out_ref, t_ref, t_sem):
-    fetch = pltpu.make_async_copy(t_any.at[:, :, pl.ds(0, HALF_LON)], t_ref, t_sem)
-    fetch.start()
+    fetches = [
+        pltpu.make_async_copy(t_any.at[j, :, pl.ds(0, HALF_LON)], t_ref.at[j], t_sem.at[j]) for j in range(3)
+    ]
+    for fetch in fetches:
+        fetch.start()
     lane = lax.broadcasted_iota(jnp.int32, (N_DEV, 128), 1)
     scaled = jnp.where(lane < 3 * MSG, msg_ref[...].astype(F32) * weight_ref[...], 0.0)
     even = (scaled * even_ref[...]).T
     odd = (scaled * (1.0 - even_ref[...])).T
     total = jnp.zeros((2 * MSG, HALF_LON), F32)
-    fetch.wait()
     for j in range(3):
+        fetches[j].wait()
         left = jnp.concatenate([even[MSG * j : MSG * (j + 1)], odd[MSG * j : MSG * (j + 1)]], axis=0).astype(BF16)
         total = total + lax.dot_general(left, t_ref[j], NN, preferred_element_type=F32)
     near = total[:MSG] + total[MSG:]
@@ -424,7 +427,7 @@
         inverse_kernel,
         jax.ShapeDtypeStruct((ROWS, LV, NLON), F32),
         [VM, ANY, VM, VM],
-        [pltpu.VMEM((3, N_DEV, HALF_LON), BF16), pltpu.SemaphoreType.DMA],
+        [pltpu.VMEM((3, N_DEV, HALF_LON), BF16), pltpu.SemaphoreType.DMA((3,))],
         10**8,
     )(msgs, table, even, weight)
 

time: 122 us -> 122 us (level)
  no operation moved by 1% of the time
where the time goes in v6:
time: 122 us; the launch traced here: 121 us
  starting transfers between devices  46.3 us (38%)
  Pallas kernels  26.5 us (22%)
  waiting for transfers between devices  22.3 us (18%)
  blocking collectives  13.2 us (11%)
  local copies, waits for them, and re-layouts  9.73 us (8%)
  other arithmetic  2 us (2%)
    all_to_all x3, starting transfers between devices, exchange(): return lax.all_to_all(value, axes, split_axis=0, concat_axis=0, tiled=True)  35.7 us
    all_to_all x3, waiting for transfers between devices, exchange(): return lax.all_to_all(value, axes, split_axis=0, concat_axis=0, tiled=True)  19.5 us
    all_to_all x1, blocking collectives, exchange(): return lax.all_to_all(value, axes, split_axis=0, concat_axis=0, tiled=True)  13.2 us
    ppermute x1, starting transfers between devices, step_of(): lax.ppermute(far, 'lat', [(i, i + 2 * (i & 1) - 1) for i in range(1, N_LA...  8.77 us
    pallas_call x1, Pallas kernels, forward(): call(forward_kernel, jax.ShapeDtypeStruct((N_DEV, 128), F32), [SM, SM, VM...  6.43 us
    pallas_call x1, Pallas kernels, tables(): pl.pallas_call(tables_kernel, out_shape=(jax.ShapeDtypeStruct((3, N_DEV,...  5.66 us
    pallas_call x1, Pallas kernels, spectral(): call(spectral_kernel, jax.ShapeDtypeStruct((N_LEV, WIDE, 128), BF16), [SM...  4.43 us
    pallas_call x1, Pallas kernels, inverse(): call(inverse_kernel, jax.ShapeDtypeStruct((ROWS, LV, NLON), F32), [VM, AN...  3.71 us
  transfers between devices with their start and end apart: 5, of which 3 were waited for; matrix products, arithmetic and copies ran while one was open for 8% of the time, Pallas kernels for 12%

profile of v6, /device:TPU:1, one launch (start us, length us, event | category | flops | bytes accessed | tf_op | source)
XLA Modules:
  0.0 120.9 jit_solution(11323038185354247559)
XLA Ops:
  0.6 0.0 copy-start.6
  0.6 0.0 copy-start.5
  0.7 2.2 %send_tables.1 = bf16[16,30,2,320]{3,2,1,0:T(2,128)(2,1)} custom-call(bf16[20,20,2,320]{3,2,1,0:T(2,128)(2,1)} %bitcast.29), custom_call_target="tpu_custom_call" | custom-call | flops 1000000 | bytes 2000000 | tf_op jit(solution)/shard_map/send_tables/pallas_call | solution.py:473
  2.9 0.0 copy-start.2
  2.9 10.4 %all-to-all-start.1 = ((bf16[16,30,2,320]{3,2,1,0:T(2,128)(2,1)}), bf16[16,30,2,320]{3,2,1,0:T(2,128)(2,1)S(1)}, u32[]{:S(2)}, u32[]{:S(2)}) async-start(bf16[16,30,2,320]{3,2,1,0:T(2,128)(2,1)} %send_tables.1), calls=%async_computation.1 | async-start | bytes 1474560 | tf_op jit(solution)/shard_map/all_to_all | solution.py:490
  13.3 0.8 dynamic-slice_bitcast_fusion
  14.1 8.8 %collective-permute-start.1 = (f32[3,2,1280]{2,1,0:T(2,128)S(1)}, f32[3,2,1280]{2,1,0:T(2,128)S(1)}, u32[]{:S(2)}, u32[]{:S(2)}) collective-permute-start(f32[3,2,1280]{2,1,0:T(2,128)S(1)} %get-tuple-element.8), channel_id=1, source_target_pairs={{16,32},{32,16},{48,64},{64,48},{80,96},{96,80},{112,128},{128,112... | collective-permute-start | bytes 92168 | tf_op jit(solution)/shard_map/ppermute | solution.py:500
  22.9 1.9 %collective-permute-start = (f32[3,2,1280]{2,1,0:T(2,128)S(1)}, f32[3,2,1280]{2,1,0:T(2,128)S(1)}, u32[]{:S(2)}, u32[]{:S(2)}) collective-permute-start(f32[3,2,1280]{2,1,0:T(2,128)S(1)} %get-tuple-element.9), channel_id=1, source_target_pairs={{0,16},{16,0},{32,48},{48,32},{64,80},{80,64},{96,112},{112,96},{1... | collective-permute-start | bytes 92168 | tf_op jit(solution)/shard_map/ppermute | solution.py:498
  24.8 5.7 %tables.1 = (bf16[3,512,1280]{2,1,0:T(8,128)(2,1)}, f32[512,128]{1,0:T(8,128)}, f32[512,128]{1,0:T(8,128)}) custom-call(s32[640]{0:T(1024)} %assign_ref.1), custom_call_target="tpu_custom_call" | custom-call | flops 10000000 | bytes 1000000 | tf_op jit(solution)/shard_map/tables/pallas_call | solution.py:135
  30.5 2.8 %collective-permute-done.1.far_ref = f32[3,2,1280]{2,1,0:T(2,128)S(1)} collective-permute-done((f32[3,2,1280]{2,1,0:T(2,128)S(1)}, f32[3,2,1280]{2,1,0:T(2,128)S(1)}, u32[]{:S(2)}, u32[]{:S(2)}) %collective-permute-start.1) | collective-permute-done | bytes 30752 | tf_op jit(solution)/shard_map/ppermute | solution.py:500
  33.2 0.0 copy-start.3
  33.2 0.0 collective-permute-done.near_ref
  33.2 0.0 copy-start.4
  33.2 0.6 copy-done.3
  33.8 0.0 copy-done.4
  33.9 6.4 %shard_map.95 = f32[512,128]{1,0:T(8,128)} custom-call(s32[1]{0:T(128)} %bitcast.1.side_ref, f32[7,7]{1,0:T(8,128)} %stencil_ref.1, f32[20,2,1280]{2,1,0:T(2,128)} %bitcast.33, f32[3,2,1280]{2,1,0:T(2,128)} %copy-done.4, f32[3,2,1280]{2,1,0:T(2,128)} %copy-done.3, s32[20,2,1280]{2,1,0:T(2,128)} %bitcast.35, bf16[3,512,1280]{2,1,0:T(8,128)(2,1)} %get-tuple-element.5.t_any, ...), custom_call_target="tpu_custom_call" | custom-call | flops 1000000000 | bytes 1000000 | tf_op jit(solution)/shard_map/pallas_call | solution.py:231
  40.3 0.0 all-to-all-done.1
  40.3 15.7 %all-to-all-start = ((f32[512,1,128]{2,1,0:T(1,128)}), f32[512,1,128]{2,1,0:T(1,128)S(1)}, u32[]{:S(2)}, u32[]{:S(2)}) async-start(f32[512,1,128]{2,1,0:T(1,128)} %bitcast.28), calls=%async_computation | async-start | bytes 524288 | tf_op jit(solution)/shard_map/all_to_all | solution.py:490
  56.0 0.0 copy-done.6
  56.0 0.7 copy.25.damping_ref
  56.7 0.0 copy-done.5
  56.7 0.1 copy.21
  56.8 0.1 copy.23
  56.9 0.0 copy-done.2
  56.9 0.1 broadcast_multiply_fusion
  57.0 0.7 mul.82.vecp_ref
  57.7 0.7 mul.78.vec_ref
  58.4 0.7 mul.75.inv_ref
  59.1 1.4 %fusion = (s32[1]{0:T(128)}, s32[1]{0:T(128)}) fusion(s32[640]{0:T(1024)} %assign_ref.1, s32[]{:T(128)S(6)} %dynamic_slice.17, s32[]{:T(128)S(6)} %dynamic_slice.19), kind=kLoop, calls=%fused_computation.7 | loop fusion | bytes 24 | tf_op jit(solution)/shard_map/dynamic_slice | solution.py:509
  60.5 1.9 %pad_add_fusion.info_ref = s32[3]{0:T(128)} fusion(s32[1]{0:T(128)} %bitcast, s32[1]{0:T(128)} %get-tuple-element.11, s32[1]{0:T(128)} %get-tuple-element.10), kind=kLoop, calls=%fused_computation.6 | loop fusion | flops 6 | bytes 24 | tf_op jit(solution)/shard_map/stack | solution.py:509
  62.4 0.3 slice.8
  62.8 1.2 reshape.68.own_ref
  63.9 0.2 slice.9
  64.1 0.9 reshape.69.shared_ref
  65.0 8.2 %all-to-all-done = f32[512,1,128]{2,1,0:T(1,128)S(1)} async-done(((f32[512,1,128]{2,1,0:T(1,128)}), f32[512,1,128]{2,1,0:T(1,128)S(1)}, u32[]{:S(2)}, u32[]{:S(2)}) %all-to-all-start) | async-done | bytes 262176 | tf_op jit(solution)/shard_map/all_to_all | solution.py:490
  73.2 0.0 copy-start.1
  73.2 0.7 copy-done.1
  73.9 4.4 %shard_map.96 = bf16[16,56,128]{2,1,0:T(8,128)(2,1)} custom-call(s32[3]{0:T(128)} %pad_add_fusion.info_ref, f32[512,128]{1,0:T(8,128)} %bitcast.34, bf16[640,320]{1,0:T(8,128)(2,1)} %reshape.68.own_ref, bf16[320,320]{1,0:T(8,128)(2,1)} %reshape.69.shared_ref, f32[32,1]{1,0:T(8,128)} %copy.25.damping_ref, f32[64,64]{1,0:T(8,128)} %mul.75.inv_ref, ...), custom_call_target="tpu_custom_call" | custom-call | flops 1000000000 | bytes 1000000 | tf_op jit(solution)/shard_map/pallas_call | solution.py:353
  78.3 13.2 %all_to_all.20.wide_ref.spec_ref = bf16[16,56,128]{2,1,0:T(8,128)(2,1)} all-to-all(bf16[16,56,128]{2,1,0:T(8,128)(2,1)} %shard_map.96), channel_id=1, replica_groups=mesh['lat'=32,'lev'=16] {'lev'}, dimensions={0} | all-to-all | bytes 458752 | tf_op jit(solution)/shard_map/all_to_all | solution.py:490
  91.6 2.2 %shard_map.97 = bf16[512,128]{1,0:T(8,128)(2,1)} custom-call(bf16[16,56,128]{2,1,0:T(8,128)(2,1)} %all_to_all.20.wide_ref.spec_ref), custom_call_target="tpu_custom_call" | custom-call | flops 10000000 | bytes 1000000 | tf_op jit(solution)/shard_map/pallas_call | solution.py:390
  93.8 9.6 %all-to-all-start.3 = ((bf16[32,16,128]{2,1,0:T(8,128)(2,1)}), bf16[32,16,128]{2,1,0:T(8,128)(2,1)S(1)}, u32[]{:S(2)}, u32[]{:S(2)}) async-start(bf16[32,16,128]{2,1,0:T(8,128)(2,1)} %bitcast.31), calls=%async_computation.3 | async-start | bytes 262144 | tf_op jit(solution)/shard_map/all_to_all | solution.py:490
  103.4 1.8 %shard_map.99 = f32[20,40,64]{2,1,0:T(8,128)} custom-call(bf16[16,56,128]{2,1,0:T(8,128)(2,1)} %all_to_all.20.wide_ref.spec_ref), custom_call_target="tpu_custom_call" | custom-call | flops 1000000 | bytes 1000000 | tf_op jit(solution)/shard_map/pallas_call | solution.py:447
  105.2 11.3 %all-to-all-done.3 = bf16[32,16,128]{2,1,0:T(8,128)(2,1)S(1)} async-done(((bf16[32,16,128]{2,1,0:T(8,128)(2,1)}), bf16[32,16,128]{2,1,0:T(8,128)(2,1)S(1)}, u32[]{:S(2)}, u32[]{:S(2)}) %all-to-all-start.3) | async-done | bytes 131104 | tf_op jit(solution)/shard_map/all_to_all | solution.py:490
  116.5 0.0 copy-start
  116.5 0.6 copy-done
  117.2 3.7 %shard_map.98 = f32[20,2,1280]{2,1,0:T(2,128)} custom-call(bf16[512,128]{1,0:T(8,128)(2,1)} %bitcast.30, bf16[3,512,1280]{2,1,0:T(8,128)(2,1)} %get-tuple-element.5.t_any, f32[512,128]{1,0:T(8,128)} %get-tuple-element.6.even_ref, f32[512,128]{1,0:T(8,128)} %get-tuple-element.7.weight_ref), custom_call_target="tpu_custom_call" | custom-call | flops 100000000 | bytes 1000000 | tf_op jit(solution)/shard_map/pallas_call | solution.py:426
  (3 shorter events, 0.0 us)
Async XLA Ops:
  0.6 55.4 %copy-start.6 = (f32[32]{0:T(128)S(1)}, f32[32]{0:T(128)}, u32[]{:S(2)}) copy-start(f32[32]{0:T(128)} %param.13) | copy-start | bytes 388
  0.6 56.1 %copy-start.5 = (f32[32,32]{1,0:T(8,128)S(1)}, f32[32,32]{1,0:T(8,128)}, u32[]{:S(2)}) copy-start(f32[32,32]{1,0:T(8,128)} %param.15) | copy-start | bytes 12292
  2.9 54.0 %copy-start.2 = (f32[32,32]{1,0:T(8,128)S(1)}, f32[32,32]{1,0:T(8,128)}, u32[]{:S(2)}) copy-start(f32[32,32]{1,0:T(8,128)} %param.14) | copy-start | bytes 12292
  2.9 37.4 %all-to-all-start.1 = ((bf16[16,30,2,320]{3,2,1,0:T(2,128)(2,1)}), bf16[16,30,2,320]{3,2,1,0:T(2,128)(2,1)S(1)}, u32[]{:S(2)}, u32[]{:S(2)}) async-start(bf16[16,30,2,320]{3,2,1,0:T(2,128)(2,1)} %send_tables.1), calls=%async_computation.1 | async-start | bytes 1474560 | tf_op jit(solution)/shard_map/all_to_all | solution.py:490
  14.1 19.1 %collective-permute-start.1 = (f32[3,2,1280]{2,1,0:T(2,128)S(1)}, f32[3,2,1280]{2,1,0:T(2,128)S(1)}, u32[]{:S(2)}, u32[]{:S(2)}) collective-permute-start(f32[3,2,1280]{2,1,0:T(2,128)S(1)} %get-tuple-element.8), channel_id=1, source_target_pairs={{16,32},{32,16},{48,64},{64,48},{80,96},{96,80},{112,128},{128,112... | collective-permute-start | bytes 92168 | tf_op jit(solution)/shard_map/ppermute | solution.py:500
  22.9 10.4 %collective-permute-start = (f32[3,2,1280]{2,1,0:T(2,128)S(1)}, f32[3,2,1280]{2,1,0:T(2,128)S(1)}, u32[]{:S(2)}, u32[]{:S(2)}) collective-permute-start(f32[3,2,1280]{2,1,0:T(2,128)S(1)} %get-tuple-element.9), channel_id=1, source_target_pairs={{0,16},{16,0},{32,48},{48,32},{64,80},{80,64},{96,112},{112,96},{1... | collective-permute-start | bytes 92168 | tf_op jit(solution)/shard_map/ppermute | solution.py:498
  33.2 0.6 copy-start.3
  33.2 0.6 copy-start.4
  40.3 32.9 %all-to-all-start = ((f32[512,1,128]{2,1,0:T(1,128)}), f32[512,1,128]{2,1,0:T(1,128)S(1)}, u32[]{:S(2)}, u32[]{:S(2)}) async-start(f32[512,1,128]{2,1,0:T(1,128)} %bitcast.28), calls=%async_computation | async-start | bytes 524288 | tf_op jit(solution)/shard_map/all_to_all | solution.py:490
  73.2 0.7 copy-start.1
  93.8 22.7 %all-to-all-start.3 = ((bf16[32,16,128]{2,1,0:T(8,128)(2,1)}), bf16[32,16,128]{2,1,0:T(8,128)(2,1)S(1)}, u32[]{:S(2)}, u32[]{:S(2)}) async-start(bf16[32,16,128]{2,1,0:T(8,128)(2,1)} %bitcast.31), calls=%async_computation.3 | async-start | bytes 262144 | tf_op jit(solution)/shard_map/all_to_all | solution.py:490
  116.5 0.6 copy-start

commit v7 on v6

--- a/solution.py
+++ b/solution.py
@@ -15,6 +15,7 @@
 NLON, HALF_LON = 1280, 640
 ROWS = 20
 LV = 2
+NLEV = 32
 QB = 40
 QP = N_LEV * QB
 HL = 320
@@ -258,14 +259,15 @@
 
 
 def spectral_kernel(
-    info_ref,
+    lat_ref,
+    lev_ref,
+    assign_ref,
     msg_ref,
     own_ref,
     shared_ref,
     damping_ref,
-    inv_ref,
-    vec_ref,
-    vecp_ref,
+    inv_in,
+    vec_in,
     out_ref,
     nbuf,
     sbuf,
@@ -284,10 +286,30 @@
                 lane = MSG * j + ROWS * k
                 nbuf[j, 16 * k : 16 * k + 16, ROWS * a : ROWS * a + ROWS] = top[:, lane : lane + ROWS]
                 sbuf[j, 16 * k : 16 * k + 16, ROWS * a : ROWS * a + ROWS] = low[:, lane : lane + ROWS]
-    damp = damping_ref[...]
 
     def exact(left, right):
         return lax.dot_general(left, right, NN, precision=HIGH, preferred_element_type=F32)
+
+    lev = lev_ref[0]
+    base = lat_ref[0] * SLOTS
+    own_wave = assign_ref[base + own_slot(lev)]
+    shared_wave = assign_ref[base + shared_slot(lev)]
+    row = lax.broadcasted_iota(jnp.int32, (NLEV, NLEV), 0)
+    column = lax.broadcasted_iota(jnp.int32, (NLEV, NLEV), 1)
+    damp = jnp.sum(jnp.where(row == column, damping_ref[...].reshape(1, NLEV), 0.0), axis=1, keepdims=True)
+    levels = (row == 2 * (column & 15) + (column >> 4)).astype(F32)
+    places = (column == 2 * (row & 15) + (row >> 4)).astype(F32)
+    inv_one = exact(inv_in[...], levels)
+    vec_one = vec_in[...]
+    vecp_one = exact(places, vec_one)
+
+    def blocks(matrix, count):
+        if count == 1:
+            return matrix
+        zero = jnp.zeros_like(matrix)
+        return jnp.concatenate(
+            [jnp.concatenate([matrix, zero], axis=1), jnp.concatenate([zero, matrix], axis=1)], axis=0
+        )
 
     def solve(units, matrix, degree, odd):
         count = len(units)
@@ -303,12 +325,11 @@
             ],
             axis=0,
         )
-        size = 32 * count
         n = degree.astype(F32)
         denominator = 1.0 + (n * (n + 1.0) / float(M * M)) * damp
-        modal = exact(inv_ref[:size, :size], forcing)
+        modal = exact(blocks(inv_one, count), forcing)
         modal = jnp.concatenate([modal[32 * u : 32 * u + 32] / denominator for u in range(count)], axis=0)
-        packed = exact(vecp_ref[:size, :size], modal)
+        packed = exact(blocks(vecp_one, count), modal)
         left = jnp.concatenate(
             [
                 part
@@ -325,13 +346,13 @@
             lats = jnp.concatenate([back[64 * u : 64 * u + 32], back[64 * u + 32 : 64 * u + 64]], axis=1)
             for tile in range(5):
                 zonal[tile, 32 * j : 32 * j + 32, :] = lats[:, 128 * tile : 128 * tile + 128]
-        return exact(vec_ref[:size, :size], modal).T
+        return exact(blocks(vec_one, count), modal).T
 
     lane = lax.broadcasted_iota(jnp.int32, (32, QP), 1)
-    whole = solve((0, 1), own_ref[...], lane + info_ref[0], (lane & 1) == 1)
+    whole = solve((0, 1), own_ref[...], lane + own_wave, (lane & 1) == 1)
     lane = lax.broadcasted_iota(jnp.int32, (32, QP // 2), 1)
     block = jnp.floor((lane.astype(F32) + 0.5) * (1.0 / 20.0)).astype(jnp.int32)
-    part = solve((2,), shared_ref[...], lane + 20 * block + 20 * info_ref[2] + info_ref[1], (lane & 1) == 1)
+    part = solve((2,), shared_ref[...], lane + 20 * block + 20 * (lev & 1) + shared_wave, (lane & 1) == 1)
     for b in range(N_LEV):
         wide[b, 0:20, 0:64] = whole[QB * b : QB * b + 20]
         wide[b, 0:20, 64:128] = whole[QB * b + 20 : QB * b + 40]
@@ -349,11 +370,11 @@
     return ref[tile, pl.ds(start, count, stride), :]
 
 
-def spectral(info, msgs, own, shared, damping, inv, vec, vecp):
+def spectral(lat, lev, assign, msgs, own, shared, damping, inv, vec):
     return call(
         spectral_kernel,
         jax.ShapeDtypeStruct((N_LEV, WIDE, 128), BF16),
-        [SM, VM, VM, VM, VM, VM, VM, VM],
+        [SM, SM, SM, VM, VM, VM, VM, VM, VM],
         [
             pltpu.VMEM((3, 32, HL), F32),
             pltpu.VMEM((3, 32, HL), F32),
@@ -362,7 +383,7 @@
             pltpu.VMEM((N_LEV, WIDE, 128), F32),
         ],
         10**9,
-    )(info, msgs, own, shared, damping, inv, vec, vecp)
+    )(lat, lev, assign, msgs, own, shared, damping, inv, vec)
 
 
 def bands_kernel(wide_ref, out_ref, rows, out, flip):
@@ -447,16 +468,6 @@
     return call(place_kernel, jax.ShapeDtypeStruct((SLOTS, QB, 64), F32), [VM], [], 10**6)(spec)
 
 
-def by_block(matrix):
-    return jnp.kron(jnp.eye(2, dtype=F32), matrix)
-
-
-def level_order(value, axis):
-    shape = value.shape
-    split = shape[:axis] + (16, 2) + shape[axis + 1 :]
-    return jnp.swapaxes(value.reshape(split), axis, axis + 1).reshape(shape)
-
-
 def send_kernel(table_ref, out_ref, sems):
     copies = []
     for b in range(N_LEV):
@@ -505,17 +516,16 @@
     msgs = forward(side.reshape(1), stencil, rows, near, far, jnp.swapaxes(offsets, 0, 1), table, even)
     got = exchange(msgs.reshape(N_DEV, 1, 128), ("lat", "lev")).reshape(N_DEV, 128)
     lev = lax.axis_index("lev")
-    mine = lax.dynamic_slice_in_dim(assign, lat * SLOTS, SLOTS)
-    info = jnp.stack([mine[own_slot(lev)], mine[shared_slot(lev)], lev & 1]).astype(jnp.int32)
     solved = spectral(
-        info,
+        lat.astype(jnp.int32).reshape(1),
+        lev.astype(jnp.int32).reshape(1),
+        assign,
         got,
         own,
         shared,
-        damping.reshape(32, 1),
-        by_block(level_order(vert_inv, 1)),
-        by_block(vert_vecs),
-        by_block(level_order(vert_vecs, 0)),
+        damping,
+        vert_inv,
+        vert_vecs,
     )
     solved = exchange(solved, "lev")
     home = exchange(bands(solved).reshape(N_LAT, N_LEV, 128), "lat").reshape(N_DEV, 128)

time: 122 us -> 118 us (0.967)
  waiting for transfers between devices: 22.3 us -> 28.6 us
  local copies, waits for them, and re-layouts: 9.73 us -> 5.36 us
  starting transfers between devices: 46.3 us -> 42.9 us
  other arithmetic: 2 us -> 0 us
    all_to_all x3, waiting for transfers between devices: 19.5 us -> 25.9 us  [exchange(): return lax.all_to_all(value, axes, split_axis=0, concat_axis=0, tiled=True)]
    all_to_all x3, starting transfers between devices: 35.7 us -> 32.2 us  [exchange(): return lax.all_to_all(value, axes, split_axis=0, concat_axis=0, tiled=True)]
    mul x4 -> x0, local copies, waits for them, and re-layouts: 2.2 us -> none  [by_block(): return jnp.kron(jnp.eye(2, dtype=F32), matrix)]
    another operation x1 -> x0, other arithmetic: 1.87 us -> none  [step_of(): jnp.stack([mine[own_slot(lev)], mine[shared_slot(lev)], lev & 1])]
    dynamic_slice x1 -> x0, local copies, waits for them, and re-layouts: 1.41 us -> none  [step_of(): mine[own_slot(lev)]]
  transfers between devices with their start and end apart: 5 -> 5, of which waited for: 3 -> 3; matrix products, arithmetic and copies ran while one was open for 8% -> 3% of each run, Pallas kernels for 12% -> 12%
where the time goes in v7:
time: 118 us; the launch traced here: 117 us
  starting transfers between devices  42.9 us (36%)
  waiting for transfers between devices  28.6 us (24%)
  Pallas kernels  26.6 us (23%)
  blocking collectives  13.2 us (11%)
  local copies, waits for them, and re-layouts  5.36 us (5%)
    all_to_all x3, starting transfers between devices, exchange(): return lax.all_to_all(value, axes, split_axis=0, concat_axis=0, tiled=True)  32.2 us
    all_to_all x3, waiting for transfers between devices, exchange(): return lax.all_to_all(value, axes, split_axis=0, concat_axis=0, tiled=True)  25.9 us
    all_to_all x1, blocking collectives, exchange(): return lax.all_to_all(value, axes, split_axis=0, concat_axis=0, tiled=True)  13.2 us
    ppermute x1, starting transfers between devices, step_of(): lax.ppermute(far, 'lat', [(i, i + 2 * (i & 1) - 1) for i in range(1, N_LA...  8.77 us
    pallas_call x1, Pallas kernels, forward(): call(forward_kernel, jax.ShapeDtypeStruct((N_DEV, 128), F32), [SM, SM, VM...  6.43 us
    pallas_call x1, Pallas kernels, tables(): pl.pallas_call(tables_kernel, out_shape=(jax.ShapeDtypeStruct((3, N_DEV,...  5.7 us
    pallas_call x1, Pallas kernels, spectral(): call(spectral_kernel, jax.ShapeDtypeStruct((N_LEV, WIDE, 128), BF16), [SM...  4.46 us
    pallas_call x1, Pallas kernels, inverse(): call(inverse_kernel, jax.ShapeDtypeStruct((ROWS, LV, NLON), F32), [VM, AN...  3.72 us
  transfers between devices with their start and end apart: 5, of which 3 were waited for; matrix products, arithmetic and copies ran while one was open for 3% of the time, Pallas kernels for 12%

profile of v7, /device:TPU:1, one launch (start us, length us, event | category | flops | bytes accessed | tf_op | source)
XLA Modules:
  0.0 117.4 jit_solution(2586314710431171847)
XLA Ops:
  0.6 2.2 %send_tables.1 = bf16[16,30,2,320]{3,2,1,0:T(2,128)(2,1)} custom-call(bf16[20,20,2,320]{3,2,1,0:T(2,128)(2,1)} %bitcast.21), custom_call_target="tpu_custom_call" | custom-call | flops 1000000 | bytes 2000000 | tf_op jit(solution)/shard_map/send_tables/pallas_call | solution.py:484
  2.9 10.4 %all-to-all-start.1 = ((bf16[16,30,2,320]{3,2,1,0:T(2,128)(2,1)}), bf16[16,30,2,320]{3,2,1,0:T(2,128)(2,1)S(1)}, u32[]{:S(2)}, u32[]{:S(2)}) async-start(bf16[16,30,2,320]{3,2,1,0:T(2,128)(2,1)} %send_tables.1), calls=%async_computation.1 | async-start | bytes 1474560 | tf_op jit(solution)/shard_map/all_to_all | solution.py:501
  13.3 0.8 dynamic-slice_bitcast_fusion
  14.0 8.8 %collective-permute-start.1 = (f32[3,2,1280]{2,1,0:T(2,128)S(1)}, f32[3,2,1280]{2,1,0:T(2,128)S(1)}, u32[]{:S(2)}, u32[]{:S(2)}) collective-permute-start(f32[3,2,1280]{2,1,0:T(2,128)S(1)} %get-tuple-element.8), channel_id=1, source_target_pairs={{16,32},{32,16},{48,64},{64,48},{80,96},{96,80},{112,128},{128,112... | collective-permute-start | bytes 92168 | tf_op jit(solution)/shard_map/ppermute | solution.py:511
  22.8 1.9 %collective-permute-start = (f32[3,2,1280]{2,1,0:T(2,128)S(1)}, f32[3,2,1280]{2,1,0:T(2,128)S(1)}, u32[]{:S(2)}, u32[]{:S(2)}) collective-permute-start(f32[3,2,1280]{2,1,0:T(2,128)S(1)} %get-tuple-element.9), channel_id=1, source_target_pairs={{0,16},{16,0},{32,48},{48,32},{64,80},{80,64},{96,112},{112,96},{1... | collective-permute-start | bytes 92168 | tf_op jit(solution)/shard_map/ppermute | solution.py:509
  24.8 5.7 %tables.1 = (bf16[3,512,1280]{2,1,0:T(8,128)(2,1)}, f32[512,128]{1,0:T(8,128)}, f32[512,128]{1,0:T(8,128)}) custom-call(s32[640]{0:T(1024)} %assign_ref.3), custom_call_target="tpu_custom_call" | custom-call | flops 10000000 | bytes 1000000 | tf_op jit(solution)/shard_map/tables/pallas_call | solution.py:136
  30.5 2.7 %collective-permute-done.1.far_ref = f32[3,2,1280]{2,1,0:T(2,128)S(1)} collective-permute-done((f32[3,2,1280]{2,1,0:T(2,128)S(1)}, f32[3,2,1280]{2,1,0:T(2,128)S(1)}, u32[]{:S(2)}, u32[]{:S(2)}) %collective-permute-start.1) | collective-permute-done | bytes 30752 | tf_op jit(solution)/shard_map/ppermute | solution.py:511
  33.2 0.0 copy-start.2
  33.2 0.0 collective-permute-done.near_ref
  33.2 0.0 copy-start.3
  33.2 0.6 copy-done.2
  33.8 0.0 copy-done.3
  33.8 6.4 %shard_map.95 = f32[512,128]{1,0:T(8,128)} custom-call(s32[1]{0:T(128)} %bitcast.2.side_ref, f32[7,7]{1,0:T(8,128)} %stencil_ref.1, f32[20,2,1280]{2,1,0:T(2,128)} %bitcast.25, f32[3,2,1280]{2,1,0:T(2,128)} %copy-done.3, f32[3,2,1280]{2,1,0:T(2,128)} %copy-done.2, s32[20,2,1280]{2,1,0:T(2,128)} %bitcast.27, bf16[3,512,1280]{2,1,0:T(8,128)(2,1)} %get-tuple-element.5.t_any, ...), custom_call_target="tpu_custom_call" | custom-call | flops 1000000000 | bytes 1000000 | tf_op jit(solution)/shard_map/pallas_call | solution.py:232
  40.3 0.0 all-to-all-done.1
  40.3 15.7 %all-to-all-start = ((f32[512,1,128]{2,1,0:T(1,128)}), f32[512,1,128]{2,1,0:T(1,128)S(1)}, u32[]{:S(2)}, u32[]{:S(2)}) async-start(f32[512,1,128]{2,1,0:T(1,128)} %bitcast.20), calls=%async_computation | async-start | bytes 524288 | tf_op jit(solution)/shard_map/all_to_all | solution.py:501
  56.0 0.3 slice.8
  56.3 1.2 %reshape.39.own_ref = bf16[640,320]{1,0:T(8,128)(2,1)} reshape(bf16[16,20,2,320]{3,2,1,0:T(2,128)(2,1)S(1)} %slice.8) | data formatting | bytes 819200 | tf_op jit(solution)/shard_map/reshape | solution.py:497
  57.5 0.2 slice.9
  57.7 0.9 reshape.40.shared_ref
  58.6 14.6 %all-to-all-done = f32[512,1,128]{2,1,0:T(1,128)S(1)} async-done(((f32[512,1,128]{2,1,0:T(1,128)}), f32[512,1,128]{2,1,0:T(1,128)S(1)}, u32[]{:S(2)}, u32[]{:S(2)}) %all-to-all-start) | async-done | bytes 262176 | tf_op jit(solution)/shard_map/all_to_all | solution.py:501
  73.2 0.0 copy-start.1
  73.2 0.7 copy-done.1
  73.9 4.5 %shard_map.96 = bf16[16,56,128]{2,1,0:T(8,128)(2,1)} custom-call(s32[1]{0:T(128)} %bitcast.lat_ref, s32[1]{0:T(128)} %bitcast.1.lev_ref, s32[640]{0:T(1024)} %assign_ref.3, f32[512,128]{1,0:T(8,128)} %bitcast.26, bf16[640,320]{1,0:T(8,128)(2,1)} %reshape.39.own_ref, bf16[320,320]{1,0:T(8,128)(2,1)} %reshape.40.shared_ref, f32[32]{0:T(128)} %damping_ref.1, ...), custom_call_target="tpu_custom_call" | custom-call | flops 1000000000 | bytes 1000000 | tf_op jit(solution)/shard_map/pallas_call | solution.py:374
  78.3 13.2 %all_to_all.20.wide_ref.spec_ref = bf16[16,56,128]{2,1,0:T(8,128)(2,1)} all-to-all(bf16[16,56,128]{2,1,0:T(8,128)(2,1)} %shard_map.96), channel_id=1, replica_groups=mesh['lat'=32,'lev'=16] {'lev'}, dimensions={0} | all-to-all | bytes 458752 | tf_op jit(solution)/shard_map/all_to_all | solution.py:501
  91.6 2.2 %shard_map.97 = bf16[512,128]{1,0:T(8,128)(2,1)} custom-call(bf16[16,56,128]{2,1,0:T(8,128)(2,1)} %all_to_all.20.wide_ref.spec_ref), custom_call_target="tpu_custom_call" | custom-call | flops 10000000 | bytes 1000000 | tf_op jit(solution)/shard_map/pallas_call | solution.py:411
  93.8 6.1 %all-to-all-start.3 = ((bf16[32,16,128]{2,1,0:T(8,128)(2,1)}), bf16[32,16,128]{2,1,0:T(8,128)(2,1)S(1)}, u32[]{:S(2)}, u32[]{:S(2)}) async-start(bf16[32,16,128]{2,1,0:T(8,128)(2,1)} %bitcast.23), calls=%async_computation.3 | async-start | bytes 262144 | tf_op jit(solution)/shard_map/all_to_all | solution.py:501
  99.9 1.8 %shard_map.99 = f32[20,40,64]{2,1,0:T(8,128)} custom-call(bf16[16,56,128]{2,1,0:T(8,128)(2,1)} %all_to_all.20.wide_ref.spec_ref), custom_call_target="tpu_custom_call" | custom-call | flops 1000000 | bytes 1000000 | tf_op jit(solution)/shard_map/pallas_call | solution.py:468
  101.7 11.3 %all-to-all-done.3 = bf16[32,16,128]{2,1,0:T(8,128)(2,1)S(1)} async-done(((bf16[32,16,128]{2,1,0:T(8,128)(2,1)}), bf16[32,16,128]{2,1,0:T(8,128)(2,1)S(1)}, u32[]{:S(2)}, u32[]{:S(2)}) %all-to-all-start.3) | async-done | bytes 131104 | tf_op jit(solution)/shard_map/all_to_all | solution.py:501
  113.1 0.0 copy-start
  113.1 0.7 copy-done
  113.7 3.7 %shard_map.98 = f32[20,2,1280]{2,1,0:T(2,128)} custom-call(bf16[512,128]{1,0:T(8,128)(2,1)} %bitcast.22, bf16[3,512,1280]{2,1,0:T(8,128)(2,1)} %get-tuple-element.5.t_any, f32[512,128]{1,0:T(8,128)} %get-tuple-element.6.even_ref, f32[512,128]{1,0:T(8,128)} %get-tuple-element.7.weight_ref), custom_call_target="tpu_custom_call" | custom-call | flops 100000000 | bytes 1000000 | tf_op jit(solution)/shard_map/pallas_call | solution.py:447
Async XLA Ops:
  2.9 37.4 %all-to-all-start.1 = ((bf16[16,30,2,320]{3,2,1,0:T(2,128)(2,1)}), bf16[16,30,2,320]{3,2,1,0:T(2,128)(2,1)S(1)}, u32[]{:S(2)}, u32[]{:S(2)}) async-start(bf16[16,30,2,320]{3,2,1,0:T(2,128)(2,1)} %send_tables.1), calls=%async_computation.1 | async-start | bytes 1474560 | tf_op jit(solution)/shard_map/all_to_all | solution.py:501
  14.0 19.1 %collective-permute-start.1 = (f32[3,2,1280]{2,1,0:T(2,128)S(1)}, f32[3,2,1280]{2,1,0:T(2,128)S(1)}, u32[]{:S(2)}, u32[]{:S(2)}) collective-permute-start(f32[3,2,1280]{2,1,0:T(2,128)S(1)} %get-tuple-element.8), channel_id=1, source_target_pairs={{16,32},{32,16},{48,64},{64,48},{80,96},{96,80},{112,128},{128,112... | collective-permute-start | bytes 92168 | tf_op jit(solution)/shard_map/ppermute | solution.py:511
  22.8 10.4 %collective-permute-start = (f32[3,2,1280]{2,1,0:T(2,128)S(1)}, f32[3,2,1280]{2,1,0:T(2,128)S(1)}, u32[]{:S(2)}, u32[]{:S(2)}) collective-permute-start(f32[3,2,1280]{2,1,0:T(2,128)S(1)} %get-tuple-element.9), channel_id=1, source_target_pairs={{0,16},{16,0},{32,48},{48,32},{64,80},{80,64},{96,112},{112,96},{1... | collective-permute-start | bytes 92168 | tf_op jit(solution)/shard_map/ppermute | solution.py:509
  33.2 0.6 copy-start.2
  33.2 0.6 copy-start.3
  40.3 32.9 %all-to-all-start = ((f32[512,1,128]{2,1,0:T(1,128)}), f32[512,1,128]{2,1,0:T(1,128)S(1)}, u32[]{:S(2)}, u32[]{:S(2)}) async-start(f32[512,1,128]{2,1,0:T(1,128)} %bitcast.20), calls=%async_computation | async-start | bytes 524288 | tf_op jit(solution)/shard_map/all_to_all | solution.py:501
  73.2 0.7 copy-start.1
  93.8 19.3 %all-to-all-start.3 = ((bf16[32,16,128]{2,1,0:T(8,128)(2,1)}), bf16[32,16,128]{2,1,0:T(8,128)(2,1)S(1)}, u32[]{:S(2)}, u32[]{:S(2)}) async-start(bf16[32,16,128]{2,1,0:T(8,128)(2,1)} %bitcast.23), calls=%async_computation.3 | async-start | bytes 262144 | tf_op jit(solution)/shard_map/all_to_all | solution.py:501
  113.1 0.7 copy-start

commit v8 on v7

--- a/solution.py
+++ b/solution.py
@@ -468,14 +468,21 @@
     return call(place_kernel, jax.ShapeDtypeStruct((SLOTS, QB, 64), F32), [VM], [], 10**6)(spec)
 
 
-def send_kernel(table_ref, out_ref, sems):
+def send_kernel(table_any, out_ref, table_ref, in_sems, sems):
+    fetches = [pltpu.make_async_copy(table_any.at[r], table_ref.at[r], in_sems.at[r]) for r in range(SLOTS)]
+    for fetch in fetches:
+        fetch.start()
     copies = []
     for b in range(N_LEV):
+        fetches[own_slot(b)].wait()
         copies.append(pltpu.make_async_copy(table_ref.at[own_slot(b)], out_ref.at[b, pl.ds(0, 20)], sems.at[2 * b]))
-        half = table_ref.at[shared_slot(b), pl.ds(10 * (b & 1), 10)]
-        copies.append(pltpu.make_async_copy(half, out_ref.at[b, pl.ds(20, 10)], sems.at[2 * b + 1]))
-    for copy in copies:
-        copy.start()
+        copies[-1].start()
+        if b & 3 == 3:
+            fetches[shared_slot(b)].wait()
+            for to in range(b - 3, b + 1):
+                half = table_ref.at[shared_slot(b), pl.ds(10 * (to & 1), 10)]
+                copies.append(pltpu.make_async_copy(half, out_ref.at[to, pl.ds(20, 10)], sems.at[2 * to + 1]))
+                copies[-1].start()
     for copy in copies:
         copy.wait()
 
@@ -484,9 +491,13 @@
     return pl.pallas_call(
         send_kernel,
         out_shape=jax.ShapeDtypeStruct((N_LEV, 30, 2, HL), BF16),
-        in_specs=[VM],
+        in_specs=[ANY],
         out_specs=ANY,
-        scratch_shapes=[pltpu.SemaphoreType.DMA((2 * N_LEV,))],
+        scratch_shapes=[
+            pltpu.VMEM((SLOTS, 20, 2, HL), BF16),
+            pltpu.SemaphoreType.DMA((SLOTS,)),
+            pltpu.SemaphoreType.DMA((2 * N_LEV,)),
+        ],
         name="send_tables",
         interpret=INTERPRET,
         cost_estimate=pl.CostEstimate(flops=10**6, bytes_accessed=2 * 10**6, transcendentals=0),

time: 118 us -> 118 us (level)
  no operation moved by 1% of the time
where the time goes in v8:
time: 118 us; the launch traced here: 117 us
  starting transfers between devices  42.9 us (36%)
  waiting for transfers between devices  28.6 us (24%)
  Pallas kernels  26.5 us (22%)
  blocking collectives  13.2 us (11%)
  local copies, waits for them, and re-layouts  5.36 us (5%)
    all_to_all x3, starting transfers between devices, exchange(): return lax.all_to_all(value, axes, split_axis=0, concat_axis=0, tiled=True)  32.2 us
    all_to_all x3, waiting for transfers between devices, exchange(): return lax.all_to_all(value, axes, split_axis=0, concat_axis=0, tiled=True)  25.9 us
    all_to_all x1, blocking collectives, exchange(): return lax.all_to_all(value, axes, split_axis=0, concat_axis=0, tiled=True)  13.2 us
    ppermute x1, starting transfers between devices, step_of(): lax.ppermute(far, 'lat', [(i, i + 2 * (i & 1) - 1) for i in range(1, N_LA...  8.77 us
    pallas_call x1, Pallas kernels, forward(): call(forward_kernel, jax.ShapeDtypeStruct((N_DEV, 128), F32), [SM, SM, VM...  6.43 us
    pallas_call x1, Pallas kernels, tables(): pl.pallas_call(tables_kernel, out_shape=(jax.ShapeDtypeStruct((3, N_DEV,...  5.7 us
    pallas_call x1, Pallas kernels, spectral(): call(spectral_kernel, jax.ShapeDtypeStruct((N_LEV, WIDE, 128), BF16), [SM...  4.45 us
    pallas_call x1, Pallas kernels, inverse(): call(inverse_kernel, jax.ShapeDtypeStruct((ROWS, LV, NLON), F32), [VM, AN...  3.71 us
  transfers between devices with their start and end apart: 5, of which 3 were waited for; matrix products, arithmetic and copies ran while one was open for 3% of the time, Pallas kernels for 12%

profile of v8, /device:TPU:1, one launch (start us, length us, event | category | flops | bytes accessed | tf_op | source)
XLA Modules:
  0.0 117.3 jit_solution(18175437951729533206)
XLA Ops:
  0.6 2.1 %send_tables.1 = bf16[16,30,2,320]{3,2,1,0:T(2,128)(2,1)} custom-call(bf16[20,20,2,320]{3,2,1,0:T(2,128)(2,1)} %bitcast.21), custom_call_target="tpu_custom_call" | custom-call | flops 1000000 | bytes 2000000 | tf_op jit(solution)/shard_map/send_tables/pallas_call | solution.py:491
  2.8 10.4 %all-to-all-start.1 = ((bf16[16,30,2,320]{3,2,1,0:T(2,128)(2,1)}), bf16[16,30,2,320]{3,2,1,0:T(2,128)(2,1)S(1)}, u32[]{:S(2)}, u32[]{:S(2)}) async-start(bf16[16,30,2,320]{3,2,1,0:T(2,128)(2,1)} %send_tables.1), calls=%async_computation.1 | async-start | bytes 1474560 | tf_op jit(solution)/shard_map/all_to_all | solution.py:512
  13.2 0.8 dynamic-slice_bitcast_fusion
  14.0 8.8 %collective-permute-start.1 = (f32[3,2,1280]{2,1,0:T(2,128)S(1)}, f32[3,2,1280]{2,1,0:T(2,128)S(1)}, u32[]{:S(2)}, u32[]{:S(2)}) collective-permute-start(f32[3,2,1280]{2,1,0:T(2,128)S(1)} %get-tuple-element.8), channel_id=1, source_target_pairs={{16,32},{32,16},{48,64},{64,48},{80,96},{96,80},{112,128},{128,112... | collective-permute-start | bytes 92168 | tf_op jit(solution)/shard_map/ppermute | solution.py:522
  22.7 1.9 %collective-permute-start = (f32[3,2,1280]{2,1,0:T(2,128)S(1)}, f32[3,2,1280]{2,1,0:T(2,128)S(1)}, u32[]{:S(2)}, u32[]{:S(2)}) collective-permute-start(f32[3,2,1280]{2,1,0:T(2,128)S(1)} %get-tuple-element.9), channel_id=1, source_target_pairs={{0,16},{16,0},{32,48},{48,32},{64,80},{80,64},{96,112},{112,96},{1... | collective-permute-start | bytes 92168 | tf_op jit(solution)/shard_map/ppermute | solution.py:520
  24.7 5.7 %tables.1 = (bf16[3,512,1280]{2,1,0:T(8,128)(2,1)}, f32[512,128]{1,0:T(8,128)}, f32[512,128]{1,0:T(8,128)}) custom-call(s32[640]{0:T(1024)} %assign_ref.3), custom_call_target="tpu_custom_call" | custom-call | flops 10000000 | bytes 1000000 | tf_op jit(solution)/shard_map/tables/pallas_call | solution.py:136
  30.4 2.7 %collective-permute-done.1.far_ref = f32[3,2,1280]{2,1,0:T(2,128)S(1)} collective-permute-done((f32[3,2,1280]{2,1,0:T(2,128)S(1)}, f32[3,2,1280]{2,1,0:T(2,128)S(1)}, u32[]{:S(2)}, u32[]{:S(2)}) %collective-permute-start.1) | collective-permute-done | bytes 30752 | tf_op jit(solution)/shard_map/ppermute | solution.py:522
  33.1 0.0 copy-start.2
  33.1 0.0 collective-permute-done.near_ref
  33.1 0.0 copy-start.3
  33.1 0.6 copy-done.2
  33.7 0.0 copy-done.3
  33.7 6.4 %shard_map.95 = f32[512,128]{1,0:T(8,128)} custom-call(s32[1]{0:T(128)} %bitcast.2.side_ref, f32[7,7]{1,0:T(8,128)} %stencil_ref.1, f32[20,2,1280]{2,1,0:T(2,128)} %bitcast.25, f32[3,2,1280]{2,1,0:T(2,128)} %copy-done.3, f32[3,2,1280]{2,1,0:T(2,128)} %copy-done.2, s32[20,2,1280]{2,1,0:T(2,128)} %bitcast.27, bf16[3,512,1280]{2,1,0:T(8,128)(2,1)} %get-tuple-element.5.t_any, ...), custom_call_target="tpu_custom_call" | custom-call | flops 1000000000 | bytes 1000000 | tf_op jit(solution)/shard_map/pallas_call | solution.py:232
  40.2 0.0 all-to-all-done.1
  40.2 15.7 %all-to-all-start = ((f32[512,1,128]{2,1,0:T(1,128)}), f32[512,1,128]{2,1,0:T(1,128)S(1)}, u32[]{:S(2)}, u32[]{:S(2)}) async-start(f32[512,1,128]{2,1,0:T(1,128)} %bitcast.20), calls=%async_computation | async-start | bytes 524288 | tf_op jit(solution)/shard_map/all_to_all | solution.py:512
  55.9 0.3 slice.8
  56.2 1.2 %reshape.39.own_ref = bf16[640,320]{1,0:T(8,128)(2,1)} reshape(bf16[16,20,2,320]{3,2,1,0:T(2,128)(2,1)S(1)} %slice.8) | data formatting | bytes 819200 | tf_op jit(solution)/shard_map/reshape | solution.py:508
  57.4 0.2 slice.9
  57.6 0.9 reshape.40.shared_ref
  58.5 14.6 %all-to-all-done = f32[512,1,128]{2,1,0:T(1,128)S(1)} async-done(((f32[512,1,128]{2,1,0:T(1,128)}), f32[512,1,128]{2,1,0:T(1,128)S(1)}, u32[]{:S(2)}, u32[]{:S(2)}) %all-to-all-start) | async-done | bytes 262176 | tf_op jit(solution)/shard_map/all_to_all | solution.py:512
  73.1 0.0 copy-start.1
  73.1 0.7 copy-done.1
  73.8 4.5 %shard_map.96 = bf16[16,56,128]{2,1,0:T(8,128)(2,1)} custom-call(s32[1]{0:T(128)} %bitcast.lat_ref, s32[1]{0:T(128)} %bitcast.1.lev_ref, s32[640]{0:T(1024)} %assign_ref.3, f32[512,128]{1,0:T(8,128)} %bitcast.26, bf16[640,320]{1,0:T(8,128)(2,1)} %reshape.39.own_ref, bf16[320,320]{1,0:T(8,128)(2,1)} %reshape.40.shared_ref, f32[32]{0:T(128)} %damping_ref.1, ...), custom_call_target="tpu_custom_call" | custom-call | flops 1000000000 | bytes 1000000 | tf_op jit(solution)/shard_map/pallas_call | solution.py:374
  78.2 13.2 %all_to_all.20.wide_ref.spec_ref = bf16[16,56,128]{2,1,0:T(8,128)(2,1)} all-to-all(bf16[16,56,128]{2,1,0:T(8,128)(2,1)} %shard_map.96), channel_id=1, replica_groups=mesh['lat'=32,'lev'=16] {'lev'}, dimensions={0} | all-to-all | bytes 458752 | tf_op jit(solution)/shard_map/all_to_all | solution.py:512
  91.5 2.2 %shard_map.97 = bf16[512,128]{1,0:T(8,128)(2,1)} custom-call(bf16[16,56,128]{2,1,0:T(8,128)(2,1)} %all_to_all.20.wide_ref.spec_ref), custom_call_target="tpu_custom_call" | custom-call | flops 10000000 | bytes 1000000 | tf_op jit(solution)/shard_map/pallas_call | solution.py:411
  93.7 6.1 %all-to-all-start.3 = ((bf16[32,16,128]{2,1,0:T(8,128)(2,1)}), bf16[32,16,128]{2,1,0:T(8,128)(2,1)S(1)}, u32[]{:S(2)}, u32[]{:S(2)}) async-start(bf16[32,16,128]{2,1,0:T(8,128)(2,1)} %bitcast.23), calls=%async_computation.3 | async-start | bytes 262144 | tf_op jit(solution)/shard_map/all_to_all | solution.py:512
  99.8 1.8 %shard_map.99 = f32[20,40,64]{2,1,0:T(8,128)} custom-call(bf16[16,56,128]{2,1,0:T(8,128)(2,1)} %all_to_all.20.wide_ref.spec_ref), custom_call_target="tpu_custom_call" | custom-call | flops 1000000 | bytes 1000000 | tf_op jit(solution)/shard_map/pallas_call | solution.py:468
  101.7 11.3 %all-to-all-done.3 = bf16[32,16,128]{2,1,0:T(8,128)(2,1)S(1)} async-done(((bf16[32,16,128]{2,1,0:T(8,128)(2,1)}), bf16[32,16,128]{2,1,0:T(8,128)(2,1)S(1)}, u32[]{:S(2)}, u32[]{:S(2)}) %all-to-all-start.3) | async-done | bytes 131104 | tf_op jit(solution)/shard_map/all_to_all | solution.py:512
  113.0 0.0 copy-start
  113.0 0.7 copy-done
  113.6 3.7 %shard_map.98 = f32[20,2,1280]{2,1,0:T(2,128)} custom-call(bf16[512,128]{1,0:T(8,128)(2,1)} %bitcast.22, bf16[3,512,1280]{2,1,0:T(8,128)(2,1)} %get-tuple-element.5.t_any, f32[512,128]{1,0:T(8,128)} %get-tuple-element.6.even_ref, f32[512,128]{1,0:T(8,128)} %get-tuple-element.7.weight_ref), custom_call_target="tpu_custom_call" | custom-call | flops 100000000 | bytes 1000000 | tf_op jit(solution)/shard_map/pallas_call | solution.py:447
Async XLA Ops:
  2.8 37.4 %all-to-all-start.1 = ((bf16[16,30,2,320]{3,2,1,0:T(2,128)(2,1)}), bf16[16,30,2,320]{3,2,1,0:T(2,128)(2,1)S(1)}, u32[]{:S(2)}, u32[]{:S(2)}) async-start(bf16[16,30,2,320]{3,2,1,0:T(2,128)(2,1)} %send_tables.1), calls=%async_computation.1 | async-start | bytes 1474560 | tf_op jit(solution)/shard_map/all_to_all | solution.py:512
  14.0 19.1 %collective-permute-start.1 = (f32[3,2,1280]{2,1,0:T(2,128)S(1)}, f32[3,2,1280]{2,1,0:T(2,128)S(1)}, u32[]{:S(2)}, u32[]{:S(2)}) collective-permute-start(f32[3,2,1280]{2,1,0:T(2,128)S(1)} %get-tuple-element.8), channel_id=1, source_target_pairs={{16,32},{32,16},{48,64},{64,48},{80,96},{96,80},{112,128},{128,112... | collective-permute-start | bytes 92168 | tf_op jit(solution)/shard_map/ppermute | solution.py:522
  22.7 10.4 %collective-permute-start = (f32[3,2,1280]{2,1,0:T(2,128)S(1)}, f32[3,2,1280]{2,1,0:T(2,128)S(1)}, u32[]{:S(2)}, u32[]{:S(2)}) collective-permute-start(f32[3,2,1280]{2,1,0:T(2,128)S(1)} %get-tuple-element.9), channel_id=1, source_target_pairs={{0,16},{16,0},{32,48},{48,32},{64,80},{80,64},{96,112},{112,96},{1... | collective-permute-start | bytes 92168 | tf_op jit(solution)/shard_map/ppermute | solution.py:520
  33.1 0.6 copy-start.2
  33.1 0.6 copy-start.3
  40.2 32.9 %all-to-all-start = ((f32[512,1,128]{2,1,0:T(1,128)}), f32[512,1,128]{2,1,0:T(1,128)S(1)}, u32[]{:S(2)}, u32[]{:S(2)}) async-start(f32[512,1,128]{2,1,0:T(1,128)} %bitcast.20), calls=%async_computation | async-start | bytes 524288 | tf_op jit(solution)/shard_map/all_to_all | solution.py:512
  73.1 0.7 copy-start.1
  93.7 19.3 %all-to-all-start.3 = ((bf16[32,16,128]{2,1,0:T(8,128)(2,1)}), bf16[32,16,128]{2,1,0:T(8,128)(2,1)S(1)}, u32[]{:S(2)}, u32[]{:S(2)}) async-start(bf16[32,16,128]{2,1,0:T(8,128)(2,1)} %bitcast.23), calls=%async_computation.3 | async-start | bytes 262144 | tf_op jit(solution)/shard_map/all_to_all | solution.py:512
  113.0 0.7 copy-start
